TPU v7x, 32 devices: a whole 2x2x4 slice. The times are simulated.
32 devices in a mesh: group: 2 (over y), sample: 16 (over z, x, core).
Axes of the slice: x: 2, y: 2, z: 4, core: 2. Of those that a mesh axis runs over, the one named last changes fastest.
Arguments:
- patches: bfloat16 [16, 256, 588], P('group', 'sample'), parts along dimension 0, may hold values from -6 to 6
- patch_weight: bfloat16 [16, 588, 1280], P('sample'), may hold values from -0.25 to 0.25
- cls_token: bfloat16 [16, 1280], P('sample'), may hold values from -6 to 6
- pos_embed: bfloat16 [16, 257, 1280], P('sample'), may hold values from -3 to 3
- ln1_gain: float32 [16, 1280], P('sample'), may hold values from 0.5 to 1.5
- ln1_bias: float32 [16, 1280], P('sample'), may hold values from -2 to 2
- w_query: bfloat16 [16, 1280, 640], P('sample'), may hold values from -8 to 8
- w_key: bfloat16 [16, 1280, 640], P('sample'), may hold values from -2 to 2
- w_value: bfloat16 [16, 1280, 640], P('sample'), may hold values from -0.15625 to 0.15625
- w_out: bfloat16 [16, 640, 1280], P('sample'), may hold values from -1 to 1
- lnf_gain: float32 [16, 1280], P('sample'), may hold values from 0.5 to 1.5
- lnf_bias: float32 [16, 1280], P('sample'), may hold values from -2 to 2
- head_w: bfloat16 [16, 1280, 1000], P('sample'), may hold values from -0.875 to 0.875
- head_bias: float32 [16, 1000], P('sample'), may hold values from -6 to 290
Outputs:
- predictive: float32 [16, 1000], P('group'), parts along dimension 0
There are 2 independent parts, one for each index of `group`. A program takes and returns all parts, laid end to end along the dimension named above; an argument that names none is the same for every part. Nothing has to cross between parts.
All inputs are finite; a program needn't handle non-finite values.
Results may differ from a plain program's by a relative error of at most 0.0023.
Values may be sent and summed in bfloat16 or wider, within the bound.
A program may use at most 64 MiB of HBM per device.

v0:
```python
import functools
import math

import jax
import jax.numpy as jnp
from jax import lax
from jax.experimental import pallas as pl
from jax.experimental.pallas import tpu as pltpu
from jax.sharding import PartitionSpec as P

HEAD_DIM = 80


epsilon = 1e-06


def combined_all(part, axis, combine):
    gathered = jax.tree.map(lambda a: lax.all_gather(a, axis), part)

    def take(source):
        return jax.tree.map(lambda a: lax.dynamic_index_in_dim(a, source, 0, False), gathered)

    return lax.fori_loop(
        1, lax.axis_size(axis), lambda source, state: combine(state, take(source)), take(0)
    )


def layer_norm(values, gain, shift):
    center = values - jnp.mean(values, axis=-1, keepdims=True)
    spread = jnp.mean(center * center, axis=-1, keepdims=True)
    return center * lax.rsqrt(spread + epsilon) * gain + shift


def shards(
    patches,
    patch_weight,
    cls_token,
    pos_embed,
    ln1_gain,
    ln1_bias,
    w_query,
    w_key,
    w_value,
    w_out,
    lnf_gain,
    lnf_bias,
    head_w,
    head_bias,
):
    embed_weight = patch_weight[0]
    position = pos_embed[0]
    gain_first = ln1_gain[0]
    bias_first = ln1_bias[0]
    query_weight = w_query[0]
    pair_weight = jnp.concatenate([w_key[0], w_value[0]], axis=1)
    out_weight = w_out[0]
    width = embed_weight.shape[1]
    inner = query_weight.shape[1]
    head_count = inner // HEAD_DIM
    leading = cls_token[0].astype(jnp.float32) + position[0].astype(jnp.float32)
    lead_norm = layer_norm(leading, gain_first, bias_first).astype(jnp.bfloat16)
    lead_pair = jnp.dot(lead_norm[None], pair_weight, preferred_element_type=jnp.float32).astype(
        jnp.bfloat16
    )
    query = jnp.dot(lead_norm[None], query_weight, preferred_element_type=jnp.float32).astype(
        jnp.bfloat16
    )
    query = query.reshape(head_count, HEAD_DIM)
    portion = lax.all_gather(patches, "sample", axis=1, tiled=True)
    image_count = portion.shape[0]
    row_count = portion.shape[1]
    flat = portion.reshape(-1, portion.shape[2])
    tokens = jnp.dot(flat, embed_weight, preferred_element_type=jnp.float32).reshape(
        image_count, row_count, width
    )
    placed = lax.dynamic_slice_in_dim(position, 1, row_count, 0)
    tokens = tokens + placed.astype(jnp.float32)[None]
    normed = layer_norm(tokens, gain_first, bias_first).astype(jnp.bfloat16)
    paired = jnp.dot(normed.reshape(-1, width), pair_weight, preferred_element_type=jnp.float32)
    key_values = paired.astype(jnp.bfloat16).reshape(image_count, row_count, 2 * inner)
    image_count = key_values.shape[0]
    lead_rows = jnp.broadcast_to(lead_pair[None], (image_count, 1, 2 * inner))
    full_rows = jnp.concatenate([lead_rows, key_values], axis=1)
    key_rows = full_rows[:, :, :inner].reshape(image_count, -1, head_count, HEAD_DIM)
    value_rows = full_rows[:, :, inner:].reshape(image_count, -1, head_count, HEAD_DIM)
    scores = jnp.einsum(
        "hd,ithd->iht", query, key_rows, preferred_element_type=jnp.float32
    ) / math.sqrt(HEAD_DIM)
    attention = jax.nn.softmax(scores, axis=-1).astype(jnp.bfloat16)
    mixed = jnp.einsum("iht,ithd->ihd", attention, value_rows, preferred_element_type=jnp.float32)
    mixed = mixed.astype(jnp.bfloat16).reshape(image_count, inner)
    hidden = leading[None] + jnp.dot(mixed, out_weight, preferred_element_type=jnp.float32)
    final = layer_norm(hidden, lnf_gain[0], lnf_bias[0]).astype(jnp.bfloat16)
    logits = jnp.dot(final, head_w[0], preferred_element_type=jnp.float32) + head_bias[0]
    logp = jax.nn.log_softmax(logits, axis=-1)
    count = lax.axis_size("sample")

    def combine(earlier, later):
        highest = jnp.maximum(earlier[0], later[0])
        summed = earlier[1] * jnp.exp(earlier[0] - highest) + later[1] * jnp.exp(later[0] - highest)
        return (highest, summed)

    peak, total = combined_all((logp, jnp.ones_like(logp)), "sample", combine)
    return peak + jnp.log(total) - math.log(count)


MESH = pl.DeviceIdType.MESH
PLANE = 4
BF16_ROWS = 16
LOWEST = -1e30


def flipped(index, turn, bits):
    out = 0
    for bit in range(bits):
        step = 1 << bit
        out = out + step * ((index // step + turn // step) % 2)
    return out


def split_in_two(values):
    high = values.astype(jnp.bfloat16)
    low = (values - high.astype(jnp.float32)).astype(jnp.bfloat16)
    return jnp.concatenate([high, low], axis=0)


def whole_kernel(
    count,
    heads,
    patches,
    cls_token,
    ln1_gain,
    ln1_bias,
    lnf_gain,
    lnf_bias,
    head_bias,
    patch_weight,
    pos_embed,
    w_query,
    w_key,
    w_value,
    w_out,
    head_w,
    out,
    embed,
    position,
    query_w,
    key_w,
    value_w,
    out_w,
    class_w,
    place,
    slots,
    tokens,
    normed,
    probe,
    gathered,
    peak,
    total,
    part,
    from_pair,
    ring,
    result,
    load_sem,
    recv_sem,
    line_sem,
    across_sem,
    pair_sem,
    relay_sem,
    tail_send,
    tail_recv,
    spread_sem,
):
    me = lax.axis_index("sample")
    core = me % 2
    chip = me // 2
    chips = count // 2
    planes = count // PLANE
    bits = planes.bit_length() - 1
    plane = me // PLANE
    spot = me % PLANE
    beside = plane * PLANE + (spot + 2) % PLANE
    twin = me + 1 - 2 * core
    images, rows, depth = patches.shape
    width = embed.shape[1]
    inner = query_w.shape[1]
    head_dim = inner // heads
    pairs = heads * images

    loads = []
    for index, (source, target) in enumerate(
        (
            (pos_embed, position),
            (w_query, query_w),
            (w_key, key_w),
            (patch_weight, embed),
            (w_value, value_w),
            (w_out, out_w),
            (head_w, class_w),
        )
    ):
        load = pltpu.make_async_copy(source.at[0], target, load_sem.at[index])
        load.start()
        loads.append(load)

    barrier = pltpu.get_barrier_semaphore()
    for step in range(1, chips):
        pl.semaphore_signal(
            barrier,
            inc=1,
            device_id={"sample": 2 * ((chip + step) % chips) + core},
            device_id_type=MESH,
        )
    pl.semaphore_signal(barrier, inc=1, device_id={"sample": twin}, device_id_type=MESH)
    pl.semaphore_wait(barrier, chips)

    def send(source, origin, target, sem):
        return pltpu.make_async_remote_copy(
            src_ref=source,
            dst_ref=slots.at[origin],
            send_sem=sem,
            recv_sem=recv_sem.at[origin],
            device_id={"sample": target},
            device_id_type=MESH,
        )

    def along(turn):
        return flipped(plane, turn, bits) * PLANE + spot

    def across(turn):
        return flipped(plane, turn, bits) * PLANE + (spot + 2) % PLANE

    def other(turn):
        return flipped(plane, turn, bits) * PLANE + spot + 1 - 2 * core

    def other_across(turn):
        return flipped(plane, turn, bits) * PLANE + (spot + 2) % PLANE + 1 - 2 * core

    def arrived(origin):
        send(slots.at[origin], origin, twin, relay_sem.at[0]).wait_recv()

    send(patches, me, beside, across_sem.at[0]).start()
    for turn in range(1, planes):
        if turn == 1 or turn % 2 == 0:
            send(patches, me, along(turn), line_sem.at[turn]).start()
    send(patches, me, twin, pair_sem.at[0]).start()
    slots[me] = patches[...]

    loads[0].wait()
    place[...] = position[...].astype(jnp.float32)[1:]
    leading = cls_token[...].astype(jnp.float32) + position[0:1, :].astype(jnp.float32)
    gain = ln1_gain[...]
    bias = ln1_bias[...]
    lead = jnp.broadcast_to(layer_norm(leading, gain, bias), (BF16_ROWS, width)).astype(jnp.bfloat16)
    loads[1].wait()
    query = jnp.dot(lead, query_w[...], preferred_element_type=jnp.float32)[:1]
    row_head = lax.broadcasted_iota(jnp.int32, (pairs, inner), 0) // images
    column = lax.broadcasted_iota(jnp.int32, (pairs, inner), 1)
    own_head = (column >= row_head * head_dim) & (column < (row_head + 1) * head_dim)
    spread = jnp.where(own_head, jnp.broadcast_to(query, (pairs, inner)), 0.0).astype(jnp.bfloat16)
    loads[2].wait()
    turned = lax.dot_general(
        spread, key_w[...], (((1,), (1,)), ((), ())), preferred_element_type=jnp.float32
    ) * (1.0 / math.sqrt(head_dim))
    probe[...] = split_in_two(turned)
    lead_row = lead[:1].astype(jnp.float32)
    first = jnp.sum(turned * lead_row, axis=1, keepdims=True)
    peak[...] = jnp.broadcast_to(first, peak.shape)
    total[...] = jnp.ones(total.shape, jnp.float32)
    gathered[...] = jnp.broadcast_to(lead_row, gathered.shape)
    loads[3].wait()

    span = PLANE * images * rows
    token_image = (lax.broadcasted_iota(jnp.int32, (pairs, span), 1) // rows) % images
    row_image = lax.broadcasted_iota(jnp.int32, (pairs, span), 0) % images
    same = token_image == row_image

    def turn_step(turn, carry):
        @pl.when(turn < planes)
        def _():
            origin = along(turn)
            arrived(origin)
            send(slots.at[origin], origin, beside, across_sem.at[turn]).start()
            send(slots.at[origin], origin, twin, pair_sem.at[turn]).start()

            @pl.when(turn % 2 == 0)
            def _():
                send(slots.at[origin], origin, along(1), line_sem.at[turn + 1]).start()

        done = turn - 1
        origin = across(done)
        arrived(origin)
        send(slots.at[origin], origin, twin, relay_sem.at[done]).start()
        arrived(other(done))
        arrived(other_across(done))

        where = flipped(plane, done, bits)
        block = slots[pl.ds(where * PLANE, PLANE)].reshape(span, depth)
        tokens[...] = jnp.dot(block, embed[...], preferred_element_type=jnp.float32)
        for one in range(PLANE):
            low = one * images * rows
            start = pl.multiple_of((where * PLANE + one) * rows, rows)
            spots = place[pl.ds(start, rows), :]
            value = tokens[low : low + images * rows, :].reshape(images, rows, width) + spots[None]
            value = layer_norm(value, gain[None], bias[None])
            normed[low : low + images * rows, :] = value.reshape(images * rows, width).astype(
                jnp.bfloat16
            )
        scores = lax.dot_general(
            probe[...], normed[...], (((1,), (1,)), ((), ())), preferred_element_type=jnp.float32
        )
        scores = jnp.where(same, scores[:pairs] + scores[pairs:], LOWEST)
        before = peak[:, :1]
        now = jnp.maximum(before, jnp.max(scores, axis=1, keepdims=True))
        shrink = jnp.exp(before - now)
        chance = jnp.where(same, jnp.exp(scores - now), 0.0)
        peak[...] = jnp.broadcast_to(now, peak.shape)
        total[...] = total[...] * shrink + jnp.sum(chance, axis=1, keepdims=True)
        gathered[...] = gathered[...] * shrink + jnp.dot(
            chance.astype(jnp.bfloat16), normed[...], preferred_element_type=jnp.float32
        )
        return carry

    lax.fori_loop(1, planes + 1, turn_step, 0)

    loads[4].wait()
    pooled = gathered[...] / total[:, :1]
    values = jnp.dot(split_in_two(pooled), value_w[...], preferred_element_type=jnp.float32)
    values = jnp.where(own_head, values[:pairs] + values[pairs:], 0.0)
    mixed = jnp.sum(values.reshape(heads, images, inner), axis=0).astype(jnp.bfloat16)
    loads[5].wait()
    hidden = leading + jnp.dot(mixed, out_w[...], preferred_element_type=jnp.float32)
    final = layer_norm(hidden, lnf_gain[...], lnf_bias[...]).astype(jnp.bfloat16)
    loads[6].wait()
    logits = (
        lax.dot_general(
            final, class_w[...], (((1,), (1,)), ((), ())), preferred_element_type=jnp.float32
        )
        + head_bias[...]
    )
    lifted = logits - jnp.max(logits, axis=-1, keepdims=True)
    logp = lifted - jnp.log(jnp.sum(jnp.exp(lifted), axis=-1, keepdims=True))

    half = part.shape[2]
    classes = out.shape[1]
    part[0] = logp[:, :half]
    part[1] = jnp.concatenate(
        [logp[:, half:], jnp.zeros((images, 2 * half - classes), jnp.float32)], axis=1
    )
    swap = pltpu.make_async_remote_copy(
        src_ref=part.at[1 - core],
        dst_ref=from_pair,
        send_sem=tail_send.at[0],
        recv_sem=tail_recv.at[0],
        device_id={"sample": twin},
        device_id_type=MESH,
    )
    swap.start()
    swap.wait_recv()
    mine = part[core]
    theirs = from_pair[...]
    high = jnp.maximum(mine, theirs)
    ring[chip] = high + jnp.log(jnp.exp(mine - high) + jnp.exp(theirs - high))

    def pass_on(origin, target, step):
        return pltpu.make_async_remote_copy(
            src_ref=ring.at[origin],
            dst_ref=ring.at[origin],
            send_sem=spread_sem.at[step],
            recv_sem=tail_recv.at[2 + origin],
            device_id={"sample": target},
            device_id_type=MESH,
        )

    for step in range(1, chips):
        pass_on(chip, 2 * ((chip + step) % chips) + core, step).start()
    for step in range(1, chips):
        pass_on((chip + step) % chips, me, step).wait_recv()
    every = ring[...]
    high = jnp.max(every, axis=0)
    result[core] = high + jnp.log(jnp.sum(jnp.exp(every - high[None]), axis=0)) - math.log(count)
    share = pltpu.make_async_remote_copy(
        src_ref=result.at[core],
        dst_ref=result.at[core],
        send_sem=tail_send.at[1],
        recv_sem=tail_recv.at[1],
        device_id={"sample": twin},
        device_id_type=MESH,
    )
    share.start()
    for turn in range(planes):
        send(patches, me, beside, across_sem.at[turn]).wait_send()
        send(patches, me, twin, pair_sem.at[turn]).wait_send()
        send(patches, me, twin, relay_sem.at[turn]).wait_send()
        if turn:
            send(patches, me, twin, line_sem.at[turn]).wait_send()
    swap.wait_send()
    for step in range(1, chips):
        pass_on(chip, twin, step).wait_send()
    pltpu.make_async_remote_copy(
        src_ref=result.at[core],
        dst_ref=result.at[1 - core],
        send_sem=tail_send.at[1],
        recv_sem=tail_recv.at[1],
        device_id={"sample": twin},
        device_id_type=MESH,
    ).wait_recv()
    share.wait_send()
    out[:, :half] = result[0]
    out[:, half:] = result[1][:, : classes - half]


def kernel_shards(
    patches,
    patch_weight,
    cls_token,
    pos_embed,
    ln1_gain,
    ln1_bias,
    w_query,
    w_key,
    w_value,
    w_out,
    lnf_gain,
    lnf_bias,
    head_w,
    head_bias,
):
    count = lax.axis_size("sample")
    images, rows, depth = patches.shape
    width = patch_weight.shape[2]
    inner = w_query.shape[2]
    heads = inner // HEAD_DIM
    pairs = heads * images
    planes = count // PLANE
    chips = count // 2
    classes = head_w.shape[2]
    half = pl.cdiv(classes, 256) * 128
    span = PLANE * images * rows
    near = pl.BlockSpec(memory_space=pltpu.VMEM)
    far = pl.BlockSpec(memory_space=pl.ANY)
    dma = pltpu.SemaphoreType.DMA
    f32, bf16 = jnp.float32, jnp.bfloat16
    class_rows = jnp.swapaxes(head_w, 1, 2)
    large = (patch_weight, pos_embed, w_query, w_key, w_value, w_out, class_rows)
    embed, position, query_w, key_w, value_w, out_w, class_w = (
        pltpu.VMEM(a.shape[1:], a.dtype) for a in large
    )
    return pl.pallas_call(
        functools.partial(whole_kernel, count, heads),
        out_shape=jax.ShapeDtypeStruct((images, classes), f32),
        in_specs=[near] * 7 + [far] * 7,
        out_specs=near,
        scratch_shapes=[
            embed,
            position,
            query_w,
            key_w,
            value_w,
            out_w,
            class_w,
            pltpu.VMEM((rows * count, width), f32),
            pltpu.VMEM((count, images, rows, depth), bf16),
            pltpu.VMEM((span, width), f32),
            pltpu.VMEM((span, width), bf16),
            pltpu.VMEM((2 * pairs, width), bf16),
            pltpu.VMEM((pairs, width), f32),
            pltpu.VMEM((pairs, 128), f32),
            pltpu.VMEM((pairs, 128), f32),
            pltpu.VMEM((2, images, half), f32),
            pltpu.VMEM((images, half), f32),
            pltpu.VMEM((chips, images, half), f32),
            pltpu.VMEM((2, images, half), f32),
            dma((7,)),
            dma((count,)),
            dma((planes,)),
            dma((planes,)),
            dma((planes,)),
            dma((planes,)),
            dma((2,)),
            dma((2 + chips,)),
            dma((chips,)),
        ],
        compiler_params=pltpu.CompilerParams(
            collective_id=0, has_side_effects=True, vmem_limit_bytes=60 << 20
        ),
    )(patches, cls_token, ln1_gain, ln1_bias, lnf_gain, lnf_bias, head_bias, *large)


def takes_kernel(mesh, patches):
    count = mesh.shape["sample"]
    planes = count // PLANE
    rows = patches.shape[1] // count
    return count % PLANE == 0 and planes & (planes - 1) == 0 and rows % BF16_ROWS == 0


def solution(mesh):
    placed = (
        P("group", "sample", None),
        P("sample", None, None),
        P("sample", None),
        P("sample", None, None),
        P("sample", None),
        P("sample", None),
        P("sample", None, None),
        P("sample", None, None),
        P("sample", None, None),
        P("sample", None, None),
        P("sample", None),
        P("sample", None),
        P("sample", None, None),
        P("sample", None),
    )

    def run(*arrays):
        step = kernel_shards if takes_kernel(mesh, arrays[0]) else shards
        return jax.shard_map(
            step, mesh=mesh, in_specs=placed, out_specs=P("group", None), check_vma=False
        )(*arrays)

    return run
```

profile of v0, /device:TPU:0, one launch (start us, length us, event | category | flops | bytes accessed | tf_op | source)
XLA Modules:
  0.0 44.3 jit_solution(8230321199020088783)
XLA Ops:
  0.0 42.9 %shard_map.136 = f32[8,1000]{1,0:T(8,128)} custom-call(bf16[8,16,588]{2,1,0:T(8,128)(2,1)} %patches.1, bf16[1,1280]{1,0:T(2,128)(2,1)} %cls_token.1, f32[1,1280]{1,0:T(1,128)} %ln1_gain.1, f32[1,1280]{1,0:T(1,128)} %ln1_bias.1, f32[1,1280]{1,0:T(1,128)} %lnf_gain.1, f32[1,1280]{1,0:T(1,128)} %lnf_bias.1, f32[1,1000]{1,0:T(1,128)} %head_bias.1, ...), custom_call_target="tpu_custom_call" | custom-call | tf_op jit(solution)/shard_map/pallas_call | solution.py:449
  42.9 1.4 %copy.16 = f32[8,1000]{1,0:T(8,128)} copy(f32[8,1000]{1,0:T(8,128)} %shard_map.136) | data formatting | bytes 64000
where the time goes:
time: 44.5 us; the launch traced here: 44.3 us
  Pallas kernels  42.9 us (96%)
  local copies, waits for them, and re-layouts  1.38 us (3%)
    pallas_call x1, Pallas kernels, kernel_shards(): pl.pallas_call(functools.partial(whole_kernel, count, heads), out_shape=j...  42.9 us
    unnamed x1, local copies, waits for them, and re-layouts  1.38 us

commit v1 on v0

v1 whole, which is shorter than its diff:
```python
import functools
import math

import jax
import jax.numpy as jnp
from jax import lax
from jax.experimental import pallas as pl
from jax.experimental.pallas import tpu as pltpu
from jax.sharding import PartitionSpec as P

HEAD_DIM = 80


epsilon = 1e-06


def combined_all(part, axis, combine):
    gathered = jax.tree.map(lambda a: lax.all_gather(a, axis), part)

    def take(source):
        return jax.tree.map(lambda a: lax.dynamic_index_in_dim(a, source, 0, False), gathered)

    return lax.fori_loop(
        1, lax.axis_size(axis), lambda source, state: combine(state, take(source)), take(0)
    )


def layer_norm(values, gain, shift):
    center = values - jnp.mean(values, axis=-1, keepdims=True)
    spread = jnp.mean(center * center, axis=-1, keepdims=True)
    return center * lax.rsqrt(spread + epsilon) * gain + shift


def shards(
    patches,
    patch_weight,
    cls_token,
    pos_embed,
    ln1_gain,
    ln1_bias,
    w_query,
    w_key,
    w_value,
    w_out,
    lnf_gain,
    lnf_bias,
    head_w,
    head_bias,
):
    embed_weight = patch_weight[0]
    position = pos_embed[0]
    gain_first = ln1_gain[0]
    bias_first = ln1_bias[0]
    query_weight = w_query[0]
    pair_weight = jnp.concatenate([w_key[0], w_value[0]], axis=1)
    out_weight = w_out[0]
    width = embed_weight.shape[1]
    inner = query_weight.shape[1]
    head_count = inner // HEAD_DIM
    leading = cls_token[0].astype(jnp.float32) + position[0].astype(jnp.float32)
    lead_norm = layer_norm(leading, gain_first, bias_first).astype(jnp.bfloat16)
    lead_pair = jnp.dot(lead_norm[None], pair_weight, preferred_element_type=jnp.float32).astype(
        jnp.bfloat16
    )
    query = jnp.dot(lead_norm[None], query_weight, preferred_element_type=jnp.float32).astype(
        jnp.bfloat16
    )
    query = query.reshape(head_count, HEAD_DIM)
    portion = lax.all_gather(patches, "sample", axis=1, tiled=True)
    image_count = portion.shape[0]
    row_count = portion.shape[1]
    flat = portion.reshape(-1, portion.shape[2])
    tokens = jnp.dot(flat, embed_weight, preferred_element_type=jnp.float32).reshape(
        image_count, row_count, width
    )
    placed = lax.dynamic_slice_in_dim(position, 1, row_count, 0)
    tokens = tokens + placed.astype(jnp.float32)[None]
    normed = layer_norm(tokens, gain_first, bias_first).astype(jnp.bfloat16)
    paired = jnp.dot(normed.reshape(-1, width), pair_weight, preferred_element_type=jnp.float32)
    key_values = paired.astype(jnp.bfloat16).reshape(image_count, row_count, 2 * inner)
    image_count = key_values.shape[0]
    lead_rows = jnp.broadcast_to(lead_pair[None], (image_count, 1, 2 * inner))
    full_rows = jnp.concatenate([lead_rows, key_values], axis=1)
    key_rows = full_rows[:, :, :inner].reshape(image_count, -1, head_count, HEAD_DIM)
    value_rows = full_rows[:, :, inner:].reshape(image_count, -1, head_count, HEAD_DIM)
    scores = jnp.einsum(
        "hd,ithd->iht", query, key_rows, preferred_element_type=jnp.float32
    ) / math.sqrt(HEAD_DIM)
    attention = jax.nn.softmax(scores, axis=-1).astype(jnp.bfloat16)
    mixed = jnp.einsum("iht,ithd->ihd", attention, value_rows, preferred_element_type=jnp.float32)
    mixed = mixed.astype(jnp.bfloat16).reshape(image_count, inner)
    hidden = leading[None] + jnp.dot(mixed, out_weight, preferred_element_type=jnp.float32)
    final = layer_norm(hidden, lnf_gain[0], lnf_bias[0]).astype(jnp.bfloat16)
    logits = jnp.dot(final, head_w[0], preferred_element_type=jnp.float32) + head_bias[0]
    logp = jax.nn.log_softmax(logits, axis=-1)
    count = lax.axis_size("sample")

    def combine(earlier, later):
        highest = jnp.maximum(earlier[0], later[0])
        summed = earlier[1] * jnp.exp(earlier[0] - highest) + later[1] * jnp.exp(later[0] - highest)
        return (highest, summed)

    peak, total = combined_all((logp, jnp.ones_like(logp)), "sample", combine)
    return peak + jnp.log(total) - math.log(count)


MESH = pl.DeviceIdType.MESH
PLANE = 4
LINE = 4
TILE_ROWS = 16
LOWEST = -1e30


def split_in_two(values):
    high = values.astype(jnp.bfloat16)
    low = (values - high.astype(jnp.float32)).astype(jnp.bfloat16)
    return jnp.concatenate([high, low], axis=0)


def pick(index, values):
    packed = sum(value << (3 * place) for place, value in enumerate(values))
    return ((index * 0 + packed) >> (3 * index)) % 8


def contract_last(left, right):
    return lax.dot_general(
        left, right, (((1,), (1,)), ((), ())), preferred_element_type=jnp.float32
    )


def whole_kernel(
    count,
    heads,
    patches,
    cls_token,
    pos_embed,
    ln1_gain,
    ln1_bias,
    patch_weight,
    w_query,
    w_key,
    w_value,
    w_out,
    head_w,
    lnf_gain,
    lnf_bias,
    head_bias,
    out,
    own_patches,
    cls_row,
    position,
    gain_row,
    bias_row,
    embed,
    query_w,
    key_w,
    value_w,
    out_w,
    class_w,
    last_gain,
    last_bias,
    class_bias,
    slots,
    basis,
    scaled,
    form,
    folded,
    constants,
    gathered,
    peak,
    total,
    part,
    from_pair,
    ring,
    result,
    load_sem,
    recv_sem,
    sent_sem,
    tail_send,
    tail_recv,
    spread_sem,
):
    f32, bf16 = jnp.float32, jnp.bfloat16
    me = lax.axis_index("sample")
    core = me % 2
    side = (me // 2) % 2
    chip = me // 2
    chips = count // 2
    plane = me // PLANE
    upper = plane // (LINE // 2)
    depth_in = plane * (1 - upper) + (LINE - 1 - plane) * upper
    inward = 1 - 2 * upper
    images, rows, depth = own_patches.shape
    padded = slots.shape[1]
    lanes = slots.shape[2]
    half = pl.cdiv(padded // TILE_ROWS, 2) * TILE_ROWS
    width = embed.shape[1]
    inner = query_w.shape[1]
    head_dim = inner // heads
    pairs = heads * images
    spots = position.shape[0] - 1

    loads = []
    for index, (source, target) in enumerate(
        (
            (patches, own_patches),
            (pos_embed.at[0], position),
            (cls_token, cls_row),
            (ln1_gain, gain_row),
            (ln1_bias, bias_row),
            (patch_weight.at[0], embed),
            (w_query.at[0], query_w),
            (w_key.at[0], key_w),
            (w_value.at[0], value_w),
            (w_out.at[0], out_w),
            (head_w.at[0], class_w),
            (lnf_gain, last_gain),
            (lnf_bias, last_bias),
            (head_bias, class_bias),
        )
    ):
        load = pltpu.make_async_copy(source, target, load_sem.at[index])
        load.start()
        loads.append(load)

    twin = me + 1 - 2 * core
    beside = plane * PLANE + (1 - side) * 2 + core

    def line(where):
        return where * PLANE + side * 2 + core

    def cross(where):
        return where * PLANE + (1 - side) * 2 + core

    span = LINE - 1
    line_at = {step: line(plane + step * inward) for step in range(-1, LINE)}
    cross_at = {step: cross(plane + step * inward) for step in range(-1, LINE)}
    nearer = line_at[1]
    farther = line_at[-1]
    opposite = line_at[span]

    barrier = pltpu.get_barrier_semaphore()

    def greet(target):
        pl.semaphore_signal(barrier, inc=1, device_id={"sample": target}, device_id_type=MESH)

    greet(twin)
    greet(beside)
    greet(nearer)

    @pl.when(depth_in == 1)
    def _():
        greet(farther)

    loads[0].wait()
    eye = (
        lax.broadcasted_iota(jnp.int32, (padded, depth), 0)
        == lax.broadcasted_iota(jnp.int32, (padded, depth), 1)
    ).astype(bf16)
    flat = own_patches[...].reshape(images * rows, depth)
    slots[me] = contract_last(eye, flat).astype(bf16)
    pl.semaphore_wait(barrier, 3 + depth_in)

    FAR, NEAR, ACROSS, TWIN, DIRECT = range(5)

    def piece(way, target, origin, part_of):
        ref = slots.at[origin, pl.ds(0, half)] if part_of == 0 else slots.at[origin, pl.ds(half, padded - half)]
        return pltpu.make_async_remote_copy(
            src_ref=ref,
            dst_ref=ref,
            send_sem=sent_sem.at[way, origin, part_of],
            recv_sem=recv_sem.at[origin, part_of],
            device_id={"sample": target},
            device_id_type=MESH,
        )

    def arrived(origin, part_of):
        piece(TWIN, twin, origin, part_of).wait_recv()

    issued = []

    def send(way, target, origin, part_of, when=None):
        issued.append((way, target, origin, part_of, when))
        piece(way, target, origin, part_of).start()

    end = depth_in == 0
    middle = depth_in == 1
    def own_sends():
        @pl.when(end)
        def _():
            send(NEAR, nearer, me, 0, end)
            send(NEAR, nearer, me, 1, end)

        @pl.when(middle)
        def _():
            send(FAR, farther, me, 0, middle)
            send(NEAR, nearer, me, 0, middle)
            send(NEAR, nearer, me, 1, middle)

        send(ACROSS, beside, me, 0)
        send(ACROSS, beside, me, 1)
        send(TWIN, twin, me, 0)
        send(TWIN, twin, me, 1)

    def on_line(which, step, part_of, crosses, relay=None, then=()):
        origin = line_at[step]
        arrived(origin, part_of)
        if relay is not None:
            target = nearer if relay == NEAR else farther
            send(relay, target, origin, part_of, which)
        if crosses:
            send(ACROSS, beside, origin, part_of, which)
        send(TWIN, twin, origin, part_of, which)

    def on_cross(which, step, part_of, relay=None):
        origin = cross_at[step]
        arrived(origin, part_of)
        if relay is not None:
            target = nearer if relay == NEAR else farther
            send(relay, target, origin, part_of, which)
        send(TWIN, twin, origin, part_of, which)

    def both(at_end, at_middle):
        pl.when(end)(at_end)
        pl.when(middle)(at_middle)

    def end_events(group):
        if group == 0:
            on_line(end, 1, 0, True)
            on_cross(end, 0, 0, NEAR)
        if group == 1:
            on_line(end, 2, 0, True)
            send(DIRECT, opposite, me, 0, end)
            send(DIRECT, opposite, me, 1, end)
            on_cross(end, 0, 1, NEAR)
        if group == 2:
            on_line(end, 2, 1, True)
        if group == 3:
            on_cross(end, 1, 0)
            on_line(end, 1, 1, False)
        if group == 4:
            on_cross(end, 2, 0)
            on_line(end, 3, 0, True)
            on_cross(end, 2, 1)
        if group == 5:
            on_line(end, 3, 1, True)
        if group == 6:
            on_cross(end, 1, 1)
        if group == 7:
            on_cross(end, 3, 0)
            on_cross(end, 3, 1)

    def middle_events(group):
        if group == 0:
            on_line(middle, -1, 0, False, NEAR)
            on_line(middle, 1, 0, True, FAR)
            on_cross(middle, 0, 0)
        if group == 1:
            on_line(middle, -1, 1, False, NEAR)
            on_line(middle, 1, 1, True, FAR)
            send(FAR, farther, me, 1, middle)
            on_cross(middle, 0, 1, FAR)
        if group == 2:
            on_line(middle, 2, 0, True)
        if group == 3:
            on_cross(middle, 1, 0)
            on_line(middle, 2, 1, True)
        if group == 4:
            on_cross(middle, 1, 1)
            on_cross(middle, -1, 0)
        if group == 5:
            on_cross(middle, -1, 1)
        if group == 6:
            on_cross(middle, 2, 0)
        if group == 7:
            on_cross(middle, 2, 1)

    def events(group):
        both(functools.partial(end_events, group), functools.partial(middle_events, group))

    own_sends()

    for index in (1, 2, 3, 4):
        loads[index].wait()
    gain = gain_row[...]
    bias = bias_row[...]
    leading = cls_row[...].astype(f32) + position[0:1, :].astype(f32)
    lead = jnp.broadcast_to(layer_norm(leading, gain, bias), (TILE_ROWS, width)).astype(bf16)
    lead_row = lead[:1].astype(f32)

    placed = position[...].astype(f32)[1:]
    placed = placed - jnp.mean(placed, axis=1, keepdims=True)
    basis[padded:, :] = placed.astype(bf16)
    scaled[padded:, :] = (placed * gain).astype(bf16)
    weight = jnp.sum(placed * placed, axis=1, keepdims=True)
    weight = jnp.transpose(jnp.broadcast_to(weight, (spots, 128)))[:1]

    loads[5].wait()
    table = embed[...].astype(f32)
    table = table - jnp.mean(table, axis=1, keepdims=True)
    table = jnp.concatenate([table, jnp.zeros((padded - depth, width), f32)], axis=0)
    basis[:padded, :] = table.astype(bf16)
    scaled[:padded, :] = (table * gain).astype(bf16)

    loads[6].wait()
    query = jnp.dot(lead, query_w[...], preferred_element_type=f32)[:1]
    head_row = lax.broadcasted_iota(jnp.int32, (TILE_ROWS, inner), 0)
    column = lax.broadcasted_iota(jnp.int32, (TILE_ROWS, inner), 1)
    own_head = (column >= head_row * head_dim) & (column < (head_row + 1) * head_dim)
    spread = jnp.where(own_head, jnp.broadcast_to(query, (TILE_ROWS, inner)), 0.0).astype(bf16)
    loads[7].wait()
    turned = contract_last(spread, key_w[...])[:heads] * (1.0 / math.sqrt(head_dim))
    first = jnp.sum(turned * lead_row, axis=1, keepdims=True)
    level = jnp.sum(turned * bias, axis=1, keepdims=True)
    constants[...] = jnp.broadcast_to(level, constants.shape)
    probe = split_in_two(turned * gain)

    events(0)

    square = contract_last(basis[:padded, :], basis[...])
    square = jnp.concatenate([square[:, :padded], 2.0 * square[:, padded:]], axis=1)
    form[:padded, :] = square.astype(bf16)
    reach = contract_last(probe, basis[...])
    reach = split_in_two(reach[:heads] + reach[heads:])
    form[padded : padded + 2 * heads, :] = reach
    sizes = jnp.concatenate([jnp.zeros((1, padded), f32), weight], axis=1)
    sizes_high = sizes.astype(bf16).astype(f32)
    sizes = jnp.concatenate(
        [sizes_high, sizes - sizes_high, jnp.zeros((TILE_ROWS - 2, padded + spots), f32)], axis=0
    )
    form[padded + 2 * heads :, :] = sizes.astype(bf16)

    events(1)

    loads[8].wait()
    folded[...] = jnp.dot(scaled[...], value_w[...], preferred_element_type=f32).astype(bf16)
    ends = jnp.concatenate([split_in_two(bias), lead[:1], jnp.zeros((TILE_ROWS - 3, width), bf16)], axis=0)
    ends = jnp.dot(ends, value_w[...], preferred_element_type=f32)
    plain = ends[0:1] + ends[1:2]
    lead_value = ends[2:3]

    first = jnp.broadcast_to(first[None], (images, heads, 1)).reshape(pairs, 1)
    peak[...] = jnp.broadcast_to(first, peak.shape)
    total[...] = jnp.ones(total.shape, f32)
    gathered[...] = jnp.zeros(gathered.shape, f32)

    cells = 2 * lanes
    lane = lax.broadcasted_iota(jnp.int32, (pairs, cells), 1)
    row_image = lax.broadcasted_iota(jnp.int32, (pairs, cells), 0) // heads
    same = (lane % lanes) // rows == row_image
    spot_row = lax.broadcasted_iota(jnp.int32, (spots, cells), 0)
    spot_lane = lax.broadcasted_iota(jnp.int32, (spots, cells), 1)
    spot_at = spot_row - (spot_lane // lanes) * rows - spot_lane % rows

    delta_end = (0, 0, 2, 1, 2, 3, 1, 3)
    delta_middle = (1, 1, 0, 2, 2, 0, 3, 3)
    across_end = (0, 1, 0, 0, 1, 0, 1, 1)
    across_middle = (0, 1, 0, 0, 1, 1, 0, 1)

    def chip_step(turn, carry):
        for index, group in ((2, 2), (3, 3), (4, 4), (5, 5), (6, 6), (7, 7)):
            pl.when(turn == index)(functools.partial(events, group))
        step = pick(turn, delta_end) * (1 - depth_in) + (pick(turn, delta_middle) - 1) * depth_in
        across = pick(turn, across_end) * (1 - depth_in) + pick(turn, across_middle) * depth_in
        where = plane + inward * step
        base = where * PLANE + 2 * (side * (1 - across) + (1 - side) * across)
        arrived(base + 1 - core, 0)
        arrived(base + 1 - core, 1)
        block = jnp.concatenate([slots[base], slots[base + 1]], axis=1)
        spot = jnp.where(spot_at == base * rows, 1.0, 0.0).astype(bf16)
        block = jnp.concatenate([block, spot], axis=0)
        image = jnp.dot(form[...], block, preferred_element_type=f32)
        norm = jnp.sum(image[:padded] * block[:padded].astype(f32), axis=0, keepdims=True)
        tail = padded + 2 * heads
        norm = norm + image[tail : tail + 1] + image[tail + 1 : tail + 2]
        rate = lax.rsqrt(norm * (1.0 / width) + epsilon)
        scores = image[padded : padded + heads] + image[padded + heads : tail]
        scores = scores * rate + constants[:, :1]
        scores = jnp.broadcast_to(scores[None], (images, heads, cells)).reshape(pairs, cells)
        scores = jnp.where(same, scores, LOWEST)
        before = peak[:, :1]
        now = jnp.maximum(before, jnp.max(scores, axis=1, keepdims=True))
        shrink = jnp.exp(before - now)
        chance = jnp.where(same, jnp.exp(scores - now), 0.0)
        peak[...] = jnp.broadcast_to(now, peak.shape)
        total[...] = total[...] * shrink + jnp.sum(chance, axis=1, keepdims=True)
        gathered[...] = gathered[...] * shrink + contract_last((chance * rate).astype(bf16), block)
        return carry

    lax.fori_loop(0, 2 * LINE, chip_step, 0)

    whole = total[:, :1]
    lead_chance = jnp.exp(first - peak[:, :1]) / whole
    pooled = split_in_two(gathered[...] / whole)
    values = jnp.dot(pooled, folded[...], preferred_element_type=f32)
    values = values[:pairs] + values[pairs:] + plain * (1.0 - lead_chance) + lead_value * lead_chance
    pair_head = lax.broadcasted_iota(jnp.int32, (pairs, inner), 0) % heads
    pair_column = lax.broadcasted_iota(jnp.int32, (pairs, inner), 1)
    mine_only = (pair_column >= pair_head * head_dim) & (pair_column < (pair_head + 1) * head_dim)
    values = jnp.where(mine_only, values, 0.0)
    mixed = jnp.sum(values.reshape(images, heads, inner), axis=1).astype(bf16)
    loads[9].wait()
    hidden = leading + jnp.dot(mixed, out_w[...], preferred_element_type=f32)
    for index in (10, 11, 12, 13):
        loads[index].wait()
    final = layer_norm(hidden, last_gain[...], last_bias[...]).astype(bf16)
    logits = contract_last(final, class_w[...]) + class_bias[...]
    lifted = logits - jnp.max(logits, axis=-1, keepdims=True)
    logp = lifted - jnp.log(jnp.sum(jnp.exp(lifted), axis=-1, keepdims=True))

    piece_width = part.shape[2]
    classes = out.shape[1]
    part[0] = logp[:, :piece_width]
    part[1] = jnp.concatenate(
        [logp[:, piece_width:], jnp.zeros((images, 2 * piece_width - classes), f32)], axis=1
    )
    swap = pltpu.make_async_remote_copy(
        src_ref=part.at[1 - core],
        dst_ref=from_pair,
        send_sem=tail_send.at[0],
        recv_sem=tail_recv.at[0],
        device_id={"sample": twin},
        device_id_type=MESH,
    )
    swap.start()
    swap.wait_recv()
    mine = part[core]
    theirs = from_pair[...]
    high = jnp.maximum(mine, theirs)
    ring[chip] = high + jnp.log(jnp.exp(mine - high) + jnp.exp(theirs - high))

    def pass_on(origin, target, step):
        return pltpu.make_async_remote_copy(
            src_ref=ring.at[origin],
            dst_ref=ring.at[origin],
            send_sem=spread_sem.at[step],
            recv_sem=tail_recv.at[2 + origin],
            device_id={"sample": target},
            device_id_type=MESH,
        )

    for step in range(1, chips):
        pass_on(chip, 2 * ((chip + step) % chips) + core, step).start()
    for step in range(1, chips):
        pass_on((chip + step) % chips, me, step).wait_recv()
    every = ring[...]
    high = jnp.max(every, axis=0)
    result[core] = high + jnp.log(jnp.sum(jnp.exp(every - high[None]), axis=0)) - math.log(count)
    share = pltpu.make_async_remote_copy(
        src_ref=result.at[core],
        dst_ref=result.at[core],
        send_sem=tail_send.at[1],
        recv_sem=tail_recv.at[1],
        device_id={"sample": twin},
        device_id_type=MESH,
    )
    share.start()

    def settle(way, target, origin, part_of):
        piece(way, target, origin, part_of).wait_send()

    for way, target, origin, part_of, when in issued:
        if when is None:
            settle(way, target, origin, part_of)
    for which in (end, middle):

        @pl.when(which)
        def _(which=which):
            for way, target, origin, part_of, when in issued:
                if when is which:
                    settle(way, target, origin, part_of)

    swap.wait_send()
    for step in range(1, chips):
        pass_on(chip, twin, step).wait_send()
    pltpu.make_async_remote_copy(
        src_ref=result.at[core],
        dst_ref=result.at[1 - core],
        send_sem=tail_send.at[1],
        recv_sem=tail_recv.at[1],
        device_id={"sample": twin},
        device_id_type=MESH,
    ).wait_recv()
    share.wait_send()
    out[:, :piece_width] = result[0]
    out[:, piece_width:] = result[1][:, : classes - piece_width]


def kernel_shards(
    patches,
    patch_weight,
    cls_token,
    pos_embed,
    ln1_gain,
    ln1_bias,
    w_query,
    w_key,
    w_value,
    w_out,
    lnf_gain,
    lnf_bias,
    head_w,
    head_bias,
):
    count = lax.axis_size("sample")
    images, rows, depth = patches.shape
    width = patch_weight.shape[2]
    inner = w_query.shape[2]
    heads = inner // HEAD_DIM
    pairs = heads * images
    chips = count // 2
    classes = head_w.shape[2]
    piece_width = pl.cdiv(classes, 256) * 128
    padded = pl.cdiv(depth, TILE_ROWS) * TILE_ROWS
    spots = pos_embed.shape[1] - 1
    far = pl.BlockSpec(memory_space=pl.ANY)
    dma = pltpu.SemaphoreType.DMA
    f32, bf16 = jnp.float32, jnp.bfloat16
    class_rows = jnp.swapaxes(head_w, 1, 2)
    given = (
        patches,
        cls_token,
        pos_embed,
        ln1_gain,
        ln1_bias,
        patch_weight,
        w_query,
        w_key,
        w_value,
        w_out,
        class_rows,
        lnf_gain,
        lnf_bias,
        head_bias,
    )
    whole = (True, False)
    held = [
        pltpu.VMEM(a.shape[1:] if a.ndim == 3 and place else a.shape, a.dtype)
        for place, a in enumerate(given)
    ]
    return pl.pallas_call(
        functools.partial(whole_kernel, count, heads),
        out_shape=jax.ShapeDtypeStruct((images, classes), f32),
        in_specs=[far] * len(given),
        out_specs=pl.BlockSpec(memory_space=pltpu.VMEM),
        scratch_shapes=[
            *held,
            pltpu.VMEM((count, padded, images * rows), bf16),
            pltpu.VMEM((padded + spots, width), bf16),
            pltpu.VMEM((padded + spots, width), bf16),
            pltpu.VMEM((padded + 2 * heads + TILE_ROWS, padded + spots), bf16),
            pltpu.VMEM((padded + spots, inner), bf16),
            pltpu.VMEM((heads, 128), f32),
            pltpu.VMEM((pairs, padded + spots), f32),
            pltpu.VMEM((pairs, 128), f32),
            pltpu.VMEM((pairs, 128), f32),
            pltpu.VMEM((2, images, piece_width), f32),
            pltpu.VMEM((images, piece_width), f32),
            pltpu.VMEM((chips, images, piece_width), f32),
            pltpu.VMEM((2, images, piece_width), f32),
            dma((len(given),)),
            dma((count, 2)),
            dma((5, count, 2)),
            dma((2,)),
            dma((2 + chips,)),
            dma((chips,)),
        ],
        compiler_params=pltpu.CompilerParams(
            collective_id=0, has_side_effects=True, vmem_limit_bytes=60 << 20
        ),
    )(*given)


def takes_kernel(mesh, patches):
    count = mesh.shape["sample"]
    rows = patches.shape[1] // count
    images = patches.shape[0] // mesh.shape["group"]
    return count == PLANE * LINE and rows % TILE_ROWS == 0 and images * rows == 128


def solution(mesh):
    placed = (
        P("group", "sample", None),
        P("sample", None, None),
        P("sample", None),
        P("sample", None, None),
        P("sample", None),
        P("sample", None),
        P("sample", None, None),
        P("sample", None, None),
        P("sample", None, None),
        P("sample", None, None),
        P("sample", None),
        P("sample", None),
        P("sample", None, None),
        P("sample", None),
    )

    def run(*arrays):
        step = kernel_shards if takes_kernel(mesh, arrays[0]) else shards
        return jax.shard_map(
            step, mesh=mesh, in_specs=placed, out_specs=P("group", None), check_vma=False
        )(*arrays)

    return run
```

time: 44.5 us -> 44.4 us (level)
  no operation moved by 1% of the time
where the time goes in v1:
time: 44.4 us; the launch traced here: 44.3 us
  Pallas kernels  42.9 us (97%)
  local copies, waits for them, and re-layouts  1.38 us (3%)
    pallas_call x1, Pallas kernels, kernel_shards(): pl.pallas_call(functools.partial(whole_kernel, count, heads), out_shape=j...  42.9 us
    unnamed x1, local copies, waits for them, and re-layouts  1.38 us

profile of v1, /device:TPU:0, one launch (start us, length us, event | category | flops | bytes accessed | tf_op | source)
XLA Modules:
  0.0 44.3 jit_solution(5088818605877611560)
XLA Ops:
  0.0 42.9 %shard_map.136 = f32[8,1000]{1,0:T(8,128)} custom-call(bf16[8,16,588]{2,1,0:T(8,128)(2,1)} %patches.1, bf16[1,1280]{1,0:T(2,128)(2,1)} %cls_token.1, bf16[1,257,1280]{2,1,0:T(8,128)(2,1)} %pos_embed.1, f32[1,1280]{1,0:T(1,128)} %ln1_gain.1, f32[1,1280]{1,0:T(1,128)} %ln1_bias.1, bf16[1,588,1280]{2,1,0:T(8,128)(2,1)} %patch_weight.1, ...), custom_call_target="tpu_custom_call" | custom-call | tf_op jit(solution)/shard_map/pallas_call | solution.py:641
  42.9 1.4 %copy.16 = f32[8,1000]{1,0:T(8,128)} copy(f32[8,1000]{1,0:T(8,128)} %shard_map.136) | data formatting | bytes 64000

commit v2 on v1

--- a/solution.py
+++ b/solution.py
@@ -109,6 +109,8 @@
 LINE = 4
 TILE_ROWS = 16
 LOWEST = -1e30
+GRAM_PARTS = 4
+FOLD_PARTS = 6
 
 
 def split_in_two(values):
@@ -117,9 +119,76 @@
     return jnp.concatenate([high, low], axis=0)
 
 
-def pick(index, values):
-    packed = sum(value << (3 * place) for place, value in enumerate(values))
-    return ((index * 0 + packed) >> (3 * index)) % 8
+PIECES = 3
+SENDS = (
+    (
+        (1,1,0,1,0), (1,1,0,1,1), (0,0,0,1,0), (1,1,0,1,2), (0,0,0,1,2), (0,0,0,1,1), (0,2,0,1,0),
+        (0,2,0,1,1), (0,2,0,1,2), (3,1,0,1,0), (1,1,0,0,0), (2,1,0,1,2), (0,2,0,0,0), (0,0,1,1,0),
+        (0,2,1,1,0), (1,1,0,0,2), (3,1,0,0,2), (0,2,0,0,2), (0,0,1,1,2), (0,2,1,1,2), (3,1,0,0,1),
+        (0,2,0,0,1), (0,0,1,1,1), (0,2,1,1,1), (0,2,1,0,0), (0,2,1,0,2), (0,0,2,1,2), (0,2,2,1,2),
+        (0,2,1,0,1), (0,0,3,1,0), (0,2,3,1,0), (0,0,2,1,1), (0,2,2,1,1), (0,0,2,1,0), (0,2,2,1,0),
+        (0,2,2,0,2), (0,2,3,0,0), (0,2,3,0,2), (0,2,2,0,1), (0,2,3,1,1), (0,2,3,0,1), (0,2,2,0,0),
+        (0,2,3,1,2),
+    ),
+    (
+        (0,1,1,1,0), (1,0,1,1,1), (0,1,1,1,2), (0,1,1,1,1), (2,1,1,1,2), (2,1,1,1,1), (1,0,1,1,0),
+        (2,1,1,1,0), (1,2,1,1,0), (1,2,1,1,1), (1,2,1,1,2), (2,1,0,1,0), (1,2,0,1,0), (1,2,1,0,1),
+        (1,0,0,1,1), (2,1,0,1,1), (1,2,0,1,1), (1,0,2,1,2), (0,1,2,1,2), (1,2,2,1,2), (1,2,1,0,0),
+        (1,2,0,1,2), (1,0,1,1,2), (0,1,2,1,1), (1,0,2,1,1), (1,2,2,1,1), (1,0,2,1,0), (0,1,2,1,0),
+        (1,2,2,1,0), (1,2,0,0,1), (1,2,0,0,0), (1,2,2,0,2), (1,0,3,1,0), (1,2,3,1,0), (1,2,1,0,2),
+        (1,2,0,0,2), (0,1,3,1,1), (1,0,3,1,1), (1,2,3,1,1), (1,2,2,0,1), (1,0,3,1,2), (0,1,3,1,2),
+        (1,2,3,1,2), (1,2,2,0,0), (1,2,3,0,0), (1,2,3,0,1), (1,2,3,0,2),
+    ),
+    (
+        (3,1,2,1,0), (2,0,2,1,1), (3,1,2,1,2), (3,1,2,1,1), (1,1,2,1,2), (1,1,2,1,1), (2,0,2,1,0),
+        (1,1,2,1,0), (2,2,2,1,0), (2,2,2,1,1), (2,2,2,1,2), (2,0,1,1,2), (3,1,1,1,2), (2,2,1,1,2),
+        (2,2,2,0,1), (2,0,2,1,2), (3,1,1,1,1), (2,0,1,1,1), (2,2,1,1,1), (1,1,3,1,0), (2,2,3,1,0),
+        (2,2,2,0,0), (2,0,1,1,0), (3,1,1,1,0), (2,2,1,1,0), (2,0,3,1,1), (1,1,3,1,1), (2,2,3,1,1),
+        (2,2,3,1,2), (2,2,1,0,2), (2,0,0,1,0), (2,2,0,1,0), (2,2,2,0,2), (3,1,0,1,1), (2,0,0,1,1),
+        (2,2,0,1,1), (2,2,1,0,1), (2,2,3,0,0), (2,0,0,1,2), (3,1,0,1,2), (2,2,0,1,2), (2,2,1,0,0),
+        (2,2,3,0,1), (2,2,0,0,0), (2,2,3,0,2), (2,2,0,0,1), (2,2,0,0,2),
+    ),
+    (
+        (2,1,3,1,0), (2,1,3,1,1), (3,0,3,1,0), (2,1,3,1,2), (3,0,3,1,2), (3,0,3,1,1), (3,2,3,1,0),
+        (3,2,3,1,1), (3,2,3,1,2), (0,1,3,1,0), (3,0,2,1,0), (3,2,2,1,0), (2,1,3,0,0), (1,1,3,1,2),
+        (3,2,3,0,0), (3,0,2,1,2), (3,2,2,1,2), (2,1,3,0,2), (0,1,3,0,2), (3,2,3,0,2), (0,1,3,0,1),
+        (3,2,3,0,1), (3,0,2,1,1), (3,2,2,1,1), (3,2,2,0,0), (3,0,0,1,0), (3,2,0,1,0), (3,0,1,1,2),
+        (3,2,1,1,2), (3,0,1,1,1), (3,2,1,1,1), (3,2,2,0,2), (3,0,1,1,0), (3,2,1,1,0), (3,2,2,0,1),
+        (3,2,0,0,0), (3,2,0,0,2), (3,2,1,0,2), (3,2,0,1,1), (3,2,1,0,1), (3,2,0,0,1), (3,2,0,1,2),
+        (3,2,1,0,0),
+    ),
+)
+EVENTS = (
+    (
+        ((-1,0,0,0,9),), (), (), ((-2,2,0,9,0),), (), ((-2,3,0,9,1),), (), ((0,0,0,10,3),(1,1,0,13,2)), (),
+        ((0,0,2,15,3),(1,1,2,18,2)), (), ((0,0,1,20,2),(1,1,1,22,2)), (),
+        ((1,0,0,24,1),(1,0,2,25,1),(2,1,2,26,2),(1,0,1,28,1)), ((3,1,0,29,2),(2,1,1,31,2),(2,1,0,33,2)),
+        ((2,0,2,35,1),(3,0,0,36,1),(3,0,2,37,1),(2,0,1,38,1),(3,1,1,39,1),(3,0,1,40,1)),
+        ((2,0,0,41,1),(3,1,2,42,1)), (),
+    ),
+    (
+        ((-1,0,0,0,11),), (), (), (), ((-2,3,0,11,0),), (), (), ((0,1,0,11,2),(1,0,1,13,1)), (),
+        ((0,1,1,14,3),(2,1,2,17,3),(1,0,0,20,1)), (), ((0,1,2,21,1),(2,1,1,22,4)), ((2,1,0,26,3),),
+        ((0,0,1,29,1),(0,0,0,30,1),(2,0,2,31,1),(3,1,0,32,2),(1,0,2,34,1)),
+        ((0,0,2,35,1),(3,1,1,36,3),(2,0,1,39,1),(3,1,2,40,3),(2,0,0,43,1)), (), ((3,0,0,44,1),),
+        ((3,0,1,45,1),(3,0,2,46,1)),
+    ),
+    (
+        ((-1,0,0,0,11),), ((-2,0,0,11,0),), (), (), (), ((1,1,2,11,3),), (), ((2,0,1,14,1),(1,1,1,15,4)), (),
+        ((3,1,0,19,2),(2,0,0,21,1)), ((1,1,0,22,3),), ((3,1,1,25,3),),
+        ((3,1,2,28,1),(1,0,2,29,1),(0,1,0,30,2)), ((2,0,2,32,1),),
+        ((0,1,1,33,3),(1,0,1,36,1),(3,0,0,37,1),(0,1,2,38,3),(1,0,0,41,1)), ((3,0,1,42,1),),
+        ((0,0,0,43,1),(3,0,2,44,1)), ((0,0,1,45,1),(0,0,2,46,1)),
+    ),
+    (
+        ((-1,0,0,0,9),), ((-2,0,0,9,1),(-2,1,0,10,0)), (), (), (), (), ((2,1,0,10,2),), ((3,0,0,12,3),),
+        ((2,1,2,15,2),), ((3,0,2,17,3),), (), ((3,0,1,20,2),(2,1,1,22,2)),
+        ((2,0,0,24,1),(0,1,0,25,2),(1,1,2,27,2)), ((1,1,1,29,2),(2,0,2,31,1),(1,1,0,32,2)),
+        ((2,0,1,34,1),(0,0,0,35,1)), ((0,0,2,36,1),(1,0,2,37,1),(0,1,1,38,1),(1,0,1,39,1),(0,0,1,40,1)),
+        ((0,1,2,41,1),(1,0,0,42,1)), (),
+    ),
+)
+ORDER = (15946945, 13862219, 1645021, 4474743)
 
 
 def contract_last(left, right):
@@ -166,6 +235,7 @@
     form,
     folded,
     constants,
+    kept,
     gathered,
     peak,
     total,
@@ -176,6 +246,7 @@
     load_sem,
     recv_sem,
     sent_sem,
+    known_sem,
     tail_send,
     tail_recv,
     spread_sem,
@@ -187,13 +258,11 @@
     chip = me // 2
     chips = count // 2
     plane = me // PLANE
-    upper = plane // (LINE // 2)
-    depth_in = plane * (1 - upper) + (LINE - 1 - plane) * upper
-    inward = 1 - 2 * upper
     images, rows, depth = own_patches.shape
     padded = slots.shape[1]
     lanes = slots.shape[2]
-    half = pl.cdiv(padded // TILE_ROWS, 2) * TILE_ROWS
+    tiles = padded // TILE_ROWS
+    cuts = tuple(TILE_ROWS * (tiles * place // PIECES) for place in range(PIECES + 1))
     width = embed.shape[1]
     inner = query_w.shape[1]
     head_dim = inner // heads
@@ -225,19 +294,11 @@
 
     twin = me + 1 - 2 * core
     beside = plane * PLANE + (1 - side) * 2 + core
-
-    def line(where):
-        return where * PLANE + side * 2 + core
-
-    def cross(where):
-        return where * PLANE + (1 - side) * 2 + core
-
-    span = LINE - 1
-    line_at = {step: line(plane + step * inward) for step in range(-1, LINE)}
-    cross_at = {step: cross(plane + step * inward) for step in range(-1, LINE)}
-    nearer = line_at[1]
-    farther = line_at[-1]
-    opposite = line_at[span]
+    here = tuple(lax.convert_element_type(plane == place, jnp.int32) for place in range(LINE))
+    line_of = tuple(
+        (place * PLANE + (1 - side) * 2 + core, place * PLANE + side * 2 + core)
+        for place in range(LINE)
+    )
 
     barrier = pltpu.get_barrier_semaphore()
 
@@ -246,11 +307,14 @@
 
     greet(twin)
     greet(beside)
-    greet(nearer)
-
-    @pl.when(depth_in == 1)
+
+    @pl.when(plane > 0)
     def _():
-        greet(farther)
+        greet(me - PLANE)
+
+    @pl.when(plane < LINE - 1)
+    def _():
+        greet(me + PLANE)
 
     loads[0].wait()
     eye = (
@@ -259,139 +323,76 @@
     ).astype(bf16)
     flat = own_patches[...].reshape(images * rows, depth)
     slots[me] = contract_last(eye, flat).astype(bf16)
-    pl.semaphore_wait(barrier, 3 + depth_in)
-
-    FAR, NEAR, ACROSS, TWIN, DIRECT = range(5)
-
-    def piece(way, target, origin, part_of):
-        ref = slots.at[origin, pl.ds(0, half)] if part_of == 0 else slots.at[origin, pl.ds(half, padded - half)]
+    pl.semaphore_wait(barrier, LINE - here[0] - here[LINE - 1])
+
+    def piece(slot, target, origin, part_of):
+        low, high = cuts[part_of], cuts[part_of + 1]
+        ref = slots.at[origin, pl.ds(low, high - low)]
         return pltpu.make_async_remote_copy(
             src_ref=ref,
             dst_ref=ref,
-            send_sem=sent_sem.at[way, origin, part_of],
+            send_sem=sent_sem.at[slot],
             recv_sem=recv_sem.at[origin, part_of],
             device_id={"sample": target},
             device_id_type=MESH,
         )
 
-    def arrived(origin, part_of):
-        piece(TWIN, twin, origin, part_of).wait_recv()
-
-    issued = []
-
-    def send(way, target, origin, part_of, when=None):
-        issued.append((way, target, origin, part_of, when))
-        piece(way, target, origin, part_of).start()
-
-    end = depth_in == 0
-    middle = depth_in == 1
-    def own_sends():
-        @pl.when(end)
-        def _():
-            send(NEAR, nearer, me, 0, end)
-            send(NEAR, nearer, me, 1, end)
-
-        @pl.when(middle)
-        def _():
-            send(FAR, farther, me, 0, middle)
-            send(NEAR, nearer, me, 0, middle)
-            send(NEAR, nearer, me, 1, middle)
-
-        send(ACROSS, beside, me, 0)
-        send(ACROSS, beside, me, 1)
-        send(TWIN, twin, me, 0)
-        send(TWIN, twin, me, 1)
-
-    def on_line(which, step, part_of, crosses, relay=None, then=()):
-        origin = line_at[step]
-        arrived(origin, part_of)
-        if relay is not None:
-            target = nearer if relay == NEAR else farther
-            send(relay, target, origin, part_of, which)
-        if crosses:
-            send(ACROSS, beside, origin, part_of, which)
-        send(TWIN, twin, origin, part_of, which)
-
-    def on_cross(which, step, part_of, relay=None):
-        origin = cross_at[step]
-        arrived(origin, part_of)
-        if relay is not None:
-            target = nearer if relay == NEAR else farther
-            send(relay, target, origin, part_of, which)
-        send(TWIN, twin, origin, part_of, which)
-
-    def both(at_end, at_middle):
-        pl.when(end)(at_end)
-        pl.when(middle)(at_middle)
-
-    def end_events(group):
-        if group == 0:
-            on_line(end, 1, 0, True)
-            on_cross(end, 0, 0, NEAR)
-        if group == 1:
-            on_line(end, 2, 0, True)
-            send(DIRECT, opposite, me, 0, end)
-            send(DIRECT, opposite, me, 1, end)
-            on_cross(end, 0, 1, NEAR)
-        if group == 2:
-            on_line(end, 2, 1, True)
-        if group == 3:
-            on_cross(end, 1, 0)
-            on_line(end, 1, 1, False)
-        if group == 4:
-            on_cross(end, 2, 0)
-            on_line(end, 3, 0, True)
-            on_cross(end, 2, 1)
-        if group == 5:
-            on_line(end, 3, 1, True)
-        if group == 6:
-            on_cross(end, 1, 1)
-        if group == 7:
-            on_cross(end, 3, 0)
-            on_cross(end, 3, 1)
-
-    def middle_events(group):
-        if group == 0:
-            on_line(middle, -1, 0, False, NEAR)
-            on_line(middle, 1, 0, True, FAR)
-            on_cross(middle, 0, 0)
-        if group == 1:
-            on_line(middle, -1, 1, False, NEAR)
-            on_line(middle, 1, 1, True, FAR)
-            send(FAR, farther, me, 1, middle)
-            on_cross(middle, 0, 1, FAR)
-        if group == 2:
-            on_line(middle, 2, 0, True)
-        if group == 3:
-            on_cross(middle, 1, 0)
-            on_line(middle, 2, 1, True)
-        if group == 4:
-            on_cross(middle, 1, 1)
-            on_cross(middle, -1, 0)
-        if group == 5:
-            on_cross(middle, -1, 1)
-        if group == 6:
-            on_cross(middle, 2, 0)
-        if group == 7:
-            on_cross(middle, 2, 1)
+    def sent(place, slot):
+        to, aside, origin, own, part_of = SENDS[place][slot]
+        target = twin if aside == 2 else line_of[to][aside]
+        return piece(slot, target, line_of[origin][own], part_of)
+
+    def tell(target, entered):
+        pl.semaphore_signal(
+            known_sem.at[entered], inc=1, device_id={"sample": target}, device_id_type=MESH
+        )
+
+    def learn(place, entered):
+        pl.semaphore_wait(known_sem.at[entered], 1)
+        if place == 1 and entered == 3:
+            tell(me - PLANE, 3)
+        if place == 2 and entered == 0:
+            tell(me + PLANE, 0)
+
+    for place in (1, 2):
+
+        @pl.when(plane == place)
+        def _(place=place):
+            tell(me - PLANE, place + 1)
+            tell(me + PLANE, place - 1)
 
     def events(group):
-        both(functools.partial(end_events, group), functools.partial(middle_events, group))
-
-    own_sends()
+        for place in range(LINE):
+            entries = EVENTS[place][group]
+            if entries:
+
+                @pl.when(plane == place)
+                def _(place=place, entries=entries):
+                    for origin, own, part_of, low, number in entries:
+                        if origin == -2:
+                            learn(place, own)
+                        if origin >= 0:
+                            piece(0, twin, line_of[origin][own], part_of).wait_recv()
+                        for slot in range(low, low + number):
+                            sent(place, slot).start()
+
+    events(0)
 
     for index in (1, 2, 3, 4):
         loads[index].wait()
+    events(1)
     gain = gain_row[...]
     bias = bias_row[...]
     leading = cls_row[...].astype(f32) + position[0:1, :].astype(f32)
     lead = jnp.broadcast_to(layer_norm(leading, gain, bias), (TILE_ROWS, width)).astype(bf16)
     lead_row = lead[:1].astype(f32)
 
+    events(2)
     placed = position[...].astype(f32)[1:]
     placed = placed - jnp.mean(placed, axis=1, keepdims=True)
     basis[padded:, :] = placed.astype(bf16)
-    scaled[padded:, :] = (placed * gain).astype(bf16)
+    scaled[padded : padded + spots, :] = (placed * gain).astype(bf16)
+    scaled[padded + spots :, :] = jnp.zeros((scaled.shape[0] - padded - spots, width), bf16)
     weight = jnp.sum(placed * placed, axis=1, keepdims=True)
     weight = jnp.transpose(jnp.broadcast_to(weight, (spots, 128)))[:1]
 
@@ -402,12 +403,14 @@
     basis[:padded, :] = table.astype(bf16)
     scaled[:padded, :] = (table * gain).astype(bf16)
 
+    events(3)
     loads[6].wait()
     query = jnp.dot(lead, query_w[...], preferred_element_type=f32)[:1]
     head_row = lax.broadcasted_iota(jnp.int32, (TILE_ROWS, inner), 0)
     column = lax.broadcasted_iota(jnp.int32, (TILE_ROWS, inner), 1)
     own_head = (column >= head_row * head_dim) & (column < (head_row + 1) * head_dim)
     spread = jnp.where(own_head, jnp.broadcast_to(query, (TILE_ROWS, inner)), 0.0).astype(bf16)
+    events(4)
     loads[7].wait()
     turned = contract_last(spread, key_w[...])[:heads] * (1.0 / math.sqrt(head_dim))
     first = jnp.sum(turned * lead_row, axis=1, keepdims=True)
@@ -415,11 +418,14 @@
     constants[...] = jnp.broadcast_to(level, constants.shape)
     probe = split_in_two(turned * gain)
 
-    events(0)
-
-    square = contract_last(basis[:padded, :], basis[...])
-    square = jnp.concatenate([square[:, :padded], 2.0 * square[:, padded:]], axis=1)
-    form[:padded, :] = square.astype(bf16)
+    for part_of in range(GRAM_PARTS):
+        events(5 + part_of)
+        low = TILE_ROWS * (tiles * part_of // GRAM_PARTS)
+        high = TILE_ROWS * (tiles * (part_of + 1) // GRAM_PARTS)
+        square = contract_last(basis[low:high, :], basis[...])
+        square = jnp.concatenate([square[:, :padded], 2.0 * square[:, padded:]], axis=1)
+        form[low:high, :] = square.astype(bf16)
+    events(5 + GRAM_PARTS)
     reach = contract_last(probe, basis[...])
     reach = split_in_two(reach[:heads] + reach[heads:])
     form[padded : padded + 2 * heads, :] = reach
@@ -430,10 +436,7 @@
     )
     form[padded + 2 * heads :, :] = sizes.astype(bf16)
 
-    events(1)
-
     loads[8].wait()
-    folded[...] = jnp.dot(scaled[...], value_w[...], preferred_element_type=f32).astype(bf16)
     ends = jnp.concatenate([split_in_two(bias), lead[:1], jnp.zeros((TILE_ROWS - 3, width), bf16)], axis=0)
     ends = jnp.dot(ends, value_w[...], preferred_element_type=f32)
     plain = ends[0:1] + ends[1:2]
@@ -452,30 +455,33 @@
     spot_lane = lax.broadcasted_iota(jnp.int32, (spots, cells), 1)
     spot_at = spot_row - (spot_lane // lanes) * rows - spot_lane % rows
 
-    delta_end = (0, 0, 2, 1, 2, 3, 1, 3)
-    delta_middle = (1, 1, 0, 2, 2, 0, 3, 3)
-    across_end = (0, 1, 0, 0, 1, 0, 1, 1)
-    across_middle = (0, 1, 0, 0, 1, 1, 0, 1)
-
-    def chip_step(turn, carry):
-        for index, group in ((2, 2), (3, 3), (4, 4), (5, 5), (6, 6), (7, 7)):
-            pl.when(turn == index)(functools.partial(events, group))
-        step = pick(turn, delta_end) * (1 - depth_in) + (pick(turn, delta_middle) - 1) * depth_in
-        across = pick(turn, across_end) * (1 - depth_in) + pick(turn, across_middle) * depth_in
-        where = plane + inward * step
-        base = where * PLANE + 2 * (side * (1 - across) + (1 - side) * across)
-        arrived(base + 1 - core, 0)
-        arrived(base + 1 - core, 1)
+    order = sum(mine * packed for mine, packed in zip(here, ORDER, strict=True))
+    first_step = 6 + GRAM_PARTS
+    fold_rows = scaled.shape[0] // FOLD_PARTS
+
+    def base_of(turn):
+        code = (order >> (3 * turn)) % 8
+        where, own = code // 2, code % 2
+        return where * PLANE + 2 * (side * own + (1 - side) * (1 - own))
+
+    def block_of(base):
         block = jnp.concatenate([slots[base], slots[base + 1]], axis=1)
         spot = jnp.where(spot_at == base * rows, 1.0, 0.0).astype(bf16)
-        block = jnp.concatenate([block, spot], axis=0)
+        return jnp.concatenate([block, spot], axis=0)
+
+    def front(base):
+        block = block_of(base)
         image = jnp.dot(form[...], block, preferred_element_type=f32)
         norm = jnp.sum(image[:padded] * block[:padded].astype(f32), axis=0, keepdims=True)
         tail = padded + 2 * heads
         norm = norm + image[tail : tail + 1] + image[tail + 1 : tail + 2]
         rate = lax.rsqrt(norm * (1.0 / width) + epsilon)
         scores = image[padded : padded + heads] + image[padded + heads : tail]
-        scores = scores * rate + constants[:, :1]
+        kept[:heads, :] = scores * rate + constants[:, :1]
+        kept[heads:, :] = jnp.broadcast_to(rate, (heads, cells))
+
+    def back(base, scores, rate):
+        block = block_of(base)
         scores = jnp.broadcast_to(scores[None], (images, heads, cells)).reshape(pairs, cells)
         scores = jnp.where(same, scores, LOWEST)
         before = peak[:, :1]
@@ -485,14 +491,40 @@
         peak[...] = jnp.broadcast_to(now, peak.shape)
         total[...] = total[...] * shrink + jnp.sum(chance, axis=1, keepdims=True)
         gathered[...] = gathered[...] * shrink + contract_last((chance * rate).astype(bf16), block)
+
+    def twin_pieces(base):
+        for part_of in range(PIECES):
+            piece(0, twin, base + 1 - core, part_of).wait_recv()
+
+    def chip_step(turn, carry):
+        for index in range(1, 2 * LINE):
+            pl.when(turn == index)(functools.partial(events, first_step + index))
+        base = base_of(turn)
+        twin_pieces(base)
+        scores = kept[:heads, :]
+        rate = kept[heads : heads + 1, :]
+        back(base_of(turn - 1), scores, rate)
+        front(base)
+
+        @pl.when(turn <= FOLD_PARTS)
+        def _():
+            low = pl.multiple_of((turn - 1) * fold_rows, TILE_ROWS)
+            folded[pl.ds(low, fold_rows), :] = jnp.dot(
+                scaled[pl.ds(low, fold_rows), :], value_w[...], preferred_element_type=f32
+            ).astype(bf16)
+
         return carry
 
-    lax.fori_loop(0, 2 * LINE, chip_step, 0)
+    events(first_step)
+    twin_pieces(base_of(0))
+    front(base_of(0))
+    lax.fori_loop(1, 2 * LINE, chip_step, 0)
+    back(base_of(2 * LINE - 1), kept[:heads, :], kept[heads : heads + 1, :])
 
     whole = total[:, :1]
     lead_chance = jnp.exp(first - peak[:, :1]) / whole
     pooled = split_in_two(gathered[...] / whole)
-    values = jnp.dot(pooled, folded[...], preferred_element_type=f32)
+    values = jnp.dot(pooled, folded[: padded + spots, :], preferred_element_type=f32)
     values = values[:pairs] + values[pairs:] + plain * (1.0 - lead_chance) + lead_value * lead_chance
     pair_head = lax.broadcasted_iota(jnp.int32, (pairs, inner), 0) % heads
     pair_column = lax.broadcasted_iota(jnp.int32, (pairs, inner), 1)
@@ -540,7 +572,8 @@
         )
 
     for step in range(1, chips):
-        pass_on(chip, 2 * ((chip + step) % chips) + core, step).start()
+        other = step - 1 + jnp.minimum(step // jnp.maximum(chip + 1, 1), 1)
+        pass_on(chip, 2 * other + core, step).start()
     for step in range(1, chips):
         pass_on((chip + step) % chips, me, step).wait_recv()
     every = ring[...]
@@ -556,19 +589,12 @@
     )
     share.start()
 
-    def settle(way, target, origin, part_of):
-        piece(way, target, origin, part_of).wait_send()
-
-    for way, target, origin, part_of, when in issued:
-        if when is None:
-            settle(way, target, origin, part_of)
-    for which in (end, middle):
-
-        @pl.when(which)
-        def _(which=which):
-            for way, target, origin, part_of, when in issued:
-                if when is which:
-                    settle(way, target, origin, part_of)
+    for place in range(LINE):
+
+        @pl.when(plane == place)
+        def _(place=place):
+            for slot in range(len(SENDS[place])):
+                sent(place, slot).wait_send()
 
     swap.wait_send()
     for step in range(1, chips):
@@ -613,6 +639,7 @@
     piece_width = pl.cdiv(classes, 256) * 128
     padded = pl.cdiv(depth, TILE_ROWS) * TILE_ROWS
     spots = pos_embed.shape[1] - 1
+    fold_rows = pl.cdiv(padded + spots, FOLD_PARTS * TILE_ROWS) * FOLD_PARTS * TILE_ROWS
     far = pl.BlockSpec(memory_space=pl.ANY)
     dma = pltpu.SemaphoreType.DMA
     f32, bf16 = jnp.float32, jnp.bfloat16
@@ -633,9 +660,8 @@
         lnf_bias,
         head_bias,
     )
-    whole = (True, False)
     held = [
-        pltpu.VMEM(a.shape[1:] if a.ndim == 3 and place else a.shape, a.dtype)
+        pltpu.VMEM(a.shape[1:] if place and a.ndim == 3 else a.shape, a.dtype)
         for place, a in enumerate(given)
     ]
     return pl.pallas_call(
@@ -647,10 +673,11 @@
             *held,
             pltpu.VMEM((count, padded, images * rows), bf16),
             pltpu.VMEM((padded + spots, width), bf16),
-            pltpu.VMEM((padded + spots, width), bf16),
+            pltpu.VMEM((fold_rows, width), bf16),
             pltpu.VMEM((padded + 2 * heads + TILE_ROWS, padded + spots), bf16),
-            pltpu.VMEM((padded + spots, inner), bf16),
+            pltpu.VMEM((fold_rows, inner), bf16),
             pltpu.VMEM((heads, 128), f32),
+            pltpu.VMEM((2 * heads, 2 * images * rows), f32),
             pltpu.VMEM((pairs, padded + spots), f32),
             pltpu.VMEM((pairs, 128), f32),
             pltpu.VMEM((pairs, 128), f32),
@@ -659,8 +686,9 @@
             pltpu.VMEM((chips, images, piece_width), f32),
             pltpu.VMEM((2, images, piece_width), f32),
             dma((len(given),)),
-            dma((count, 2)),
-            dma((5, count, 2)),
+            dma((count, PIECES)),
+            dma((max(len(place) for place in SENDS),)),
+            pltpu.SemaphoreType.REGULAR((LINE,)),
             dma((2,)),
             dma((2 + chips,)),
             dma((chips,)),

time: 44.4 us -> 40.3 us (0.908)
  Pallas kernels: 42.9 us -> 38.7 us
    pallas_call x1, Pallas kernels: 42.9 us -> 38.7 us  [kernel_shards(): pl.pallas_call(functools.partial(whole_kernel, count, heads), out_shape=j...]
where the time goes in v2:
time: 40.3 us; the launch traced here: 40.1 us
  Pallas kernels  38.7 us (96%)
  local copies, waits for them, and re-layouts  1.38 us (3%)
    pallas_call x1, Pallas kernels, kernel_shards(): pl.pallas_call(functools.partial(whole_kernel, count, heads), out_shape=j...  38.7 us
    unnamed x1, local copies, waits for them, and re-layouts  1.38 us

profile of v2, /device:TPU:0, one launch (start us, length us, event | category | flops | bytes accessed | tf_op | source)
XLA Modules:
  0.0 40.1 jit_solution(16177872362556034542)
XLA Ops:
  0.0 38.7 %shard_map.136 = f32[8,1000]{1,0:T(8,128)} custom-call(bf16[8,16,588]{2,1,0:T(8,128)(2,1)} %patches.1, bf16[1,1280]{1,0:T(2,128)(2,1)} %cls_token.1, bf16[1,257,1280]{2,1,0:T(8,128)(2,1)} %pos_embed.1, f32[1,1280]{1,0:T(1,128)} %ln1_gain.1, f32[1,1280]{1,0:T(1,128)} %ln1_bias.1, bf16[1,588,1280]{2,1,0:T(8,128)(2,1)} %patch_weight.1, ...), custom_call_target="tpu_custom_call" | custom-call | tf_op jit(solution)/shard_map/pallas_call | solution.py:667
  38.7 1.4 %copy.16 = f32[8,1000]{1,0:T(8,128)} copy(f32[8,1000]{1,0:T(8,128)} %shard_map.136) | data formatting | bytes 64000

commit v3 on v2

--- a/solution.py
+++ b/solution.py
@@ -109,7 +109,7 @@
 LINE = 4
 TILE_ROWS = 16
 LOWEST = -1e30
-GRAM_PARTS = 4
+GRAM_PARTS = 2
 FOLD_PARTS = 6
 
 
@@ -119,76 +119,89 @@
     return jnp.concatenate([high, low], axis=0)
 
 
-PIECES = 3
+PIECES = 4
 SENDS = (
     (
-        (1,1,0,1,0), (1,1,0,1,1), (0,0,0,1,0), (1,1,0,1,2), (0,0,0,1,2), (0,0,0,1,1), (0,2,0,1,0),
-        (0,2,0,1,1), (0,2,0,1,2), (3,1,0,1,0), (1,1,0,0,0), (2,1,0,1,2), (0,2,0,0,0), (0,0,1,1,0),
-        (0,2,1,1,0), (1,1,0,0,2), (3,1,0,0,2), (0,2,0,0,2), (0,0,1,1,2), (0,2,1,1,2), (3,1,0,0,1),
-        (0,2,0,0,1), (0,0,1,1,1), (0,2,1,1,1), (0,2,1,0,0), (0,2,1,0,2), (0,0,2,1,2), (0,2,2,1,2),
-        (0,2,1,0,1), (0,0,3,1,0), (0,2,3,1,0), (0,0,2,1,1), (0,2,2,1,1), (0,0,2,1,0), (0,2,2,1,0),
-        (0,2,2,0,2), (0,2,3,0,0), (0,2,3,0,2), (0,2,2,0,1), (0,2,3,1,1), (0,2,3,0,1), (0,2,2,0,0),
-        (0,2,3,1,2),
+        (0,0,0,1,0), (1,1,0,1,0), (1,1,0,1,2), (1,1,0,1,3), (0,0,0,1,3), (0,0,0,1,1), (1,1,0,1,1),
+        (0,0,0,1,2), (0,2,0,1,0), (0,2,0,1,1), (0,2,0,1,2), (0,2,0,1,3), (2,1,0,1,1), (1,1,0,0,0),
+        (0,2,0,0,0), (0,0,1,1,0), (0,2,1,1,0), (2,1,0,0,3), (3,1,0,0,3), (1,1,0,0,3), (0,2,0,0,3),
+        (0,0,1,1,2), (0,2,1,1,2), (1,1,0,0,1), (2,1,0,0,1), (0,2,0,0,1), (0,0,1,1,1), (0,2,1,1,1),
+        (2,1,0,0,2), (3,1,0,0,2), (0,2,0,0,2), (0,0,1,1,3), (0,2,1,1,3), (0,2,1,0,0), (0,2,1,0,2),
+        (0,0,2,1,1), (0,2,2,1,1), (0,2,1,0,1), (0,0,2,1,2), (0,2,2,1,2), (0,2,1,0,3), (0,0,2,1,3),
+        (0,2,2,1,3), (0,0,2,1,0), (0,2,2,1,0), (0,2,2,0,1), (0,2,3,1,3), (0,2,2,0,2), (0,2,3,0,1),
+        (0,0,3,1,0), (0,2,3,1,0), (0,2,2,0,3), (0,2,3,0,3), (0,2,2,0,0), (0,2,3,1,2), (0,2,3,0,2),
+        (0,2,3,1,1), (0,2,3,0,0),
     ),
     (
-        (0,1,1,1,0), (1,0,1,1,1), (0,1,1,1,2), (0,1,1,1,1), (2,1,1,1,2), (2,1,1,1,1), (1,0,1,1,0),
-        (2,1,1,1,0), (1,2,1,1,0), (1,2,1,1,1), (1,2,1,1,2), (2,1,0,1,0), (1,2,0,1,0), (1,2,1,0,1),
-        (1,0,0,1,1), (2,1,0,1,1), (1,2,0,1,1), (1,0,2,1,2), (0,1,2,1,2), (1,2,2,1,2), (1,2,1,0,0),
-        (1,2,0,1,2), (1,0,1,1,2), (0,1,2,1,1), (1,0,2,1,1), (1,2,2,1,1), (1,0,2,1,0), (0,1,2,1,0),
-        (1,2,2,1,0), (1,2,0,0,1), (1,2,0,0,0), (1,2,2,0,2), (1,0,3,1,0), (1,2,3,1,0), (1,2,1,0,2),
-        (1,2,0,0,2), (0,1,3,1,1), (1,0,3,1,1), (1,2,3,1,1), (1,2,2,0,1), (1,0,3,1,2), (0,1,3,1,2),
-        (1,2,3,1,2), (1,2,2,0,0), (1,2,3,0,0), (1,2,3,0,1), (1,2,3,0,2),
+        (0,1,1,1,0), (2,1,1,1,1), (1,0,1,1,1), (2,1,1,1,0), (0,1,1,1,2), (2,1,1,1,2), (1,0,1,1,0),
+        (0,1,1,1,1), (0,1,1,1,3), (1,0,1,1,3), (1,0,1,1,2), (2,1,1,1,3), (1,2,1,1,0), (1,2,1,1,1),
+        (1,2,1,1,2), (1,2,1,1,3), (2,1,0,1,0), (1,2,0,1,0), (1,2,1,0,1), (2,1,0,1,2), (1,0,0,1,2),
+        (1,2,0,1,2), (1,2,1,0,0), (1,0,2,1,1), (0,1,2,1,1), (1,2,2,1,1), (2,1,0,1,3), (1,2,0,1,3),
+        (1,2,1,0,3), (0,1,2,1,2), (1,0,2,1,2), (1,2,2,1,2), (1,2,0,1,1), (1,2,1,0,2), (0,1,2,1,3),
+        (1,0,2,1,3), (1,2,2,1,3), (0,1,2,1,0), (1,0,2,1,0), (1,2,2,1,0), (1,2,0,0,2), (1,2,0,0,0),
+        (0,1,3,1,3), (1,0,3,1,3), (1,2,3,1,3), (1,2,2,0,1), (1,2,2,0,2), (0,1,3,1,0), (1,0,3,1,0),
+        (1,2,3,1,0), (1,2,2,0,3), (1,2,2,0,0), (1,2,3,0,1), (1,2,0,0,3), (1,0,3,1,2), (0,1,3,1,2),
+        (1,2,3,1,2), (1,2,3,0,3), (1,2,0,0,1), (0,1,3,1,1), (1,2,3,1,1), (1,2,3,0,0), (1,2,3,0,2),
     ),
     (
-        (3,1,2,1,0), (2,0,2,1,1), (3,1,2,1,2), (3,1,2,1,1), (1,1,2,1,2), (1,1,2,1,1), (2,0,2,1,0),
-        (1,1,2,1,0), (2,2,2,1,0), (2,2,2,1,1), (2,2,2,1,2), (2,0,1,1,2), (3,1,1,1,2), (2,2,1,1,2),
-        (2,2,2,0,1), (2,0,2,1,2), (3,1,1,1,1), (2,0,1,1,1), (2,2,1,1,1), (1,1,3,1,0), (2,2,3,1,0),
-        (2,2,2,0,0), (2,0,1,1,0), (3,1,1,1,0), (2,2,1,1,0), (2,0,3,1,1), (1,1,3,1,1), (2,2,3,1,1),
-        (2,2,3,1,2), (2,2,1,0,2), (2,0,0,1,0), (2,2,0,1,0), (2,2,2,0,2), (3,1,0,1,1), (2,0,0,1,1),
-        (2,2,0,1,1), (2,2,1,0,1), (2,2,3,0,0), (2,0,0,1,2), (3,1,0,1,2), (2,2,0,1,2), (2,2,1,0,0),
-        (2,2,3,0,1), (2,2,0,0,0), (2,2,3,0,2), (2,2,0,0,1), (2,2,0,0,2),
+        (1,1,2,1,1), (2,0,2,1,1), (3,1,2,1,0), (1,1,2,1,2), (2,0,2,1,3), (1,1,2,1,3), (1,1,2,1,0),
+        (3,1,2,1,2), (3,1,2,1,1), (2,0,2,1,2), (3,1,2,1,3), (2,2,2,1,0), (2,2,2,1,1), (2,2,2,1,2),
+        (2,2,2,1,3), (3,1,1,1,1), (2,0,1,1,1), (2,2,1,1,1), (3,1,1,1,0), (2,0,1,1,0), (2,2,1,1,0),
+        (2,2,2,0,1), (3,1,1,1,2), (2,0,1,1,2), (2,2,1,1,2), (1,1,3,1,0), (2,0,3,1,0), (2,2,3,1,0),
+        (2,2,2,0,3), (1,1,3,1,2), (2,0,3,1,2), (2,2,3,1,2), (2,2,2,0,2), (3,1,1,1,3), (2,0,1,1,3),
+        (2,2,1,1,3), (1,1,3,1,1), (2,2,3,1,1), (2,2,1,0,1), (3,1,0,1,1), (2,0,2,1,0), (2,2,0,1,1),
+        (2,0,0,1,0), (3,1,0,1,0), (2,2,0,1,0), (2,2,3,1,3), (2,2,1,0,0), (3,1,0,1,2), (2,2,0,1,2),
+        (2,2,1,0,2), (2,2,3,0,1), (2,2,0,0,3), (2,2,3,0,0), (3,1,0,1,3), (2,2,0,1,3), (2,2,3,0,2),
+        (2,2,1,0,3), (2,2,2,0,0), (2,2,0,0,0), (2,2,3,0,3), (2,2,0,0,1), (2,2,0,0,2),
     ),
     (
-        (2,1,3,1,0), (2,1,3,1,1), (3,0,3,1,0), (2,1,3,1,2), (3,0,3,1,2), (3,0,3,1,1), (3,2,3,1,0),
-        (3,2,3,1,1), (3,2,3,1,2), (0,1,3,1,0), (3,0,2,1,0), (3,2,2,1,0), (2,1,3,0,0), (1,1,3,1,2),
-        (3,2,3,0,0), (3,0,2,1,2), (3,2,2,1,2), (2,1,3,0,2), (0,1,3,0,2), (3,2,3,0,2), (0,1,3,0,1),
-        (3,2,3,0,1), (3,0,2,1,1), (3,2,2,1,1), (3,2,2,0,0), (3,0,0,1,0), (3,2,0,1,0), (3,0,1,1,2),
-        (3,2,1,1,2), (3,0,1,1,1), (3,2,1,1,1), (3,2,2,0,2), (3,0,1,1,0), (3,2,1,1,0), (3,2,2,0,1),
-        (3,2,0,0,0), (3,2,0,0,2), (3,2,1,0,2), (3,2,0,1,1), (3,2,1,0,1), (3,2,0,0,1), (3,2,0,1,2),
-        (3,2,1,0,0),
+        (2,1,3,1,0), (3,0,3,1,1), (2,1,3,1,2), (3,0,3,1,3), (2,1,3,1,1), (2,1,3,1,3), (3,0,3,1,2),
+        (3,2,3,1,0), (3,2,3,1,1), (3,2,3,1,2), (3,2,3,1,3), (1,1,3,1,3), (3,0,2,1,0), (3,2,2,1,0),
+        (3,0,3,1,0), (2,1,3,0,1), (1,1,3,0,1), (0,1,3,0,1), (3,2,3,0,1), (3,0,2,1,2), (3,2,2,1,2),
+        (2,1,3,0,3), (0,1,3,0,3), (3,2,3,0,3), (3,0,2,1,1), (3,2,2,1,1), (0,1,3,0,2), (3,2,3,0,2),
+        (3,0,2,1,3), (3,2,2,1,3), (3,0,1,1,1), (3,2,1,1,1), (3,2,2,0,0), (3,0,1,1,0), (3,2,1,1,0),
+        (3,0,1,1,2), (3,2,1,1,2), (3,2,3,0,0), (3,2,2,0,2), (3,2,2,0,1), (3,0,1,1,3), (3,2,1,1,3),
+        (3,2,2,0,3), (3,0,0,1,1), (3,2,0,1,1), (3,2,0,0,3), (3,2,1,0,1), (3,0,0,1,0), (3,2,0,1,0),
+        (3,2,1,0,0), (3,2,0,1,2), (3,2,1,0,2), (3,2,0,1,3), (3,2,1,0,3), (3,2,0,0,1), (3,2,0,0,2),
+        (3,2,0,0,0),
     ),
 )
 EVENTS = (
     (
-        ((-1,0,0,0,9),), (), (), ((-2,2,0,9,0),), (), ((-2,3,0,9,1),), (), ((0,0,0,10,3),(1,1,0,13,2)), (),
-        ((0,0,2,15,3),(1,1,2,18,2)), (), ((0,0,1,20,2),(1,1,1,22,2)), (),
-        ((1,0,0,24,1),(1,0,2,25,1),(2,1,2,26,2),(1,0,1,28,1)), ((3,1,0,29,2),(2,1,1,31,2),(2,1,0,33,2)),
-        ((2,0,2,35,1),(3,0,0,36,1),(3,0,2,37,1),(2,0,1,38,1),(3,1,1,39,1),(3,0,1,40,1)),
-        ((2,0,0,41,1),(3,1,2,42,1)), (),
+        ((-1,0,0,0,12),), (), (), ((-2,2,0,12,1),), (), (), ((0,0,0,13,2),(-2,3,0,15,0),(1,1,0,15,2)),
+        ((0,0,3,17,4),(1,1,2,21,2),(0,0,1,23,3)), ((1,1,1,26,2),(0,0,2,28,3),(1,1,3,31,2)), (),
+        ((1,0,0,33,1),), (), ((1,0,2,34,1),(2,1,1,35,2)), ((1,0,1,37,1),(2,1,2,38,2),(1,0,3,40,1)),
+        ((2,1,3,41,2),(2,1,0,43,2)), (), ((2,0,1,45,1),(3,1,3,46,1),(2,0,2,47,1),(3,0,1,48,1)),
+        ((3,1,0,49,2),(2,0,3,51,1),(3,0,3,52,1),(2,0,0,53,1)), ((3,1,2,54,1),(3,0,2,55,1),(3,1,1,56,1)),
+        ((3,0,0,57,1),), (), (),
     ),
     (
-        ((-1,0,0,0,11),), (), (), (), ((-2,3,0,11,0),), (), (), ((0,1,0,11,2),(1,0,1,13,1)), (),
-        ((0,1,1,14,3),(2,1,2,17,3),(1,0,0,20,1)), (), ((0,1,2,21,1),(2,1,1,22,4)), ((2,1,0,26,3),),
-        ((0,0,1,29,1),(0,0,0,30,1),(2,0,2,31,1),(3,1,0,32,2),(1,0,2,34,1)),
-        ((0,0,2,35,1),(3,1,1,36,3),(2,0,1,39,1),(3,1,2,40,3),(2,0,0,43,1)), (), ((3,0,0,44,1),),
-        ((3,0,1,45,1),(3,0,2,46,1)),
+        ((-1,0,0,0,16),), (), (), (), ((-2,3,0,16,0),), ((0,1,0,16,2),), ((1,0,1,18,1),(0,1,2,19,3)),
+        ((1,0,0,22,1),(2,1,1,23,3),(0,1,3,26,2),(1,0,3,28,1),(2,1,2,29,3),(0,1,1,32,1)),
+        ((1,0,2,33,1),(2,1,3,34,3)), ((2,1,0,37,3),), ((0,0,2,40,1),), ((0,0,0,41,1),),
+        ((3,1,3,42,3),(2,0,1,45,1)), (), ((2,0,2,46,1),(3,1,0,47,3)), ((2,0,3,50,1),(2,0,0,51,1)),
+        ((3,0,1,52,1),(0,0,3,53,1),(3,1,2,54,3),(3,0,3,57,1),(0,0,1,58,1)), ((3,1,1,59,2),), ((3,0,0,61,1),),
+        (), (), ((3,0,2,62,1),),
     ),
     (
-        ((-1,0,0,0,11),), ((-2,0,0,11,0),), (), (), (), ((1,1,2,11,3),), (), ((2,0,1,14,1),(1,1,1,15,4)), (),
-        ((3,1,0,19,2),(2,0,0,21,1)), ((1,1,0,22,3),), ((3,1,1,25,3),),
-        ((3,1,2,28,1),(1,0,2,29,1),(0,1,0,30,2)), ((2,0,2,32,1),),
-        ((0,1,1,33,3),(1,0,1,36,1),(3,0,0,37,1),(0,1,2,38,3),(1,0,0,41,1)), ((3,0,1,42,1),),
-        ((0,0,0,43,1),(3,0,2,44,1)), ((0,0,1,45,1),(0,0,2,46,1)),
+        ((-1,0,0,0,15),), ((-2,0,0,15,0),), (), (), (), ((1,1,1,15,3),),
+        ((1,1,0,18,3),(2,0,1,21,1),(1,1,2,22,3)),
+        ((3,1,0,25,3),(2,0,3,28,1),(3,1,2,29,3),(2,0,2,32,1),(1,1,3,33,3)),
+        ((3,1,1,36,2),(1,0,1,38,1),(0,1,1,39,3),(0,1,0,42,3),(3,1,3,45,1)), (), ((1,0,0,46,1),(0,1,2,47,2)),
+        ((1,0,2,49,1),(3,0,1,50,1)), ((0,0,3,51,1),(3,0,0,52,1)), ((0,1,3,53,2),(3,0,2,55,1)),
+        ((1,0,3,56,1),(2,0,0,57,1)), (), ((0,0,0,58,1),(3,0,3,59,1),(0,0,1,60,1)), ((0,0,2,61,1),), (), (),
+        (), (),
     ),
     (
-        ((-1,0,0,0,9),), ((-2,0,0,9,1),(-2,1,0,10,0)), (), (), (), (), ((2,1,0,10,2),), ((3,0,0,12,3),),
-        ((2,1,2,15,2),), ((3,0,2,17,3),), (), ((3,0,1,20,2),(2,1,1,22,2)),
-        ((2,0,0,24,1),(0,1,0,25,2),(1,1,2,27,2)), ((1,1,1,29,2),(2,0,2,31,1),(1,1,0,32,2)),
-        ((2,0,1,34,1),(0,0,0,35,1)), ((0,0,2,36,1),(1,0,2,37,1),(0,1,1,38,1),(1,0,1,39,1),(0,0,1,40,1)),
-        ((0,1,2,41,1),(1,0,0,42,1)), (),
+        ((-1,0,0,0,11),), ((-2,1,0,11,1),(-2,0,0,12,0)), (), (), (), ((2,1,0,12,2),),
+        ((3,0,1,14,5),(2,1,2,19,2)), ((3,0,3,21,3),(2,1,1,24,2),(3,0,2,26,2),(2,1,3,28,2)),
+        ((1,1,1,30,2),(2,0,0,32,1)), ((1,1,0,33,2),), ((1,1,2,35,2),(3,0,0,37,1)), (),
+        ((2,0,2,38,1),(2,0,1,39,1),(1,1,3,40,2)), ((2,0,3,42,1),(0,1,1,43,2)),
+        ((0,0,3,45,1),(1,0,1,46,1),(0,1,0,47,2)), ((1,0,0,49,1),(0,1,2,50,1)), ((1,0,2,51,1),(0,1,3,52,1)),
+        ((1,0,3,53,1),), ((0,0,1,54,1),(0,0,2,55,1)), ((0,0,0,56,1),), (), (),
     ),
 )
-ORDER = (15946945, 13862219, 1645021, 4474743)
+ORDER = (14570689, 14437003, 1713117, 575407)
 
 
 def contract_last(left, right):
@@ -390,7 +403,8 @@
     events(2)
     placed = position[...].astype(f32)[1:]
     placed = placed - jnp.mean(placed, axis=1, keepdims=True)
-    basis[padded:, :] = placed.astype(bf16)
+    top = 2 * heads
+    basis[top + padded :, :] = placed.astype(bf16)
     scaled[padded : padded + spots, :] = (placed * gain).astype(bf16)
     scaled[padded + spots :, :] = jnp.zeros((scaled.shape[0] - padded - spots, width), bf16)
     weight = jnp.sum(placed * placed, axis=1, keepdims=True)
@@ -400,7 +414,7 @@
     table = embed[...].astype(f32)
     table = table - jnp.mean(table, axis=1, keepdims=True)
     table = jnp.concatenate([table, jnp.zeros((padded - depth, width), f32)], axis=0)
-    basis[:padded, :] = table.astype(bf16)
+    basis[top : top + padded, :] = table.astype(bf16)
     scaled[:padded, :] = (table * gain).astype(bf16)
 
     events(3)
@@ -416,25 +430,25 @@
     first = jnp.sum(turned * lead_row, axis=1, keepdims=True)
     level = jnp.sum(turned * bias, axis=1, keepdims=True)
     constants[...] = jnp.broadcast_to(level, constants.shape)
-    probe = split_in_two(turned * gain)
-
+    basis[:top, :] = split_in_two(turned * gain)
+
+    features = padded + spots
     for part_of in range(GRAM_PARTS):
         events(5 + part_of)
-        low = TILE_ROWS * (tiles * part_of // GRAM_PARTS)
-        high = TILE_ROWS * (tiles * (part_of + 1) // GRAM_PARTS)
-        square = contract_last(basis[low:high, :], basis[...])
-        square = jnp.concatenate([square[:, :padded], 2.0 * square[:, padded:]], axis=1)
-        form[low:high, :] = square.astype(bf16)
-    events(5 + GRAM_PARTS)
-    reach = contract_last(probe, basis[...])
-    reach = split_in_two(reach[:heads] + reach[heads:])
-    form[padded : padded + 2 * heads, :] = reach
+        low = 256 * (pl.cdiv(features, 256) * part_of // GRAM_PARTS)
+        high = min(features, 256 * (pl.cdiv(features, 256) * (part_of + 1) // GRAM_PARTS))
+        square = contract_last(basis[: top + padded, :], basis[top + low : top + high, :])
+        place = low + lax.broadcasted_iota(jnp.int32, (padded, high - low), 1)
+        form[top : top + padded, low:high] = jnp.where(
+            place < padded, square[top:], 2.0 * square[top:]
+        ).astype(bf16)
+        form[:top, low:high] = split_in_two(square[:heads] + square[heads:top])
     sizes = jnp.concatenate([jnp.zeros((1, padded), f32), weight], axis=1)
     sizes_high = sizes.astype(bf16).astype(f32)
     sizes = jnp.concatenate(
         [sizes_high, sizes - sizes_high, jnp.zeros((TILE_ROWS - 2, padded + spots), f32)], axis=0
     )
-    form[padded + 2 * heads :, :] = sizes.astype(bf16)
+    form[top + padded :, :] = sizes.astype(bf16)
 
     loads[8].wait()
     ends = jnp.concatenate([split_in_two(bias), lead[:1], jnp.zeros((TILE_ROWS - 3, width), bf16)], axis=0)
@@ -456,7 +470,7 @@
     spot_at = spot_row - (spot_lane // lanes) * rows - spot_lane % rows
 
     order = sum(mine * packed for mine, packed in zip(here, ORDER, strict=True))
-    first_step = 6 + GRAM_PARTS
+    first_step = 5 + GRAM_PARTS
     fold_rows = scaled.shape[0] // FOLD_PARTS
 
     def base_of(turn):
@@ -472,11 +486,13 @@
     def front(base):
         block = block_of(base)
         image = jnp.dot(form[...], block, preferred_element_type=f32)
-        norm = jnp.sum(image[:padded] * block[:padded].astype(f32), axis=0, keepdims=True)
-        tail = padded + 2 * heads
+        norm = jnp.sum(
+            image[top : top + padded] * block[:padded].astype(f32), axis=0, keepdims=True
+        )
+        tail = top + padded
         norm = norm + image[tail : tail + 1] + image[tail + 1 : tail + 2]
         rate = lax.rsqrt(norm * (1.0 / width) + epsilon)
-        scores = image[padded : padded + heads] + image[padded + heads : tail]
+        scores = image[:heads] + image[heads:top]
         kept[:heads, :] = scores * rate + constants[:, :1]
         kept[heads:, :] = jnp.broadcast_to(rate, (heads, cells))
 
@@ -497,8 +513,8 @@
             piece(0, twin, base + 1 - core, part_of).wait_recv()
 
     def chip_step(turn, carry):
-        for index in range(1, 2 * LINE):
-            pl.when(turn == index)(functools.partial(events, first_step + index))
+        for index in range(1, 2 * LINE - 1):
+            pl.when(turn == index)(functools.partial(events, first_step + 2 * index))
         base = base_of(turn)
         twin_pieces(base)
         scores = kept[:heads, :]
@@ -506,6 +522,9 @@
         back(base_of(turn - 1), scores, rate)
         front(base)
 
+        for index in range(1, FOLD_PARTS + 1):
+            pl.when(turn == index)(functools.partial(events, first_step + 2 * index + 1))
+
         @pl.when(turn <= FOLD_PARTS)
         def _():
             low = pl.multiple_of((turn - 1) * fold_rows, TILE_ROWS)
@@ -518,7 +537,12 @@
     events(first_step)
     twin_pieces(base_of(0))
     front(base_of(0))
-    lax.fori_loop(1, 2 * LINE, chip_step, 0)
+    events(first_step + 1)
+    lax.fori_loop(1, 2 * LINE - 1, chip_step, 0)
+    back(base_of(2 * LINE - 2), kept[:heads, :], kept[heads : heads + 1, :])
+    events(first_step + 4 * LINE - 2)
+    twin_pieces(base_of(2 * LINE - 1))
+    front(base_of(2 * LINE - 1))
     back(base_of(2 * LINE - 1), kept[:heads, :], kept[heads : heads + 1, :])
 
     whole = total[:, :1]
@@ -672,7 +696,7 @@
         scratch_shapes=[
             *held,
             pltpu.VMEM((count, padded, images * rows), bf16),
-            pltpu.VMEM((padded + spots, width), bf16),
+            pltpu.VMEM((2 * heads + padded + spots, width), bf16),
             pltpu.VMEM((fold_rows, width), bf16),
             pltpu.VMEM((padded + 2 * heads + TILE_ROWS, padded + spots), bf16),
             pltpu.VMEM((fold_rows, inner), bf16),

time: 40.3 us -> 36.1 us (0.90)
  Pallas kernels: 38.7 us -> 34.5 us
    pallas_call x1, Pallas kernels: 38.7 us -> 34.5 us  [kernel_shards(): pl.pallas_call(functools.partial(whole_kernel, count, heads), out_shape=j...]
where the time goes in v3:
time: 36.1 us; the launch traced here: 35.9 us
  Pallas kernels  34.5 us (96%)
  local copies, waits for them, and re-layouts  1.38 us (4%)
    pallas_call x1, Pallas kernels, kernel_shards(): pl.pallas_call(functools.partial(whole_kernel, count, heads), out_shape=j...  34.5 us
    unnamed x1, local copies, waits for them, and re-layouts  1.38 us

profile of v3, /device:TPU:0, one launch (start us, length us, event | category | flops | bytes accessed | tf_op | source)
XLA Modules:
  0.0 35.9 jit_solution(8981795048844051891)
XLA Ops:
  0.0 34.5 %shard_map.136 = f32[8,1000]{1,0:T(8,128)} custom-call(bf16[8,16,588]{2,1,0:T(8,128)(2,1)} %patches.1, bf16[1,1280]{1,0:T(2,128)(2,1)} %cls_token.1, bf16[1,257,1280]{2,1,0:T(8,128)(2,1)} %pos_embed.1, f32[1,1280]{1,0:T(1,128)} %ln1_gain.1, f32[1,1280]{1,0:T(1,128)} %ln1_bias.1, bf16[1,588,1280]{2,1,0:T(8,128)(2,1)} %patch_weight.1, ...), custom_call_target="tpu_custom_call" | custom-call | tf_op jit(solution)/shard_map/pallas_call | solution.py:691
  34.5 1.4 %copy.16 = f32[8,1000]{1,0:T(8,128)} copy(f32[8,1000]{1,0:T(8,128)} %shard_map.136) | data formatting | bytes 64000

commit v4 on v3

--- a/solution.py
+++ b/solution.py
@@ -247,6 +247,7 @@
     scaled,
     form,
     folded,
+    ends,
     constants,
     kept,
     gathered,
@@ -258,11 +259,11 @@
     result,
     load_sem,
     recv_sem,
+    twin_sem,
     sent_sem,
     known_sem,
     tail_send,
     tail_recv,
-    spread_sem,
 ):
     f32, bf16 = jnp.float32, jnp.bfloat16
     me = lax.axis_index("sample")
@@ -338,22 +339,44 @@
     slots[me] = contract_last(eye, flat).astype(bf16)
     pl.semaphore_wait(barrier, LINE - here[0] - here[LINE - 1])
 
-    def piece(slot, target, origin, part_of):
-        low, high = cuts[part_of], cuts[part_of + 1]
-        ref = slots.at[origin, pl.ds(low, high - low)]
+    def passing(ref, target, sent_by, got_by):
         return pltpu.make_async_remote_copy(
             src_ref=ref,
             dst_ref=ref,
-            send_sem=sent_sem.at[slot],
-            recv_sem=recv_sem.at[origin, part_of],
+            send_sem=sent_by,
+            recv_sem=got_by,
             device_id={"sample": target},
             device_id_type=MESH,
         )
 
+    def rows_of(part_of):
+        return pl.ds(cuts[part_of], cuts[part_of + 1] - cuts[part_of])
+
     def sent(place, slot):
         to, aside, origin, own, part_of = SENDS[place][slot]
-        target = twin if aside == 2 else line_of[to][aside]
-        return piece(slot, target, line_of[origin][own], part_of)
+        inside = aside // 2
+        source = line_of[origin][own]
+        got_by = twin_sem.at[source // 2] if inside else recv_sem.at[source // 2, part_of]
+        target = twin if inside else line_of[to][aside]
+        ref = slots.at[source, rows_of(part_of)]
+        return passing(ref, target, sent_sem.at[inside, part_of], got_by)
+
+    def got(source, part_of):
+        ref = slots.at[source, rows_of(part_of)]
+        passing(ref, twin, sent_sem.at[0, 0], recv_sem.at[source // 2, part_of]).wait_recv()
+
+    def got_from_twin(base):
+        ref = slots.at[base + 1 - core]
+        passing(ref, twin, sent_sem.at[0, 0], twin_sem.at[base // 2]).wait_recv()
+
+    def all_sent(place):
+        for inside in range(2):
+            for part_of in range(PIECES):
+                number = sum(
+                    1 for entry in SENDS[place] if (entry[1] // 2, entry[4]) == (inside, part_of)
+                )
+                ref = slots.at[pl.ds(0, number), rows_of(part_of)]
+                passing(ref, twin, sent_sem.at[inside, part_of], twin_sem.at[0]).wait_send()
 
     def tell(target, entered):
         pl.semaphore_signal(
@@ -385,7 +408,7 @@
                         if origin == -2:
                             learn(place, own)
                         if origin >= 0:
-                            piece(0, twin, line_of[origin][own], part_of).wait_recv()
+                            got(line_of[origin][own], part_of)
                         for slot in range(low, low + number):
                             sent(place, slot).start()
 
@@ -406,7 +429,9 @@
     top = 2 * heads
     basis[top + padded :, :] = placed.astype(bf16)
     scaled[padded : padded + spots, :] = (placed * gain).astype(bf16)
-    scaled[padded + spots :, :] = jnp.zeros((scaled.shape[0] - padded - spots, width), bf16)
+    scaled[padded + spots :, :] = jnp.concatenate(
+        [split_in_two(bias), lead[:1], jnp.zeros((ends.shape[0] - 3, width), bf16)], axis=0
+    )
     weight = jnp.sum(placed * placed, axis=1, keepdims=True)
     weight = jnp.transpose(jnp.broadcast_to(weight, (spots, 128)))[:1]
 
@@ -451,11 +476,6 @@
     form[top + padded :, :] = sizes.astype(bf16)
 
     loads[8].wait()
-    ends = jnp.concatenate([split_in_two(bias), lead[:1], jnp.zeros((TILE_ROWS - 3, width), bf16)], axis=0)
-    ends = jnp.dot(ends, value_w[...], preferred_element_type=f32)
-    plain = ends[0:1] + ends[1:2]
-    lead_value = ends[2:3]
-
     first = jnp.broadcast_to(first[None], (images, heads, 1)).reshape(pairs, 1)
     peak[...] = jnp.broadcast_to(first, peak.shape)
     total[...] = jnp.ones(total.shape, f32)
@@ -508,15 +528,11 @@
         total[...] = total[...] * shrink + jnp.sum(chance, axis=1, keepdims=True)
         gathered[...] = gathered[...] * shrink + contract_last((chance * rate).astype(bf16), block)
 
-    def twin_pieces(base):
-        for part_of in range(PIECES):
-            piece(0, twin, base + 1 - core, part_of).wait_recv()
-
     def chip_step(turn, carry):
-        for index in range(1, 2 * LINE - 1):
+        for index in range(1, 2 * LINE):
             pl.when(turn == index)(functools.partial(events, first_step + 2 * index))
         base = base_of(turn)
-        twin_pieces(base)
+        got_from_twin(base)
         scores = kept[:heads, :]
         rate = kept[heads : heads + 1, :]
         back(base_of(turn - 1), scores, rate)
@@ -528,28 +544,30 @@
         @pl.when(turn <= FOLD_PARTS)
         def _():
             low = pl.multiple_of((turn - 1) * fold_rows, TILE_ROWS)
-            folded[pl.ds(low, fold_rows), :] = jnp.dot(
+            product = jnp.dot(
                 scaled[pl.ds(low, fold_rows), :], value_w[...], preferred_element_type=f32
-            ).astype(bf16)
+            )
+            folded[pl.ds(low, fold_rows), :] = product.astype(bf16)
+            ends[...] = product[fold_rows - ends.shape[0] :]
 
         return carry
 
     events(first_step)
-    twin_pieces(base_of(0))
+    got_from_twin(base_of(0))
     front(base_of(0))
     events(first_step + 1)
-    lax.fori_loop(1, 2 * LINE - 1, chip_step, 0)
-    back(base_of(2 * LINE - 2), kept[:heads, :], kept[heads : heads + 1, :])
-    events(first_step + 4 * LINE - 2)
-    twin_pieces(base_of(2 * LINE - 1))
-    front(base_of(2 * LINE - 1))
+    lax.fori_loop(1, 2 * LINE, chip_step, 0)
     back(base_of(2 * LINE - 1), kept[:heads, :], kept[heads : heads + 1, :])
 
-    whole = total[:, :1]
-    lead_chance = jnp.exp(first - peak[:, :1]) / whole
-    pooled = split_in_two(gathered[...] / whole)
-    values = jnp.dot(pooled, folded[: padded + spots, :], preferred_element_type=f32)
-    values = values[:pairs] + values[pairs:] + plain * (1.0 - lead_chance) + lead_value * lead_chance
+    plain = ends[0:1, :] + ends[1:2, :]
+    lead_value = ends[2:3, :]
+    values = jnp.dot(
+        split_in_two(gathered[...]), folded[: padded + spots, :], preferred_element_type=f32
+    )
+    share = 1.0 / total[:, :1]
+    lead_chance = jnp.exp(first - peak[:, :1]) * share
+    values = (values[:pairs] + values[pairs:]) * share
+    values = values + plain + (lead_value - plain) * lead_chance
     pair_head = lax.broadcasted_iota(jnp.int32, (pairs, inner), 0) % heads
     pair_column = lax.broadcasted_iota(jnp.int32, (pairs, inner), 1)
     mine_only = (pair_column >= pair_head * head_dim) & (pair_column < (pair_head + 1) * head_dim)
@@ -585,21 +603,13 @@
     high = jnp.maximum(mine, theirs)
     ring[chip] = high + jnp.log(jnp.exp(mine - high) + jnp.exp(theirs - high))
 
-    def pass_on(origin, target, step):
-        return pltpu.make_async_remote_copy(
-            src_ref=ring.at[origin],
-            dst_ref=ring.at[origin],
-            send_sem=spread_sem.at[step],
-            recv_sem=tail_recv.at[2 + origin],
-            device_id={"sample": target},
-            device_id_type=MESH,
-        )
+    def pass_on(ref, target):
+        return passing(ref, target, tail_send.at[2], tail_recv.at[2])
 
     for step in range(1, chips):
         other = step - 1 + jnp.minimum(step // jnp.maximum(chip + 1, 1), 1)
-        pass_on(chip, 2 * other + core, step).start()
-    for step in range(1, chips):
-        pass_on((chip + step) % chips, me, step).wait_recv()
+        pass_on(ring.at[chip], 2 * other + core).start()
+    pass_on(ring.at[pl.ds(0, chips - 1)], twin).wait_recv()
     every = ring[...]
     high = jnp.max(every, axis=0)
     result[core] = high + jnp.log(jnp.sum(jnp.exp(every - high[None]), axis=0)) - math.log(count)
@@ -617,12 +627,10 @@
 
         @pl.when(plane == place)
         def _(place=place):
-            for slot in range(len(SENDS[place])):
-                sent(place, slot).wait_send()
+            all_sent(place)
 
     swap.wait_send()
-    for step in range(1, chips):
-        pass_on(chip, twin, step).wait_send()
+    pass_on(ring.at[pl.ds(0, chips - 1)], twin).wait_send()
     pltpu.make_async_remote_copy(
         src_ref=result.at[core],
         dst_ref=result.at[1 - core],
@@ -663,7 +671,8 @@
     piece_width = pl.cdiv(classes, 256) * 128
     padded = pl.cdiv(depth, TILE_ROWS) * TILE_ROWS
     spots = pos_embed.shape[1] - 1
-    fold_rows = pl.cdiv(padded + spots, FOLD_PARTS * TILE_ROWS) * FOLD_PARTS * TILE_ROWS
+    tall = FOLD_PARTS * TILE_ROWS
+    fold_rows = pl.cdiv(padded + spots + TILE_ROWS, tall) * tall
     far = pl.BlockSpec(memory_space=pl.ANY)
     dma = pltpu.SemaphoreType.DMA
     f32, bf16 = jnp.float32, jnp.bfloat16
@@ -700,6 +709,7 @@
             pltpu.VMEM((fold_rows, width), bf16),
             pltpu.VMEM((padded + 2 * heads + TILE_ROWS, padded + spots), bf16),
             pltpu.VMEM((fold_rows, inner), bf16),
+            pltpu.VMEM((fold_rows - padded - spots, inner), f32),
             pltpu.VMEM((heads, 128), f32),
             pltpu.VMEM((2 * heads, 2 * images * rows), f32),
             pltpu.VMEM((pairs, padded + spots), f32),
@@ -710,12 +720,12 @@
             pltpu.VMEM((chips, images, piece_width), f32),
             pltpu.VMEM((2, images, piece_width), f32),
             dma((len(given),)),
-            dma((count, PIECES)),
-            dma((max(len(place) for place in SENDS),)),
+            dma((chips, PIECES)),
+            dma((chips,)),
+            dma((2, PIECES)),
             pltpu.SemaphoreType.REGULAR((LINE,)),
-            dma((2,)),
-            dma((2 + chips,)),
-            dma((chips,)),
+            dma((3,)),
+            dma((3,)),
         ],
         compiler_params=pltpu.CompilerParams(
             collective_id=0, has_side_effects=True, vmem_limit_bytes=60 << 20

time: 36.1 us -> 35.5 us (0.983)
  Pallas kernels: 34.5 us -> 33.9 us
    pallas_call x1, Pallas kernels: 34.5 us -> 33.9 us  [kernel_shards(): pl.pallas_call(functools.partial(whole_kernel, count, heads), out_shape=j...]
where the time goes in v4:
time: 35.5 us; the launch traced here: 35.3 us
  Pallas kernels  33.9 us (95%)
  local copies, waits for them, and re-layouts  1.38 us (4%)
    pallas_call x1, Pallas kernels, kernel_shards(): pl.pallas_call(functools.partial(whole_kernel, count, heads), out_shape=j...  33.9 us
    unnamed x1, local copies, waits for them, and re-layouts  1.38 us

profile of v4, /device:TPU:0, one launch (start us, length us, event | category | flops | bytes accessed | tf_op | source)
XLA Modules:
  0.0 35.3 jit_solution(5622732065901247230)
XLA Ops:
  0.0 33.9 %shard_map.136 = f32[8,1000]{1,0:T(8,128)} custom-call(bf16[8,16,588]{2,1,0:T(8,128)(2,1)} %patches.1, bf16[1,1280]{1,0:T(2,128)(2,1)} %cls_token.1, bf16[1,257,1280]{2,1,0:T(8,128)(2,1)} %pos_embed.1, f32[1,1280]{1,0:T(1,128)} %ln1_gain.1, f32[1,1280]{1,0:T(1,128)} %ln1_bias.1, bf16[1,588,1280]{2,1,0:T(8,128)(2,1)} %patch_weight.1, ...), custom_call_target="tpu_custom_call" | custom-call | tf_op jit(solution)/shard_map/pallas_call | solution.py:700
  33.9 1.4 %copy.16 = f32[8,1000]{1,0:T(8,128)} copy(f32[8,1000]{1,0:T(8,128)} %shard_map.136) | data formatting | bytes 64000

commit v5 on v4

--- a/solution.py
+++ b/solution.py
@@ -110,7 +110,7 @@
 TILE_ROWS = 16
 LOWEST = -1e30
 GRAM_PARTS = 2
-FOLD_PARTS = 6
+FOLD_PARTS = 3
 
 
 def split_in_two(values):
@@ -122,86 +122,86 @@
 PIECES = 4
 SENDS = (
     (
-        (0,0,0,1,0), (1,1,0,1,0), (1,1,0,1,2), (1,1,0,1,3), (0,0,0,1,3), (0,0,0,1,1), (1,1,0,1,1),
-        (0,0,0,1,2), (0,2,0,1,0), (0,2,0,1,1), (0,2,0,1,2), (0,2,0,1,3), (2,1,0,1,1), (1,1,0,0,0),
-        (0,2,0,0,0), (0,0,1,1,0), (0,2,1,1,0), (2,1,0,0,3), (3,1,0,0,3), (1,1,0,0,3), (0,2,0,0,3),
-        (0,0,1,1,2), (0,2,1,1,2), (1,1,0,0,1), (2,1,0,0,1), (0,2,0,0,1), (0,0,1,1,1), (0,2,1,1,1),
-        (2,1,0,0,2), (3,1,0,0,2), (0,2,0,0,2), (0,0,1,1,3), (0,2,1,1,3), (0,2,1,0,0), (0,2,1,0,2),
-        (0,0,2,1,1), (0,2,2,1,1), (0,2,1,0,1), (0,0,2,1,2), (0,2,2,1,2), (0,2,1,0,3), (0,0,2,1,3),
-        (0,2,2,1,3), (0,0,2,1,0), (0,2,2,1,0), (0,2,2,0,1), (0,2,3,1,3), (0,2,2,0,2), (0,2,3,0,1),
-        (0,0,3,1,0), (0,2,3,1,0), (0,2,2,0,3), (0,2,3,0,3), (0,2,2,0,0), (0,2,3,1,2), (0,2,3,0,2),
-        (0,2,3,1,1), (0,2,3,0,0),
+        (1,1,0,1,2), (1,1,0,1,1), (0,0,0,1,1), (0,0,0,1,3), (1,1,0,1,3), (1,1,0,1,0), (0,2,0,1,0),
+        (0,2,0,1,1), (0,2,0,1,2), (0,2,0,1,3), (2,1,0,1,1), (2,1,0,1,0), (0,2,0,0,1), (0,0,1,1,1),
+        (2,1,0,1,3), (0,2,1,1,1), (1,1,0,0,3), (3,1,0,0,3), (0,2,0,0,3), (0,0,0,1,0), (0,2,1,1,3),
+        (0,0,1,1,2), (0,2,1,1,2), (0,0,1,1,0), (0,2,1,1,0), (0,0,0,1,2), (0,2,1,0,3), (0,2,1,0,1),
+        (0,0,2,1,1), (0,2,2,1,1), (2,1,0,0,0), (3,1,0,0,0), (0,2,0,0,0), (0,0,2,1,0), (0,2,2,1,0),
+        (0,2,1,0,2), (0,0,2,1,2), (0,2,2,1,2), (0,2,1,0,0), (0,0,2,1,3), (0,2,2,1,3), (3,1,0,0,2),
+        (0,2,0,0,2), (0,2,2,0,1), (0,2,2,0,0), (0,2,3,1,0), (0,2,3,0,2), (0,2,2,0,2), (0,0,3,1,3),
+        (0,2,3,1,3), (0,2,2,0,3), (0,2,3,1,1), (0,2,3,0,0), (0,2,3,1,2), (0,2,3,0,1), (0,2,3,0,3),
     ),
     (
-        (0,1,1,1,0), (2,1,1,1,1), (1,0,1,1,1), (2,1,1,1,0), (0,1,1,1,2), (2,1,1,1,2), (1,0,1,1,0),
-        (0,1,1,1,1), (0,1,1,1,3), (1,0,1,1,3), (1,0,1,1,2), (2,1,1,1,3), (1,2,1,1,0), (1,2,1,1,1),
-        (1,2,1,1,2), (1,2,1,1,3), (2,1,0,1,0), (1,2,0,1,0), (1,2,1,0,1), (2,1,0,1,2), (1,0,0,1,2),
-        (1,2,0,1,2), (1,2,1,0,0), (1,0,2,1,1), (0,1,2,1,1), (1,2,2,1,1), (2,1,0,1,3), (1,2,0,1,3),
-        (1,2,1,0,3), (0,1,2,1,2), (1,0,2,1,2), (1,2,2,1,2), (1,2,0,1,1), (1,2,1,0,2), (0,1,2,1,3),
-        (1,0,2,1,3), (1,2,2,1,3), (0,1,2,1,0), (1,0,2,1,0), (1,2,2,1,0), (1,2,0,0,2), (1,2,0,0,0),
-        (0,1,3,1,3), (1,0,3,1,3), (1,2,3,1,3), (1,2,2,0,1), (1,2,2,0,2), (0,1,3,1,0), (1,0,3,1,0),
-        (1,2,3,1,0), (1,2,2,0,3), (1,2,2,0,0), (1,2,3,0,1), (1,2,0,0,3), (1,0,3,1,2), (0,1,3,1,2),
-        (1,2,3,1,2), (1,2,3,0,3), (1,2,0,0,1), (0,1,3,1,1), (1,2,3,1,1), (1,2,3,0,0), (1,2,3,0,2),
+        (0,1,1,1,1), (0,1,1,1,3), (1,0,1,1,3), (1,0,1,1,1), (2,1,1,1,0), (2,1,1,1,2), (2,1,1,1,1),
+        (2,1,1,1,3), (0,1,1,1,2), (1,0,1,1,0), (0,1,1,1,0), (1,2,1,1,0), (1,2,1,1,1), (1,2,1,1,2),
+        (1,2,1,1,3), (3,1,1,1,3), (1,0,1,1,2), (1,0,0,1,2), (2,1,0,1,2), (1,2,0,1,2), (0,1,1,0,3),
+        (1,2,1,0,3), (1,0,0,1,1), (1,2,0,1,1), (1,2,1,0,1), (1,0,2,1,1), (0,1,2,1,1), (1,2,2,1,1),
+        (1,2,0,1,3), (2,1,1,0,0), (1,2,1,0,0), (1,0,2,1,0), (0,1,2,1,0), (1,2,2,1,0), (1,0,0,1,0),
+        (1,2,0,1,0), (1,0,2,1,2), (0,1,2,1,2), (1,2,2,1,2), (1,0,2,1,3), (0,1,2,1,3), (1,2,2,1,3),
+        (1,2,1,0,2), (1,2,0,0,2), (1,2,0,0,3), (1,2,0,0,1), (0,1,3,1,0), (1,2,3,1,0), (1,2,2,0,1),
+        (0,1,3,1,3), (1,0,3,1,3), (1,2,3,1,3), (1,2,2,0,0), (1,0,3,1,1), (0,1,3,1,1), (1,2,3,1,1),
+        (1,2,0,0,0), (0,1,3,1,2), (1,2,3,1,2), (1,2,2,0,2), (1,2,2,0,3), (1,2,3,0,3), (1,2,3,0,2),
+        (1,2,3,0,1), (1,2,3,0,0),
     ),
     (
-        (1,1,2,1,1), (2,0,2,1,1), (3,1,2,1,0), (1,1,2,1,2), (2,0,2,1,3), (1,1,2,1,3), (1,1,2,1,0),
-        (3,1,2,1,2), (3,1,2,1,1), (2,0,2,1,2), (3,1,2,1,3), (2,2,2,1,0), (2,2,2,1,1), (2,2,2,1,2),
-        (2,2,2,1,3), (3,1,1,1,1), (2,0,1,1,1), (2,2,1,1,1), (3,1,1,1,0), (2,0,1,1,0), (2,2,1,1,0),
-        (2,2,2,0,1), (3,1,1,1,2), (2,0,1,1,2), (2,2,1,1,2), (1,1,3,1,0), (2,0,3,1,0), (2,2,3,1,0),
-        (2,2,2,0,3), (1,1,3,1,2), (2,0,3,1,2), (2,2,3,1,2), (2,2,2,0,2), (3,1,1,1,3), (2,0,1,1,3),
-        (2,2,1,1,3), (1,1,3,1,1), (2,2,3,1,1), (2,2,1,0,1), (3,1,0,1,1), (2,0,2,1,0), (2,2,0,1,1),
-        (2,0,0,1,0), (3,1,0,1,0), (2,2,0,1,0), (2,2,3,1,3), (2,2,1,0,0), (3,1,0,1,2), (2,2,0,1,2),
-        (2,2,1,0,2), (2,2,3,0,1), (2,2,0,0,3), (2,2,3,0,0), (3,1,0,1,3), (2,2,0,1,3), (2,2,3,0,2),
-        (2,2,1,0,3), (2,2,2,0,0), (2,2,0,0,0), (2,2,3,0,3), (2,2,0,0,1), (2,2,0,0,2),
+        (1,1,2,1,1), (3,1,2,1,3), (1,1,2,1,0), (3,1,2,1,1), (1,1,2,1,2), (3,1,2,1,2), (2,0,2,1,3),
+        (2,0,2,1,0), (3,1,2,1,0), (2,0,2,1,1), (1,1,2,1,3), (2,2,2,1,0), (2,2,2,1,1), (2,2,2,1,2),
+        (2,2,2,1,3), (3,1,1,1,0), (2,2,1,1,0), (3,1,1,1,2), (2,0,1,1,2), (2,2,1,1,2), (2,2,2,0,3),
+        (2,0,1,1,1), (3,1,1,1,1), (2,2,1,1,1), (2,0,3,1,1), (2,2,3,1,1), (2,2,2,0,0), (2,2,3,1,3),
+        (2,2,2,0,1), (2,0,0,1,1), (3,1,0,1,1), (2,2,0,1,1), (2,0,3,1,0), (2,2,3,1,0), (3,1,0,1,0),
+        (2,2,0,1,0), (2,0,2,1,2), (1,1,3,1,2), (2,2,3,1,2), (2,2,1,0,2), (2,0,1,1,3), (2,2,1,1,3),
+        (3,1,0,1,3), (2,0,0,1,3), (2,2,0,1,3), (2,2,1,0,1), (2,2,3,0,1), (3,1,0,1,2), (2,0,0,1,2),
+        (2,2,0,1,2), (2,2,3,0,3), (2,2,0,0,1), (2,2,1,0,0), (2,2,3,0,2), (2,2,3,0,0), (2,2,2,0,2),
+        (2,2,0,0,0), (2,2,1,0,3), (2,2,0,0,3), (2,2,0,0,2),
     ),
     (
-        (2,1,3,1,0), (3,0,3,1,1), (2,1,3,1,2), (3,0,3,1,3), (2,1,3,1,1), (2,1,3,1,3), (3,0,3,1,2),
-        (3,2,3,1,0), (3,2,3,1,1), (3,2,3,1,2), (3,2,3,1,3), (1,1,3,1,3), (3,0,2,1,0), (3,2,2,1,0),
-        (3,0,3,1,0), (2,1,3,0,1), (1,1,3,0,1), (0,1,3,0,1), (3,2,3,0,1), (3,0,2,1,2), (3,2,2,1,2),
-        (2,1,3,0,3), (0,1,3,0,3), (3,2,3,0,3), (3,0,2,1,1), (3,2,2,1,1), (0,1,3,0,2), (3,2,3,0,2),
-        (3,0,2,1,3), (3,2,2,1,3), (3,0,1,1,1), (3,2,1,1,1), (3,2,2,0,0), (3,0,1,1,0), (3,2,1,1,0),
-        (3,0,1,1,2), (3,2,1,1,2), (3,2,3,0,0), (3,2,2,0,2), (3,2,2,0,1), (3,0,1,1,3), (3,2,1,1,3),
-        (3,2,2,0,3), (3,0,0,1,1), (3,2,0,1,1), (3,2,0,0,3), (3,2,1,0,1), (3,0,0,1,0), (3,2,0,1,0),
-        (3,2,1,0,0), (3,2,0,1,2), (3,2,1,0,2), (3,2,0,1,3), (3,2,1,0,3), (3,2,0,0,1), (3,2,0,0,2),
-        (3,2,0,0,0),
+        (2,1,3,1,1), (3,0,3,1,3), (2,1,3,1,3), (2,1,3,1,0), (2,1,3,1,2), (3,0,3,1,2), (3,2,3,1,0),
+        (3,2,3,1,1), (3,2,3,1,2), (3,2,3,1,3), (1,1,3,1,0), (1,1,3,1,3), (1,1,3,1,1), (3,0,2,1,3),
+        (3,0,3,1,0), (3,2,2,1,3), (2,1,3,0,3), (3,2,3,0,3), (3,0,2,1,1), (3,2,2,1,1), (2,1,3,0,2),
+        (0,1,3,0,2), (1,1,3,0,2), (3,2,3,0,2), (3,0,2,1,2), (3,2,2,1,2), (3,0,2,1,0), (3,2,2,1,0),
+        (3,0,1,1,0), (3,2,1,1,0), (3,2,2,0,3), (1,1,3,0,0), (0,1,3,0,0), (3,2,3,0,0), (3,0,3,1,1),
+        (3,2,2,0,1), (3,0,1,1,2), (3,2,1,1,2), (3,2,2,0,2), (3,0,1,1,3), (3,2,1,1,3), (3,2,0,0,3),
+        (3,0,1,1,1), (3,2,1,1,1), (3,2,2,0,0), (3,0,0,1,1), (3,2,0,1,1), (3,2,1,0,0), (3,2,0,1,0),
+        (0,1,3,0,1), (3,2,3,0,1), (3,2,1,0,2), (3,2,0,1,3), (3,2,0,0,0), (3,2,1,0,3), (3,2,0,1,2),
+        (3,2,1,0,1), (3,2,0,0,1), (3,2,0,0,2),
     ),
 )
 EVENTS = (
     (
-        ((-1,0,0,0,12),), (), (), ((-2,2,0,12,1),), (), (), ((0,0,0,13,2),(-2,3,0,15,0),(1,1,0,15,2)),
-        ((0,0,3,17,4),(1,1,2,21,2),(0,0,1,23,3)), ((1,1,1,26,2),(0,0,2,28,3),(1,1,3,31,2)), (),
-        ((1,0,0,33,1),), (), ((1,0,2,34,1),(2,1,1,35,2)), ((1,0,1,37,1),(2,1,2,38,2),(1,0,3,40,1)),
-        ((2,1,3,41,2),(2,1,0,43,2)), (), ((2,0,1,45,1),(3,1,3,46,1),(2,0,2,47,1),(3,0,1,48,1)),
-        ((3,1,0,49,2),(2,0,3,51,1),(3,0,3,52,1),(2,0,0,53,1)), ((3,1,2,54,1),(3,0,2,55,1),(3,1,1,56,1)),
-        ((3,0,0,57,1),), (), (),
+        ((-1,0,0,0,10),), (), (), ((-2,2,0,10,2),), (), (), ((-2,3,0,12,0),(0,0,1,12,1)),
+        ((1,1,1,13,3),(0,0,3,16,3)), ((1,1,3,19,2),(1,1,2,21,2)), ((1,1,0,23,2),),
+        ((1,0,3,25,2),(1,0,1,27,1)),
+        ((2,1,1,28,2),(0,0,0,30,3),(2,1,0,33,2),(1,0,2,35,1),(2,1,2,36,2),(1,0,0,38,1)),
+        ((2,1,3,39,2),(0,0,2,41,2)), ((2,0,1,43,1),), ((2,0,0,44,1),(3,1,0,45,1),(3,0,2,46,1),(2,0,2,47,1)),
+        (), ((3,1,3,48,2),), ((2,0,3,50,1),), ((3,1,1,51,1),(3,0,0,52,1),(3,1,2,53,1)), (),
+        ((3,0,1,54,1),(3,0,3,55,1)), (),
     ),
     (
-        ((-1,0,0,0,16),), (), (), (), ((-2,3,0,16,0),), ((0,1,0,16,2),), ((1,0,1,18,1),(0,1,2,19,3)),
-        ((1,0,0,22,1),(2,1,1,23,3),(0,1,3,26,2),(1,0,3,28,1),(2,1,2,29,3),(0,1,1,32,1)),
-        ((1,0,2,33,1),(2,1,3,34,3)), ((2,1,0,37,3),), ((0,0,2,40,1),), ((0,0,0,41,1),),
-        ((3,1,3,42,3),(2,0,1,45,1)), (), ((2,0,2,46,1),(3,1,0,47,3)), ((2,0,3,50,1),(2,0,0,51,1)),
-        ((3,0,1,52,1),(0,0,3,53,1),(3,1,2,54,3),(3,0,3,57,1),(0,0,1,58,1)), ((3,1,1,59,2),), ((3,0,0,61,1),),
-        (), (), ((3,0,2,62,1),),
+        ((-1,0,0,0,15),), (), (), (), ((-2,3,0,15,1),), (), ((0,1,2,16,4),(1,0,3,20,2)),
+        ((0,1,1,22,2),(1,0,1,24,1),(2,1,1,25,3),(0,1,3,28,1)), ((1,0,0,29,2),(2,1,0,31,3),(0,1,0,34,2)),
+        ((2,1,2,36,3),), ((2,1,3,39,3),(1,0,2,42,1)), ((0,0,2,43,1),(0,0,3,44,1)),
+        ((0,0,1,45,1),(3,1,0,46,2),(2,0,1,48,1),(3,1,3,49,3)), ((2,0,0,52,1),(3,1,1,53,3)),
+        ((0,0,0,56,1),(3,1,2,57,2)), ((2,0,2,59,1),), ((2,0,3,60,1),(3,0,3,61,1),(3,0,2,62,1)), (),
+        ((3,0,1,63,1),(3,0,0,64,1)), (), (), (),
     ),
     (
-        ((-1,0,0,0,15),), ((-2,0,0,15,0),), (), (), (), ((1,1,1,15,3),),
-        ((1,1,0,18,3),(2,0,1,21,1),(1,1,2,22,3)),
-        ((3,1,0,25,3),(2,0,3,28,1),(3,1,2,29,3),(2,0,2,32,1),(1,1,3,33,3)),
-        ((3,1,1,36,2),(1,0,1,38,1),(0,1,1,39,3),(0,1,0,42,3),(3,1,3,45,1)), (), ((1,0,0,46,1),(0,1,2,47,2)),
-        ((1,0,2,49,1),(3,0,1,50,1)), ((0,0,3,51,1),(3,0,0,52,1)), ((0,1,3,53,2),(3,0,2,55,1)),
-        ((1,0,3,56,1),(2,0,0,57,1)), (), ((0,0,0,58,1),(3,0,3,59,1),(0,0,1,60,1)), ((0,0,2,61,1),), (), (),
-        (), (),
+        ((-1,0,0,0,15),), ((-2,0,0,15,0),), (), (), (), ((1,1,0,15,2),), ((1,1,2,17,3),(2,0,3,20,1)),
+        ((1,1,1,21,3),(3,1,1,24,2),(2,0,0,26,1)), ((3,1,3,27,1),(2,0,1,28,1),(0,1,1,29,3)),
+        ((3,1,0,32,2),(0,1,0,34,2),(3,1,2,36,3)), ((1,0,2,39,1),(1,1,3,40,2),(0,1,3,42,3),(1,0,1,45,1)),
+        ((3,0,1,46,1),(0,1,2,47,3)), ((3,0,3,50,1),(0,0,1,51,1),(1,0,0,52,1),(3,0,2,53,1),(3,0,0,54,1)),
+        ((2,0,2,55,1),), ((0,0,0,56,1),(1,0,3,57,1)), (), ((0,0,3,58,1),(0,0,2,59,1)), (), (), (), (), (),
     ),
     (
-        ((-1,0,0,0,11),), ((-2,1,0,11,1),(-2,0,0,12,0)), (), (), (), ((2,1,0,12,2),),
-        ((3,0,1,14,5),(2,1,2,19,2)), ((3,0,3,21,3),(2,1,1,24,2),(3,0,2,26,2),(2,1,3,28,2)),
-        ((1,1,1,30,2),(2,0,0,32,1)), ((1,1,0,33,2),), ((1,1,2,35,2),(3,0,0,37,1)), (),
-        ((2,0,2,38,1),(2,0,1,39,1),(1,1,3,40,2)), ((2,0,3,42,1),(0,1,1,43,2)),
-        ((0,0,3,45,1),(1,0,1,46,1),(0,1,0,47,2)), ((1,0,0,49,1),(0,1,2,50,1)), ((1,0,2,51,1),(0,1,3,52,1)),
-        ((1,0,3,53,1),), ((0,0,1,54,1),(0,0,2,55,1)), ((0,0,0,56,1),), (), (),
+        ((-1,0,0,0,10),), ((-2,1,0,10,3),(-2,0,0,13,0)), (), (), (), ((2,1,3,13,3),),
+        ((3,0,3,16,2),(2,1,1,18,2)), ((3,0,2,20,4),(2,1,2,24,2)), ((2,1,0,26,2),),
+        ((1,1,0,28,2),(2,0,3,30,1)), ((3,0,0,31,3),(2,0,1,34,2)),
+        ((1,1,2,36,2),(2,0,2,38,1),(1,1,3,39,2),(0,0,3,41,1),(1,1,1,42,2)),
+        ((2,0,0,44,1),(0,1,1,45,2),(1,0,0,47,1),(0,1,0,48,1)), ((3,0,1,49,2),),
+        ((1,0,2,51,1),(0,1,3,52,1),(0,0,0,53,1),(1,0,3,54,1)), ((0,1,2,55,1),), ((1,0,1,56,1),), (),
+        ((0,0,1,57,1),(0,0,2,58,1)), (), (), (),
     ),
 )
-ORDER = (14570689, 14437003, 1713117, 575407)
+ORDER = (14551705, 13862219, 680701, 583919)
 
 
 def contract_last(left, right):
@@ -281,7 +281,8 @@
     inner = query_w.shape[1]
     head_dim = inner // heads
     pairs = heads * images
-    spots = position.shape[0] - 1
+    spots = basis.shape[0] - 2 * heads - padded
+    held_rows = position.shape[0]
 
     loads = []
     for index, (source, target) in enumerate(
@@ -302,9 +303,9 @@
             (head_bias, class_bias),
         )
     ):
-        load = pltpu.make_async_copy(source, target, load_sem.at[index])
+        loads.append(pltpu.make_async_copy(source, target, load_sem.at[index]))
+    for load in loads[:5]:
         load.start()
-        loads.append(load)
 
     twin = me + 1 - 2 * core
     beside = plane * PLANE + (1 - side) * 2 + core
@@ -331,6 +332,8 @@
         greet(me + PLANE)
 
     loads[0].wait()
+    for load in loads[5:7]:
+        load.start()
     eye = (
         lax.broadcasted_iota(jnp.int32, (padded, depth), 0)
         == lax.broadcasted_iota(jnp.int32, (padded, depth), 1)
@@ -413,6 +416,8 @@
                             sent(place, slot).start()
 
     events(0)
+    for load in loads[7:]:
+        load.start()
 
     for index in (1, 2, 3, 4):
         loads[index].wait()
@@ -424,16 +429,19 @@
     lead_row = lead[:1].astype(f32)
 
     events(2)
-    placed = position[...].astype(f32)[1:]
+    placed = position[...].astype(f32)
     placed = placed - jnp.mean(placed, axis=1, keepdims=True)
+    blank = jnp.zeros((spots - held_rows, width), f32)
     top = 2 * heads
+    placed = jnp.concatenate([placed, blank], axis=0)
     basis[top + padded :, :] = placed.astype(bf16)
-    scaled[padded : padded + spots, :] = (placed * gain).astype(bf16)
-    scaled[padded + spots :, :] = jnp.concatenate(
-        [split_in_two(bias), lead[:1], jnp.zeros((ends.shape[0] - 3, width), bf16)], axis=0
-    )
-    weight = jnp.sum(placed * placed, axis=1, keepdims=True)
-    weight = jnp.transpose(jnp.broadcast_to(weight, (spots, 128)))[:1]
+    bias_high = bias.astype(bf16).astype(f32)
+    ending = jnp.concatenate([blank[3:], bias_high, bias - bias_high, lead_row], axis=0)
+    ending = jnp.concatenate([jnp.zeros((held_rows, width), f32), ending], axis=0)
+    scaled[padded:, :] = (placed * gain + ending).astype(bf16)
+    weight = jnp.broadcast_to(jnp.sum(placed * placed, axis=1, keepdims=True), (spots, 128))
+    weight = jnp.concatenate([weight, jnp.zeros((-spots % 128, 128), f32)], axis=0)
+    weight = jnp.transpose(weight)[:1, :spots]
 
     loads[5].wait()
     table = embed[...].astype(f32)
@@ -487,7 +495,7 @@
     same = (lane % lanes) // rows == row_image
     spot_row = lax.broadcasted_iota(jnp.int32, (spots, cells), 0)
     spot_lane = lax.broadcasted_iota(jnp.int32, (spots, cells), 1)
-    spot_at = spot_row - (spot_lane // lanes) * rows - spot_lane % rows
+    spot_at = spot_row - 1 - (spot_lane // lanes) * rows - spot_lane % rows
 
     order = sum(mine * packed for mine, packed in zip(here, ORDER, strict=True))
     first_step = 5 + GRAM_PARTS
@@ -528,6 +536,14 @@
         total[...] = total[...] * shrink + jnp.sum(chance, axis=1, keepdims=True)
         gathered[...] = gathered[...] * shrink + contract_last((chance * rate).astype(bf16), block)
 
+    def fold(part_of):
+        low = pl.multiple_of(part_of * fold_rows, TILE_ROWS)
+        product = jnp.dot(
+            scaled[pl.ds(low, fold_rows), :], value_w[...], preferred_element_type=f32
+        )
+        folded[pl.ds(low, fold_rows), :] = product.astype(bf16)
+        ends[...] = product[fold_rows - ends.shape[0] :]
+
     def chip_step(turn, carry):
         for index in range(1, 2 * LINE):
             pl.when(turn == index)(functools.partial(events, first_step + 2 * index))
@@ -538,17 +554,12 @@
         back(base_of(turn - 1), scores, rate)
         front(base)
 
-        for index in range(1, FOLD_PARTS + 1):
+        for index in range(1, 2 * LINE - 1):
             pl.when(turn == index)(functools.partial(events, first_step + 2 * index + 1))
 
-        @pl.when(turn <= FOLD_PARTS)
+        @pl.when(turn < FOLD_PARTS)
         def _():
-            low = pl.multiple_of((turn - 1) * fold_rows, TILE_ROWS)
-            product = jnp.dot(
-                scaled[pl.ds(low, fold_rows), :], value_w[...], preferred_element_type=f32
-            )
-            folded[pl.ds(low, fold_rows), :] = product.astype(bf16)
-            ends[...] = product[fold_rows - ends.shape[0] :]
+            fold(turn)
 
         return carry
 
@@ -556,13 +567,15 @@
     got_from_twin(base_of(0))
     front(base_of(0))
     events(first_step + 1)
+    fold(0)
     lax.fori_loop(1, 2 * LINE, chip_step, 0)
     back(base_of(2 * LINE - 1), kept[:heads, :], kept[heads : heads + 1, :])
 
-    plain = ends[0:1, :] + ends[1:2, :]
-    lead_value = ends[2:3, :]
+    last = ends.shape[0]
+    plain = ends[last - 3 : last - 2, :] + ends[last - 2 : last - 1, :]
+    lead_value = ends[last - 1 :, :]
     values = jnp.dot(
-        split_in_two(gathered[...]), folded[: padded + spots, :], preferred_element_type=f32
+        split_in_two(gathered[...]), folded[...], preferred_element_type=f32
     )
     share = 1.0 / total[:, :1]
     lead_chance = jnp.exp(first - peak[:, :1]) * share
@@ -577,8 +590,23 @@
     hidden = leading + jnp.dot(mixed, out_w[...], preferred_element_type=f32)
     for index in (10, 11, 12, 13):
         loads[index].wait()
-    final = layer_norm(hidden, last_gain[...], last_bias[...]).astype(bf16)
-    logits = contract_last(final, class_w[...]) + class_bias[...]
+    center = hidden - jnp.mean(hidden, axis=-1, keepdims=True)
+    shift = last_bias[...]
+    shift_high = shift.astype(bf16)
+    shift_low = (shift - shift_high.astype(f32)).astype(bf16)
+    rows_in = jnp.concatenate(
+        [
+            center * last_gain[...],
+            shift_high.astype(f32),
+            shift_low.astype(f32),
+            jnp.zeros((TILE_ROWS - images - 2, width), f32),
+        ],
+        axis=0,
+    ).astype(bf16)
+    spread_out = jnp.mean(center * center, axis=-1, keepdims=True)
+    products = contract_last(rows_in, class_w[...])
+    moved = products[images : images + 1] + products[images + 1 : images + 2] + class_bias[...]
+    logits = products[:images] * lax.rsqrt(spread_out + epsilon) + moved
     lifted = logits - jnp.max(logits, axis=-1, keepdims=True)
     logp = lifted - jnp.log(jnp.sum(jnp.exp(lifted), axis=-1, keepdims=True))
 
@@ -670,9 +698,8 @@
     classes = head_w.shape[2]
     piece_width = pl.cdiv(classes, 256) * 128
     padded = pl.cdiv(depth, TILE_ROWS) * TILE_ROWS
-    spots = pos_embed.shape[1] - 1
     tall = FOLD_PARTS * TILE_ROWS
-    fold_rows = pl.cdiv(padded + spots + TILE_ROWS, tall) * tall
+    features = pl.cdiv(padded + pos_embed.shape[1] + 3, tall) * tall
     far = pl.BlockSpec(memory_space=pl.ANY)
     dma = pltpu.SemaphoreType.DMA
     f32, bf16 = jnp.float32, jnp.bfloat16
@@ -705,14 +732,14 @@
         scratch_shapes=[
             *held,
             pltpu.VMEM((count, padded, images * rows), bf16),
-            pltpu.VMEM((2 * heads + padded + spots, width), bf16),
-            pltpu.VMEM((fold_rows, width), bf16),
-            pltpu.VMEM((padded + 2 * heads + TILE_ROWS, padded + spots), bf16),
-            pltpu.VMEM((fold_rows, inner), bf16),
-            pltpu.VMEM((fold_rows - padded - spots, inner), f32),
+            pltpu.VMEM((2 * heads + features, width), bf16),
+            pltpu.VMEM((features, width), bf16),
+            pltpu.VMEM((padded + 2 * heads + TILE_ROWS, features), bf16),
+            pltpu.VMEM((features, inner), bf16),
+            pltpu.VMEM((TILE_ROWS, inner), f32),
             pltpu.VMEM((heads, 128), f32),
             pltpu.VMEM((2 * heads, 2 * images * rows), f32),
-            pltpu.VMEM((pairs, padded + spots), f32),
+            pltpu.VMEM((pairs, features), f32),
             pltpu.VMEM((pairs, 128), f32),
             pltpu.VMEM((pairs, 128), f32),
             pltpu.VMEM((2, images, piece_width), f32),

time: 35.5 us -> 34 us (0.958)
  Pallas kernels: 33.9 us -> 32.4 us
    pallas_call x1, Pallas kernels: 33.9 us -> 32.4 us  [kernel_shards(): pl.pallas_call(functools.partial(whole_kernel, count, heads), out_shape=j...]
where the time goes in v5:
time: 34 us; the launch traced here: 33.8 us
  Pallas kernels  32.4 us (95%)
  local copies, waits for them, and re-layouts  1.38 us (4%)
    pallas_call x1, Pallas kernels, kernel_shards(): pl.pallas_call(functools.partial(whole_kernel, count, heads), out_shape=j...  32.4 us
    unnamed x1, local copies, waits for them, and re-layouts  1.38 us

profile of v5, /device:TPU:0, one launch (start us, length us, event | category | flops | bytes accessed | tf_op | source)
XLA Modules:
  0.0 33.8 jit_solution(10101185688942218032)
XLA Ops:
  0.0 32.4 %shard_map.136 = f32[8,1000]{1,0:T(8,128)} custom-call(bf16[8,16,588]{2,1,0:T(8,128)(2,1)} %patches.1, bf16[1,1280]{1,0:T(2,128)(2,1)} %cls_token.1, bf16[1,257,1280]{2,1,0:T(8,128)(2,1)} %pos_embed.1, f32[1,1280]{1,0:T(1,128)} %ln1_gain.1, f32[1,1280]{1,0:T(1,128)} %ln1_bias.1, bf16[1,588,1280]{2,1,0:T(8,128)(2,1)} %patch_weight.1, ...), custom_call_target="tpu_custom_call" | custom-call | tf_op jit(solution)/shard_map/pallas_call | solution.py:727
  32.5 1.4 %copy.16 = f32[8,1000]{1,0:T(8,128)} copy(f32[8,1000]{1,0:T(8,128)} %shard_map.136) | data formatting | bytes 64000

commit v6 on v5

--- a/solution.py
+++ b/solution.py
@@ -726,7 +726,7 @@
     ]
     return pl.pallas_call(
         functools.partial(whole_kernel, count, heads),
-        out_shape=jax.ShapeDtypeStruct((images, classes), f32),
+        out_shape=pltpu.VMEM((images, classes), f32),
         in_specs=[far] * len(given),
         out_specs=pl.BlockSpec(memory_space=pltpu.VMEM),
         scratch_shapes=[

time: 34 us -> 32.6 us (0.959)
  local copies, waits for them, and re-layouts: 1.38 us -> 0.62 us
  Pallas kernels: 32.4 us -> 31.8 us
    unnamed x1, local copies, waits for them, and re-layouts: 1.38 us -> 0.62 us
    pallas_call x1, Pallas kernels: 32.4 us -> 31.8 us  [kernel_shards(): pl.pallas_call(functools.partial(whole_kernel, count, heads), out_shape=p...]
where the time goes in v6:
time: 32.6 us; the launch traced here: 32.5 us
  Pallas kernels  31.8 us (98%)
  local copies, waits for them, and re-layouts  0.62 us (2%)
    pallas_call x1, Pallas kernels, kernel_shards(): pl.pallas_call(functools.partial(whole_kernel, count, heads), out_shape=p...  31.8 us

profile of v6, /device:TPU:0, one launch (start us, length us, event | category | flops | bytes accessed | tf_op | source)
XLA Modules:
  0.0 32.5 jit_solution(16455489525793148517)
XLA Ops:
  0.0 31.8 %shard_map.136 = f32[8,1000]{1,0:T(8,128)S(1)} custom-call(bf16[8,16,588]{2,1,0:T(8,128)(2,1)} %patches.1, bf16[1,1280]{1,0:T(2,128)(2,1)} %cls_token.1, bf16[1,257,1280]{2,1,0:T(8,128)(2,1)} %pos_embed.1, f32[1,1280]{1,0:T(1,128)} %ln1_gain.1, f32[1,1280]{1,0:T(1,128)} %ln1_bias.1, bf16[1,588,1280]{2,1,0:T(8,128)(2,1)} %patch_weight.1, ...), custom_call_target="tpu_custom_call" | custom-call | tf_op jit(solution)/shard_map/pallas_call | solution.py:727
  31.9 0.6 %copy.16 = f32[8,1000]{1,0:T(8,128)} copy(f32[8,1000]{1,0:T(8,128)S(1)} %shard_map.136) | data formatting | bytes 64000

commit v7 on v6

--- a/solution.py
+++ b/solution.py
@@ -122,86 +122,85 @@
 PIECES = 4
 SENDS = (
     (
-        (1,1,0,1,2), (1,1,0,1,1), (0,0,0,1,1), (0,0,0,1,3), (1,1,0,1,3), (1,1,0,1,0), (0,2,0,1,0),
-        (0,2,0,1,1), (0,2,0,1,2), (0,2,0,1,3), (2,1,0,1,1), (2,1,0,1,0), (0,2,0,0,1), (0,0,1,1,1),
-        (2,1,0,1,3), (0,2,1,1,1), (1,1,0,0,3), (3,1,0,0,3), (0,2,0,0,3), (0,0,0,1,0), (0,2,1,1,3),
-        (0,0,1,1,2), (0,2,1,1,2), (0,0,1,1,0), (0,2,1,1,0), (0,0,0,1,2), (0,2,1,0,3), (0,2,1,0,1),
-        (0,0,2,1,1), (0,2,2,1,1), (2,1,0,0,0), (3,1,0,0,0), (0,2,0,0,0), (0,0,2,1,0), (0,2,2,1,0),
-        (0,2,1,0,2), (0,0,2,1,2), (0,2,2,1,2), (0,2,1,0,0), (0,0,2,1,3), (0,2,2,1,3), (3,1,0,0,2),
-        (0,2,0,0,2), (0,2,2,0,1), (0,2,2,0,0), (0,2,3,1,0), (0,2,3,0,2), (0,2,2,0,2), (0,0,3,1,3),
-        (0,2,3,1,3), (0,2,2,0,3), (0,2,3,1,1), (0,2,3,0,0), (0,2,3,1,2), (0,2,3,0,1), (0,2,3,0,3),
+        (0,0,0,1,3), (1,1,0,1,1), (1,1,0,1,0), (1,1,0,1,2), (1,1,0,1,3), (0,0,0,1,0), (0,2,0,1,0),
+        (0,2,0,1,1), (0,2,0,1,2), (0,2,0,1,3), (3,1,0,1,0), (1,1,0,0,3), (0,0,0,1,1), (2,1,0,0,3),
+        (0,2,0,0,3), (0,0,1,1,2), (0,2,1,1,2), (3,1,0,1,3), (1,1,0,0,0), (0,2,0,0,0), (0,2,1,1,0),
+        (0,0,0,1,2), (0,2,1,1,3), (0,0,1,1,1), (0,2,1,1,1), (3,1,0,0,1), (0,2,0,0,1), (0,2,1,0,2),
+        (2,1,0,1,0), (0,2,1,0,3), (2,1,0,0,2), (3,1,0,0,2), (0,2,0,0,2), (0,0,2,1,0), (0,2,2,1,0),
+        (0,2,1,0,1), (0,0,2,1,2), (0,2,2,1,2), (0,2,3,0,3), (0,0,2,1,3), (0,2,2,1,3), (0,0,2,1,1),
+        (0,2,2,1,1), (0,2,3,0,0), (0,2,1,0,0), (0,2,2,0,0), (0,2,3,0,1), (0,2,2,0,2), (0,2,3,1,3),
+        (0,2,3,0,2), (0,2,2,0,3), (0,2,3,1,1), (0,2,2,0,1), (0,2,3,1,0), (0,2,3,1,2),
     ),
     (
-        (0,1,1,1,1), (0,1,1,1,3), (1,0,1,1,3), (1,0,1,1,1), (2,1,1,1,0), (2,1,1,1,2), (2,1,1,1,1),
-        (2,1,1,1,3), (0,1,1,1,2), (1,0,1,1,0), (0,1,1,1,0), (1,2,1,1,0), (1,2,1,1,1), (1,2,1,1,2),
-        (1,2,1,1,3), (3,1,1,1,3), (1,0,1,1,2), (1,0,0,1,2), (2,1,0,1,2), (1,2,0,1,2), (0,1,1,0,3),
-        (1,2,1,0,3), (1,0,0,1,1), (1,2,0,1,1), (1,2,1,0,1), (1,0,2,1,1), (0,1,2,1,1), (1,2,2,1,1),
-        (1,2,0,1,3), (2,1,1,0,0), (1,2,1,0,0), (1,0,2,1,0), (0,1,2,1,0), (1,2,2,1,0), (1,0,0,1,0),
-        (1,2,0,1,0), (1,0,2,1,2), (0,1,2,1,2), (1,2,2,1,2), (1,0,2,1,3), (0,1,2,1,3), (1,2,2,1,3),
-        (1,2,1,0,2), (1,2,0,0,2), (1,2,0,0,3), (1,2,0,0,1), (0,1,3,1,0), (1,2,3,1,0), (1,2,2,0,1),
-        (0,1,3,1,3), (1,0,3,1,3), (1,2,3,1,3), (1,2,2,0,0), (1,0,3,1,1), (0,1,3,1,1), (1,2,3,1,1),
-        (1,2,0,0,0), (0,1,3,1,2), (1,2,3,1,2), (1,2,2,0,2), (1,2,2,0,3), (1,2,3,0,3), (1,2,3,0,2),
-        (1,2,3,0,1), (1,2,3,0,0),
+        (2,1,1,1,0), (2,1,1,1,3), (2,1,1,1,1), (0,1,1,1,2), (1,0,1,1,3), (2,1,1,1,2), (0,1,1,1,0),
+        (0,1,1,1,3), (0,1,1,1,1), (1,0,1,1,2), (1,2,1,1,0), (1,2,1,1,1), (1,2,1,1,2), (1,2,1,1,3),
+        (1,0,1,1,0), (2,1,0,1,1), (1,0,0,1,1), (1,2,0,1,1), (0,1,1,0,3), (1,2,1,0,3), (1,2,0,1,0),
+        (1,2,1,0,2), (1,0,2,1,0), (0,1,2,1,0), (1,2,2,1,0), (1,0,0,1,2), (2,1,0,1,2), (1,2,0,1,2),
+        (1,0,1,1,1), (1,0,2,1,3), (0,1,2,1,3), (1,2,2,1,3), (2,1,0,1,3), (1,2,0,1,3), (0,1,2,1,1),
+        (1,0,2,1,1), (1,2,2,1,1), (1,0,2,1,2), (1,2,2,1,2), (0,1,1,0,0), (1,2,1,0,0), (1,2,0,0,3),
+        (1,2,0,0,1), (1,2,2,0,0), (0,1,3,1,3), (1,0,3,1,3), (1,2,3,1,3), (1,2,0,0,2), (1,2,0,0,0),
+        (1,0,3,1,1), (0,1,3,1,1), (1,2,3,1,1), (1,2,1,0,1), (1,2,2,0,3), (0,1,3,1,0), (1,0,3,1,0),
+        (1,2,3,1,0), (1,2,2,0,1), (0,1,3,1,2), (1,2,3,1,2), (1,2,2,0,2), (1,2,3,0,3), (1,2,3,0,1),
+        (1,2,3,0,2), (1,2,3,0,0),
     ),
     (
-        (1,1,2,1,1), (3,1,2,1,3), (1,1,2,1,0), (3,1,2,1,1), (1,1,2,1,2), (3,1,2,1,2), (2,0,2,1,3),
-        (2,0,2,1,0), (3,1,2,1,0), (2,0,2,1,1), (1,1,2,1,3), (2,2,2,1,0), (2,2,2,1,1), (2,2,2,1,2),
-        (2,2,2,1,3), (3,1,1,1,0), (2,2,1,1,0), (3,1,1,1,2), (2,0,1,1,2), (2,2,1,1,2), (2,2,2,0,3),
-        (2,0,1,1,1), (3,1,1,1,1), (2,2,1,1,1), (2,0,3,1,1), (2,2,3,1,1), (2,2,2,0,0), (2,2,3,1,3),
-        (2,2,2,0,1), (2,0,0,1,1), (3,1,0,1,1), (2,2,0,1,1), (2,0,3,1,0), (2,2,3,1,0), (3,1,0,1,0),
-        (2,2,0,1,0), (2,0,2,1,2), (1,1,3,1,2), (2,2,3,1,2), (2,2,1,0,2), (2,0,1,1,3), (2,2,1,1,3),
-        (3,1,0,1,3), (2,0,0,1,3), (2,2,0,1,3), (2,2,1,0,1), (2,2,3,0,1), (3,1,0,1,2), (2,0,0,1,2),
-        (2,2,0,1,2), (2,2,3,0,3), (2,2,0,0,1), (2,2,1,0,0), (2,2,3,0,2), (2,2,3,0,0), (2,2,2,0,2),
-        (2,2,0,0,0), (2,2,1,0,3), (2,2,0,0,3), (2,2,0,0,2),
+        (1,1,2,1,0), (1,1,2,1,3), (1,1,2,1,1), (2,0,2,1,3), (3,1,2,1,0), (2,0,2,1,0), (2,0,2,1,1),
+        (3,1,2,1,2), (3,1,2,1,3), (3,1,2,1,1), (1,1,2,1,2), (2,0,2,1,2), (2,2,2,1,0), (2,2,2,1,1),
+        (2,2,2,1,2), (2,2,2,1,3), (0,1,2,1,2), (3,1,1,1,0), (2,0,1,1,0), (2,2,1,1,0), (2,0,1,1,3),
+        (3,1,1,1,3), (2,2,1,1,3), (2,2,2,0,3), (3,1,1,1,1), (2,0,1,1,1), (2,2,1,1,1), (1,1,3,1,1),
+        (2,0,3,1,1), (2,2,3,1,1), (2,2,2,0,0), (1,1,3,1,0), (2,2,3,1,0), (2,2,2,0,1), (2,0,1,1,2),
+        (3,1,1,1,2), (2,2,1,1,2), (2,0,3,1,2), (1,1,3,1,2), (2,2,3,1,2), (2,2,2,0,2), (2,2,3,1,3),
+        (2,2,1,0,0), (2,2,1,0,3), (2,2,0,0,3), (2,0,0,1,1), (3,1,0,1,1), (2,2,0,1,1), (2,2,1,0,1),
+        (3,1,0,1,2), (2,2,0,1,2), (2,2,3,0,3), (2,2,3,0,1), (2,2,0,1,3), (2,2,3,0,0), (2,2,1,0,2),
+        (2,2,3,0,2), (2,0,0,1,0), (2,2,0,1,0), (2,2,0,0,1), (2,2,0,0,2), (2,2,0,0,0),
     ),
     (
-        (2,1,3,1,1), (3,0,3,1,3), (2,1,3,1,3), (2,1,3,1,0), (2,1,3,1,2), (3,0,3,1,2), (3,2,3,1,0),
-        (3,2,3,1,1), (3,2,3,1,2), (3,2,3,1,3), (1,1,3,1,0), (1,1,3,1,3), (1,1,3,1,1), (3,0,2,1,3),
-        (3,0,3,1,0), (3,2,2,1,3), (2,1,3,0,3), (3,2,3,0,3), (3,0,2,1,1), (3,2,2,1,1), (2,1,3,0,2),
-        (0,1,3,0,2), (1,1,3,0,2), (3,2,3,0,2), (3,0,2,1,2), (3,2,2,1,2), (3,0,2,1,0), (3,2,2,1,0),
-        (3,0,1,1,0), (3,2,1,1,0), (3,2,2,0,3), (1,1,3,0,0), (0,1,3,0,0), (3,2,3,0,0), (3,0,3,1,1),
-        (3,2,2,0,1), (3,0,1,1,2), (3,2,1,1,2), (3,2,2,0,2), (3,0,1,1,3), (3,2,1,1,3), (3,2,0,0,3),
-        (3,0,1,1,1), (3,2,1,1,1), (3,2,2,0,0), (3,0,0,1,1), (3,2,0,1,1), (3,2,1,0,0), (3,2,0,1,0),
-        (0,1,3,0,1), (3,2,3,0,1), (3,2,1,0,2), (3,2,0,1,3), (3,2,0,0,0), (3,2,1,0,3), (3,2,0,1,2),
-        (3,2,1,0,1), (3,2,0,0,1), (3,2,0,0,2),
+        (2,1,3,1,1), (2,1,3,1,0), (3,0,3,1,3), (3,0,3,1,0), (2,1,3,1,2), (2,1,3,1,3), (3,2,3,1,0),
+        (3,2,3,1,1), (3,2,3,1,2), (3,2,3,1,3), (1,1,3,1,3), (3,0,2,1,0), (3,2,2,1,0), (0,1,3,0,3),
+        (2,1,3,0,3), (3,0,3,1,1), (3,2,3,0,3), (3,0,2,1,2), (3,2,2,1,2), (2,1,3,0,0), (0,1,3,0,0),
+        (3,2,3,0,0), (3,0,3,1,2), (3,0,2,1,3), (3,2,2,1,3), (3,0,2,1,1), (3,2,2,1,1), (3,0,0,1,0),
+        (3,2,0,1,0), (3,2,2,0,0), (0,1,3,0,1), (3,2,3,0,1), (3,0,1,1,0), (3,2,1,1,0), (3,2,2,0,2),
+        (3,0,1,1,3), (3,2,1,1,3), (3,0,0,1,3), (3,2,0,1,3), (0,1,3,0,2), (1,1,3,0,2), (3,2,3,0,2),
+        (3,0,1,1,1), (3,2,1,1,1), (3,2,2,0,3), (3,0,1,1,2), (3,2,1,1,2), (3,2,0,0,1), (3,2,2,0,1),
+        (3,2,0,0,0), (3,2,0,1,1), (3,2,1,0,0), (3,2,0,1,2), (3,2,0,0,2), (3,2,1,0,3), (3,2,0,0,3),
+        (3,2,1,0,1), (3,2,1,0,2),
     ),
 )
 EVENTS = (
     (
-        ((-1,0,0,0,10),), (), (), ((-2,2,0,10,2),), (), (), ((-2,3,0,12,0),(0,0,1,12,1)),
-        ((1,1,1,13,3),(0,0,3,16,3)), ((1,1,3,19,2),(1,1,2,21,2)), ((1,1,0,23,2),),
-        ((1,0,3,25,2),(1,0,1,27,1)),
-        ((2,1,1,28,2),(0,0,0,30,3),(2,1,0,33,2),(1,0,2,35,1),(2,1,2,36,2),(1,0,0,38,1)),
-        ((2,1,3,39,2),(0,0,2,41,2)), ((2,0,1,43,1),), ((2,0,0,44,1),(3,1,0,45,1),(3,0,2,46,1),(2,0,2,47,1)),
-        (), ((3,1,3,48,2),), ((2,0,3,50,1),), ((3,1,1,51,1),(3,0,0,52,1),(3,1,2,53,1)), (),
-        ((3,0,1,54,1),(3,0,3,55,1)), (),
+        ((-1,0,0,0,10),), (), (), ((-2,2,0,10,0),), (), (), ((-2,3,0,10,1),(0,0,3,11,4)),
+        ((1,1,2,15,2),(0,0,0,17,3)), ((1,1,0,20,1),(1,1,3,21,2)), ((1,1,1,23,2),),
+        ((0,0,1,25,2),(1,0,2,27,1),(1,0,3,28,2)), ((0,0,2,30,3),),
+        ((2,1,0,33,2),(1,0,1,35,1),(2,1,2,36,2),(3,0,3,38,1),(2,1,3,39,2)), ((2,1,1,41,2),),
+        ((3,0,0,43,1),(1,0,0,44,1)), (), ((2,0,0,45,1),(3,0,1,46,1),(2,0,2,47,1),(3,1,3,48,1),(3,0,2,49,1)),
+        ((2,0,3,50,1),(3,1,1,51,1)), ((2,0,1,52,1),(3,1,0,53,1),(3,1,2,54,1)), (), (), (),
     ),
     (
-        ((-1,0,0,0,15),), (), (), (), ((-2,3,0,15,1),), (), ((0,1,2,16,4),(1,0,3,20,2)),
-        ((0,1,1,22,2),(1,0,1,24,1),(2,1,1,25,3),(0,1,3,28,1)), ((1,0,0,29,2),(2,1,0,31,3),(0,1,0,34,2)),
-        ((2,1,2,36,3),), ((2,1,3,39,3),(1,0,2,42,1)), ((0,0,2,43,1),(0,0,3,44,1)),
-        ((0,0,1,45,1),(3,1,0,46,2),(2,0,1,48,1),(3,1,3,49,3)), ((2,0,0,52,1),(3,1,1,53,3)),
-        ((0,0,0,56,1),(3,1,2,57,2)), ((2,0,2,59,1),), ((2,0,3,60,1),(3,0,3,61,1),(3,0,2,62,1)), (),
-        ((3,0,1,63,1),(3,0,0,64,1)), (), (), (),
+        ((-1,0,0,0,14),), (), (), (), ((-2,3,0,14,0),), (), ((0,1,1,14,4),(1,0,3,18,2)),
+        ((0,1,0,20,1),(1,0,2,21,1),(2,1,0,22,3),(0,1,2,25,3)), ((2,1,3,28,4),(0,1,3,32,2)), ((2,1,1,34,3),),
+        ((2,1,2,37,2),(1,0,0,39,2),(0,0,3,41,1)), ((0,0,1,42,1),), ((2,0,0,43,1),(3,1,3,44,3),(0,0,2,47,1)),
+        ((0,0,0,48,1),(3,1,1,49,3),(1,0,1,52,1)), ((2,0,3,53,1),(3,1,0,54,3),(2,0,1,57,1),(3,1,2,58,2)),
+        ((2,0,2,60,1),), ((3,0,3,61,1),), (), ((3,0,1,62,1),), (), (), ((3,0,2,63,1),(3,0,0,64,1)),
     ),
     (
-        ((-1,0,0,0,15),), ((-2,0,0,15,0),), (), (), (), ((1,1,0,15,2),), ((1,1,2,17,3),(2,0,3,20,1)),
-        ((1,1,1,21,3),(3,1,1,24,2),(2,0,0,26,1)), ((3,1,3,27,1),(2,0,1,28,1),(0,1,1,29,3)),
-        ((3,1,0,32,2),(0,1,0,34,2),(3,1,2,36,3)), ((1,0,2,39,1),(1,1,3,40,2),(0,1,3,42,3),(1,0,1,45,1)),
-        ((3,0,1,46,1),(0,1,2,47,3)), ((3,0,3,50,1),(0,0,1,51,1),(1,0,0,52,1),(3,0,2,53,1),(3,0,0,54,1)),
-        ((2,0,2,55,1),), ((0,0,0,56,1),(1,0,3,57,1)), (), ((0,0,3,58,1),(0,0,2,59,1)), (), (), (), (), (),
+        ((-1,0,0,0,16),), ((-2,0,0,16,1),), (), (), (), ((1,1,0,17,3),), ((1,1,3,20,3),(2,0,3,23,1)),
+        ((1,1,1,24,3),(3,1,1,27,3),(2,0,0,30,1)), ((3,1,0,31,2),(2,0,1,33,1),(1,1,2,34,3)),
+        ((3,1,2,37,3),(2,0,2,40,1),(3,1,3,41,1),(1,0,0,42,1)), ((1,0,3,43,1),(0,0,3,44,1)),
+        ((0,1,1,45,3),(1,0,1,48,1)),
+        ((0,1,2,49,2),(3,0,3,51,1),(3,0,1,52,1),(0,1,3,53,1),(3,0,0,54,1),(1,0,2,55,1)), ((3,0,2,56,1),),
+        ((0,1,0,57,2),), (), ((0,0,1,59,1),(0,0,2,60,1)), (), (), (), (), ((0,0,0,61,1),),
     ),
     (
-        ((-1,0,0,0,10),), ((-2,1,0,10,3),(-2,0,0,13,0)), (), (), (), ((2,1,3,13,3),),
-        ((3,0,3,16,2),(2,1,1,18,2)), ((3,0,2,20,4),(2,1,2,24,2)), ((2,1,0,26,2),),
-        ((1,1,0,28,2),(2,0,3,30,1)), ((3,0,0,31,3),(2,0,1,34,2)),
-        ((1,1,2,36,2),(2,0,2,38,1),(1,1,3,39,2),(0,0,3,41,1),(1,1,1,42,2)),
-        ((2,0,0,44,1),(0,1,1,45,2),(1,0,0,47,1),(0,1,0,48,1)), ((3,0,1,49,2),),
-        ((1,0,2,51,1),(0,1,3,52,1),(0,0,0,53,1),(1,0,3,54,1)), ((0,1,2,55,1),), ((1,0,1,56,1),), (),
-        ((0,0,1,57,1),(0,0,2,58,1)), (), (), (),
+        ((-1,0,0,0,10),), ((-2,1,0,10,1),(-2,0,0,11,0)), (), (), (), ((2,1,0,11,2),),
+        ((3,0,3,13,4),(2,1,2,17,2)), ((3,0,0,19,3),), ((2,1,3,22,3),),
+        ((2,1,1,25,2),(0,1,0,27,2),(2,0,0,29,1)),
+        ((3,0,1,30,2),(1,1,0,32,2),(2,0,2,34,1),(1,1,3,35,2),(0,1,3,37,2)), ((3,0,2,39,3),),
+        ((1,1,1,42,2),(2,0,3,44,1),(1,1,2,45,2),(0,0,1,47,1),(2,0,1,48,1)),
+        ((0,0,0,49,1),(0,1,1,50,1),(1,0,0,51,1)), ((0,1,2,52,1),(0,0,2,53,1),(1,0,3,54,1)), (),
+        ((0,0,3,55,1),), (), ((1,0,1,56,1),(1,0,2,57,1)), (), (), (),
     ),
 )
-ORDER = (14551705, 13862219, 680701, 583919)
+ORDER = (15936025, 13869387, 470813, 4245423)
 
 
 def contract_last(left, right):
@@ -362,43 +361,42 @@
         got_by = twin_sem.at[source // 2] if inside else recv_sem.at[source // 2, part_of]
         target = twin if inside else line_of[to][aside]
         ref = slots.at[source, rows_of(part_of)]
-        return passing(ref, target, sent_sem.at[inside, part_of], got_by)
+        return passing(ref, target, sent_sem.at[PIECES if inside else part_of], got_by)
 
     def got(source, part_of):
         ref = slots.at[source, rows_of(part_of)]
-        passing(ref, twin, sent_sem.at[0, 0], recv_sem.at[source // 2, part_of]).wait_recv()
+        passing(ref, twin, sent_sem.at[0], recv_sem.at[source // 2, part_of]).wait_recv()
 
     def got_from_twin(base):
         ref = slots.at[base + 1 - core]
-        passing(ref, twin, sent_sem.at[0, 0], twin_sem.at[base // 2]).wait_recv()
+        passing(ref, twin, sent_sem.at[0], twin_sem.at[base // 2]).wait_recv()
 
     def all_sent(place):
-        for inside in range(2):
-            for part_of in range(PIECES):
-                number = sum(
-                    1 for entry in SENDS[place] if (entry[1] // 2, entry[4]) == (inside, part_of)
-                )
-                ref = slots.at[pl.ds(0, number), rows_of(part_of)]
-                passing(ref, twin, sent_sem.at[inside, part_of], twin_sem.at[0]).wait_send()
-
-    def tell(target, entered):
+        for part_of in range(PIECES):
+            number = sum(1 for entry in SENDS[place] if entry[1] < 2 and entry[4] == part_of)
+            ref = slots.at[pl.ds(0, number), rows_of(part_of)]
+            passing(ref, twin, sent_sem.at[part_of], twin_sem.at[0]).wait_send()
+        ref = slots.at[pl.ds(0, chips)]
+        passing(ref, twin, sent_sem.at[PIECES], twin_sem.at[0]).wait_send()
+
+    def tell(target, far):
         pl.semaphore_signal(
-            known_sem.at[entered], inc=1, device_id={"sample": target}, device_id_type=MESH
+            known_sem.at[far], inc=1, device_id={"sample": target}, device_id_type=MESH
         )
 
     def learn(place, entered):
-        pl.semaphore_wait(known_sem.at[entered], 1)
+        pl.semaphore_wait(known_sem.at[abs(entered - place) - 2], 1)
         if place == 1 and entered == 3:
-            tell(me - PLANE, 3)
+            tell(me - PLANE, 1)
         if place == 2 and entered == 0:
-            tell(me + PLANE, 0)
+            tell(me + PLANE, 1)
 
     for place in (1, 2):
 
         @pl.when(plane == place)
         def _(place=place):
-            tell(me - PLANE, place + 1)
-            tell(me + PLANE, place - 1)
+            tell(me - PLANE, 0)
+            tell(me + PLANE, 0)
 
     def events(group):
         for place in range(LINE):
@@ -749,8 +747,8 @@
             dma((len(given),)),
             dma((chips, PIECES)),
             dma((chips,)),
-            dma((2, PIECES)),
-            pltpu.SemaphoreType.REGULAR((LINE,)),
+            dma((PIECES + 1,)),
+            pltpu.SemaphoreType.REGULAR((LINE - 2,)),
             dma((3,)),
             dma((3,)),
         ],

time: 32.6 us -> 32.2 us (0.988)
  Pallas kernels: 31.8 us -> 31.4 us
    pallas_call x1, Pallas kernels: 31.8 us -> 31.4 us  [kernel_shards(): pl.pallas_call(functools.partial(whole_kernel, count, heads), out_shape=p...]
where the time goes in v7:
time: 32.2 us; the launch traced here: 32.1 us
  Pallas kernels  31.4 us (98%)
  local copies, waits for them, and re-layouts  0.62 us (2%)
    pallas_call x1, Pallas kernels, kernel_shards(): pl.pallas_call(functools.partial(whole_kernel, count, heads), out_shape=p...  31.4 us

profile of v7, /device:TPU:0, one launch (start us, length us, event | category | flops | bytes accessed | tf_op | source)
XLA Modules:
  0.0 32.1 jit_solution(12580474979437431005)
XLA Ops:
  0.0 31.4 %shard_map.136 = f32[8,1000]{1,0:T(8,128)S(1)} custom-call(bf16[8,16,588]{2,1,0:T(8,128)(2,1)} %patches.1, bf16[1,1280]{1,0:T(2,128)(2,1)} %cls_token.1, bf16[1,257,1280]{2,1,0:T(8,128)(2,1)} %pos_embed.1, f32[1,1280]{1,0:T(1,128)} %ln1_gain.1, f32[1,1280]{1,0:T(1,128)} %ln1_bias.1, bf16[1,588,1280]{2,1,0:T(8,128)(2,1)} %patch_weight.1, ...), custom_call_target="tpu_custom_call" | custom-call | tf_op jit(solution)/shard_map/pallas_call | solution.py:725
  31.5 0.6 %copy.16 = f32[8,1000]{1,0:T(8,128)} copy(f32[8,1000]{1,0:T(8,128)S(1)} %shard_map.136) | data formatting | bytes 64000

commit v8 on v7

--- a/solution.py
+++ b/solution.py
@@ -122,85 +122,86 @@
 PIECES = 4
 SENDS = (
     (
-        (0,0,0,1,3), (1,1,0,1,1), (1,1,0,1,0), (1,1,0,1,2), (1,1,0,1,3), (0,0,0,1,0), (0,2,0,1,0),
-        (0,2,0,1,1), (0,2,0,1,2), (0,2,0,1,3), (3,1,0,1,0), (1,1,0,0,3), (0,0,0,1,1), (2,1,0,0,3),
-        (0,2,0,0,3), (0,0,1,1,2), (0,2,1,1,2), (3,1,0,1,3), (1,1,0,0,0), (0,2,0,0,0), (0,2,1,1,0),
-        (0,0,0,1,2), (0,2,1,1,3), (0,0,1,1,1), (0,2,1,1,1), (3,1,0,0,1), (0,2,0,0,1), (0,2,1,0,2),
-        (2,1,0,1,0), (0,2,1,0,3), (2,1,0,0,2), (3,1,0,0,2), (0,2,0,0,2), (0,0,2,1,0), (0,2,2,1,0),
-        (0,2,1,0,1), (0,0,2,1,2), (0,2,2,1,2), (0,2,3,0,3), (0,0,2,1,3), (0,2,2,1,3), (0,0,2,1,1),
-        (0,2,2,1,1), (0,2,3,0,0), (0,2,1,0,0), (0,2,2,0,0), (0,2,3,0,1), (0,2,2,0,2), (0,2,3,1,3),
-        (0,2,3,0,2), (0,2,2,0,3), (0,2,3,1,1), (0,2,2,0,1), (0,2,3,1,0), (0,2,3,1,2),
+        (1,1,0,1,3), (0,0,0,1,3), (1,1,0,1,1), (0,0,0,1,0), (0,0,0,1,2), (1,1,0,1,2), (0,2,0,1,0),
+        (0,2,0,1,1), (0,2,0,1,2), (0,2,0,1,3), (2,1,0,1,1), (2,1,0,1,0), (2,1,0,1,2), (0,2,0,0,3),
+        (0,0,1,1,0), (0,2,1,1,0), (0,2,0,0,0), (0,0,1,1,2), (0,2,1,1,2), (1,1,0,1,0), (1,1,0,0,2),
+        (0,2,0,0,2), (0,0,1,1,3), (0,2,1,1,3), (0,2,1,1,1), (0,0,0,1,1), (0,2,1,0,0), (0,0,2,1,0),
+        (0,2,2,1,0), (0,2,1,0,2), (0,2,1,0,3), (0,2,2,1,1), (0,0,2,1,2), (0,2,2,1,2), (0,0,3,1,3),
+        (0,2,3,1,3), (0,0,2,1,3), (0,2,2,1,3), (3,1,0,0,1), (0,2,0,0,1), (0,2,1,0,1), (0,2,2,0,0),
+        (0,0,3,1,1), (0,2,3,1,1), (0,0,3,1,0), (0,2,3,1,0), (0,2,2,0,2), (0,2,2,0,1), (0,0,3,1,2),
+        (0,2,3,1,2), (0,2,3,0,3), (0,2,2,0,3), (0,2,3,0,1), (0,2,3,0,0), (0,2,3,0,2),
     ),
     (
-        (2,1,1,1,0), (2,1,1,1,3), (2,1,1,1,1), (0,1,1,1,2), (1,0,1,1,3), (2,1,1,1,2), (0,1,1,1,0),
-        (0,1,1,1,3), (0,1,1,1,1), (1,0,1,1,2), (1,2,1,1,0), (1,2,1,1,1), (1,2,1,1,2), (1,2,1,1,3),
-        (1,0,1,1,0), (2,1,0,1,1), (1,0,0,1,1), (1,2,0,1,1), (0,1,1,0,3), (1,2,1,0,3), (1,2,0,1,0),
-        (1,2,1,0,2), (1,0,2,1,0), (0,1,2,1,0), (1,2,2,1,0), (1,0,0,1,2), (2,1,0,1,2), (1,2,0,1,2),
-        (1,0,1,1,1), (1,0,2,1,3), (0,1,2,1,3), (1,2,2,1,3), (2,1,0,1,3), (1,2,0,1,3), (0,1,2,1,1),
-        (1,0,2,1,1), (1,2,2,1,1), (1,0,2,1,2), (1,2,2,1,2), (0,1,1,0,0), (1,2,1,0,0), (1,2,0,0,3),
-        (1,2,0,0,1), (1,2,2,0,0), (0,1,3,1,3), (1,0,3,1,3), (1,2,3,1,3), (1,2,0,0,2), (1,2,0,0,0),
-        (1,0,3,1,1), (0,1,3,1,1), (1,2,3,1,1), (1,2,1,0,1), (1,2,2,0,3), (0,1,3,1,0), (1,0,3,1,0),
-        (1,2,3,1,0), (1,2,2,0,1), (0,1,3,1,2), (1,2,3,1,2), (1,2,2,0,2), (1,2,3,0,3), (1,2,3,0,1),
-        (1,2,3,0,2), (1,2,3,0,0),
+        (1,0,1,1,3), (0,1,1,1,0), (1,0,1,1,0), (2,1,1,1,2), (1,0,1,1,2), (2,1,1,1,0), (0,1,1,1,2),
+        (1,0,1,1,1), (0,1,1,1,3), (0,1,1,1,1), (1,2,1,1,0), (1,2,1,1,1), (1,2,1,1,2), (1,2,1,1,3),
+        (3,1,1,1,1), (3,1,1,1,3), (1,0,0,1,3), (2,1,0,1,3), (1,2,0,1,3), (2,1,1,0,3), (1,2,1,0,3),
+        (2,1,1,1,3), (1,0,0,1,1), (1,2,0,1,1), (1,2,1,0,0), (1,0,2,1,0), (0,1,2,1,0), (2,1,1,1,1),
+        (1,2,2,1,0), (1,2,0,1,2), (1,2,1,0,2), (0,1,2,1,2), (1,0,2,1,2), (1,2,2,1,2), (0,1,1,0,1),
+        (2,1,1,0,1), (1,2,1,0,1), (1,0,2,1,1), (1,2,2,1,1), (1,2,0,0,3), (1,0,3,1,1), (0,1,3,1,1),
+        (1,2,3,1,1), (1,2,0,0,1), (1,0,0,1,0), (1,2,0,1,0), (1,0,3,1,0), (0,1,3,1,0), (1,2,3,1,0),
+        (1,2,2,0,0), (1,2,0,0,2), (1,0,3,1,2), (0,1,3,1,2), (1,2,3,1,2), (1,2,2,0,2), (1,2,2,0,1),
+        (1,2,2,0,3), (1,2,3,0,1), (1,0,3,1,3), (1,2,3,1,3), (1,2,0,0,0), (1,2,2,1,3), (1,2,3,0,0),
+        (1,2,3,0,2), (1,2,3,0,3),
     ),
     (
-        (1,1,2,1,0), (1,1,2,1,3), (1,1,2,1,1), (2,0,2,1,3), (3,1,2,1,0), (2,0,2,1,0), (2,0,2,1,1),
-        (3,1,2,1,2), (3,1,2,1,3), (3,1,2,1,1), (1,1,2,1,2), (2,0,2,1,2), (2,2,2,1,0), (2,2,2,1,1),
-        (2,2,2,1,2), (2,2,2,1,3), (0,1,2,1,2), (3,1,1,1,0), (2,0,1,1,0), (2,2,1,1,0), (2,0,1,1,3),
-        (3,1,1,1,3), (2,2,1,1,3), (2,2,2,0,3), (3,1,1,1,1), (2,0,1,1,1), (2,2,1,1,1), (1,1,3,1,1),
-        (2,0,3,1,1), (2,2,3,1,1), (2,2,2,0,0), (1,1,3,1,0), (2,2,3,1,0), (2,2,2,0,1), (2,0,1,1,2),
-        (3,1,1,1,2), (2,2,1,1,2), (2,0,3,1,2), (1,1,3,1,2), (2,2,3,1,2), (2,2,2,0,2), (2,2,3,1,3),
-        (2,2,1,0,0), (2,2,1,0,3), (2,2,0,0,3), (2,0,0,1,1), (3,1,0,1,1), (2,2,0,1,1), (2,2,1,0,1),
-        (3,1,0,1,2), (2,2,0,1,2), (2,2,3,0,3), (2,2,3,0,1), (2,2,0,1,3), (2,2,3,0,0), (2,2,1,0,2),
-        (2,2,3,0,2), (2,0,0,1,0), (2,2,0,1,0), (2,2,0,0,1), (2,2,0,0,2), (2,2,0,0,0),
+        (2,0,2,1,2), (2,0,2,1,3), (2,0,2,1,0), (3,1,2,1,2), (1,1,2,1,0), (3,1,2,1,0), (1,1,2,1,2),
+        (1,1,2,1,1), (2,0,2,1,1), (3,1,2,1,3), (3,1,2,1,1), (2,2,2,1,0), (2,2,2,1,1), (2,2,2,1,2),
+        (2,2,2,1,3), (0,1,2,1,1), (0,1,2,1,3), (3,1,1,1,2), (2,0,1,1,2), (2,2,1,1,2), (3,1,1,1,0),
+        (2,0,1,1,0), (2,2,1,1,0), (2,2,2,0,2), (2,0,3,1,1), (2,2,3,1,1), (1,1,2,0,3), (2,2,2,0,3),
+        (2,0,0,1,1), (3,1,0,1,1), (2,2,0,1,1), (2,0,3,1,3), (1,1,3,1,3), (2,2,3,1,3), (2,2,2,0,0),
+        (2,0,0,1,0), (3,1,0,1,0), (2,2,0,1,0), (1,1,2,1,3), (2,2,3,1,2), (0,1,2,0,1), (2,2,2,0,1),
+        (3,1,0,1,2), (2,0,0,1,2), (2,2,0,1,2), (2,2,1,0,2), (2,2,1,0,0), (2,2,3,0,1), (2,0,0,1,3),
+        (3,1,0,1,3), (2,2,0,1,3), (2,2,1,0,3), (2,2,0,0,1), (2,2,1,1,3), (2,2,3,0,3), (2,0,3,1,0),
+        (2,2,3,1,0), (2,2,1,1,1), (2,2,0,0,0), (2,2,3,0,2), (2,2,1,0,1), (2,2,0,0,2), (2,2,0,0,3),
+        (2,2,3,0,0),
     ),
     (
-        (2,1,3,1,1), (2,1,3,1,0), (3,0,3,1,3), (3,0,3,1,0), (2,1,3,1,2), (2,1,3,1,3), (3,2,3,1,0),
-        (3,2,3,1,1), (3,2,3,1,2), (3,2,3,1,3), (1,1,3,1,3), (3,0,2,1,0), (3,2,2,1,0), (0,1,3,0,3),
-        (2,1,3,0,3), (3,0,3,1,1), (3,2,3,0,3), (3,0,2,1,2), (3,2,2,1,2), (2,1,3,0,0), (0,1,3,0,0),
-        (3,2,3,0,0), (3,0,3,1,2), (3,0,2,1,3), (3,2,2,1,3), (3,0,2,1,1), (3,2,2,1,1), (3,0,0,1,0),
-        (3,2,0,1,0), (3,2,2,0,0), (0,1,3,0,1), (3,2,3,0,1), (3,0,1,1,0), (3,2,1,1,0), (3,2,2,0,2),
-        (3,0,1,1,3), (3,2,1,1,3), (3,0,0,1,3), (3,2,0,1,3), (0,1,3,0,2), (1,1,3,0,2), (3,2,3,0,2),
-        (3,0,1,1,1), (3,2,1,1,1), (3,2,2,0,3), (3,0,1,1,2), (3,2,1,1,2), (3,2,0,0,1), (3,2,2,0,1),
-        (3,2,0,0,0), (3,2,0,1,1), (3,2,1,0,0), (3,2,0,1,2), (3,2,0,0,2), (3,2,1,0,3), (3,2,0,0,3),
-        (3,2,1,0,1), (3,2,1,0,2),
+        (3,0,3,1,1), (2,1,3,1,1), (3,0,3,1,0), (2,1,3,1,3), (3,0,3,1,2), (2,1,3,1,2), (3,0,3,1,3),
+        (3,2,3,1,0), (3,2,3,1,1), (3,2,3,1,2), (3,2,3,1,3), (1,1,3,1,1), (1,1,3,1,0), (1,1,3,1,2),
+        (0,1,3,1,3), (3,0,2,1,2), (3,2,2,1,2), (3,2,3,0,1), (3,0,2,1,0), (3,2,2,1,0), (3,2,3,0,0),
+        (3,0,2,1,3), (3,2,2,1,3), (2,1,3,1,0), (2,1,3,0,2), (3,2,3,0,2), (3,0,2,1,1), (3,2,2,1,1),
+        (3,2,3,0,3), (3,0,1,1,1), (3,2,1,1,1), (3,2,2,0,2), (3,0,1,1,3), (3,2,1,1,3), (3,2,2,0,0),
+        (3,0,1,1,2), (3,2,1,1,2), (3,0,1,1,0), (3,2,1,1,0), (3,2,2,0,3), (3,2,0,1,1), (3,2,2,0,1),
+        (3,0,0,1,0), (3,2,0,1,0), (3,2,1,0,1), (3,0,0,1,2), (3,2,0,1,2), (3,2,1,0,3), (3,0,0,1,3),
+        (3,2,0,1,3), (3,2,1,0,2), (3,2,1,0,0), (3,2,0,0,0), (3,2,0,0,2), (3,2,0,0,3), (3,2,0,0,1),
     ),
 )
 EVENTS = (
     (
-        ((-1,0,0,0,10),), (), (), ((-2,2,0,10,0),), (), (), ((-2,3,0,10,1),(0,0,3,11,4)),
-        ((1,1,2,15,2),(0,0,0,17,3)), ((1,1,0,20,1),(1,1,3,21,2)), ((1,1,1,23,2),),
-        ((0,0,1,25,2),(1,0,2,27,1),(1,0,3,28,2)), ((0,0,2,30,3),),
-        ((2,1,0,33,2),(1,0,1,35,1),(2,1,2,36,2),(3,0,3,38,1),(2,1,3,39,2)), ((2,1,1,41,2),),
-        ((3,0,0,43,1),(1,0,0,44,1)), (), ((2,0,0,45,1),(3,0,1,46,1),(2,0,2,47,1),(3,1,3,48,1),(3,0,2,49,1)),
-        ((2,0,3,50,1),(3,1,1,51,1)), ((2,0,1,52,1),(3,1,0,53,1),(3,1,2,54,1)), (), (), (),
+        ((-1,0,0,0,10),), (), (), ((-2,2,0,10,3),), (), (), ((-2,3,0,13,0),(0,0,3,13,1)),
+        ((1,1,0,14,2),(0,0,0,16,1)), ((1,1,2,17,2),(0,0,2,19,3),(1,1,3,22,2)), ((1,1,1,24,1),),
+        ((1,0,0,25,2),),
+        ((2,1,0,27,2),(1,0,2,29,1),(1,0,3,30,1),(2,1,1,31,1),(2,1,2,32,2),(3,1,3,34,2),(2,1,3,36,2)),
+        ((0,0,1,38,2),(1,0,1,40,1),(2,0,0,41,1),(3,1,1,42,2)), ((3,1,0,44,2),),
+        ((2,0,2,46,1),(2,0,1,47,1),(3,1,2,48,2),(3,0,3,50,1)), (), ((2,0,3,51,1),), (), ((3,0,1,52,1),), (),
+        ((3,0,0,53,1),), ((3,0,2,54,1),),
     ),
     (
-        ((-1,0,0,0,14),), (), (), (), ((-2,3,0,14,0),), (), ((0,1,1,14,4),(1,0,3,18,2)),
-        ((0,1,0,20,1),(1,0,2,21,1),(2,1,0,22,3),(0,1,2,25,3)), ((2,1,3,28,4),(0,1,3,32,2)), ((2,1,1,34,3),),
-        ((2,1,2,37,2),(1,0,0,39,2),(0,0,3,41,1)), ((0,0,1,42,1),), ((2,0,0,43,1),(3,1,3,44,3),(0,0,2,47,1)),
-        ((0,0,0,48,1),(3,1,1,49,3),(1,0,1,52,1)), ((2,0,3,53,1),(3,1,0,54,3),(2,0,1,57,1),(3,1,2,58,2)),
-        ((2,0,2,60,1),), ((3,0,3,61,1),), (), ((3,0,1,62,1),), (), (), ((3,0,2,63,1),(3,0,0,64,1)),
+        ((-1,0,0,0,14),), (), (), (), ((-2,3,0,14,2),), (), ((0,1,3,16,3),(1,0,3,19,2)),
+        ((0,1,1,21,3),(1,0,0,24,1),(2,1,0,25,4),(0,1,2,29,1)), ((1,0,2,30,1),(2,1,2,31,3)),
+        ((1,0,1,34,3),(2,1,1,37,2)), ((0,0,3,39,1),(3,1,1,40,3),(0,0,1,43,1)),
+        ((0,1,0,44,2),(3,1,0,46,3),(2,0,0,49,1),(0,0,2,50,1)), ((3,1,2,51,3),(2,0,2,54,1),(2,0,1,55,1)),
+        ((2,0,3,56,1),(3,0,1,57,1),(3,1,3,58,2)), ((0,0,0,60,1),(2,1,3,61,1),(3,0,0,62,1)), (),
+        ((3,0,2,63,1),), (), ((3,0,3,64,1),), (), (), (),
     ),
     (
-        ((-1,0,0,0,16),), ((-2,0,0,16,1),), (), (), (), ((1,1,0,17,3),), ((1,1,3,20,3),(2,0,3,23,1)),
-        ((1,1,1,24,3),(3,1,1,27,3),(2,0,0,30,1)), ((3,1,0,31,2),(2,0,1,33,1),(1,1,2,34,3)),
-        ((3,1,2,37,3),(2,0,2,40,1),(3,1,3,41,1),(1,0,0,42,1)), ((1,0,3,43,1),(0,0,3,44,1)),
-        ((0,1,1,45,3),(1,0,1,48,1)),
-        ((0,1,2,49,2),(3,0,3,51,1),(3,0,1,52,1),(0,1,3,53,1),(3,0,0,54,1),(1,0,2,55,1)), ((3,0,2,56,1),),
-        ((0,1,0,57,2),), (), ((0,0,1,59,1),(0,0,2,60,1)), (), (), (), (), ((0,0,0,61,1),),
+        ((-1,0,0,0,15),), ((-2,0,0,15,2),), (), (), (), ((1,1,2,17,3),), ((1,1,0,20,3),(2,0,2,23,1)),
+        ((3,1,1,24,2),(2,0,3,26,2)), ((0,1,1,28,3),(3,1,3,31,3),(2,0,0,34,1),(0,1,0,35,3)),
+        ((3,1,2,38,2),(2,0,1,40,2),(0,1,2,42,3),(1,0,2,45,1)), ((1,0,0,46,1),(3,0,1,47,1),(0,1,3,48,3)),
+        ((1,0,3,51,1),(0,0,1,52,1)), ((1,1,3,53,1),(3,0,3,54,1),(3,1,0,55,2)),
+        ((1,1,1,57,1),(0,0,0,58,1),(3,0,2,59,1),(1,0,1,60,1),(0,0,2,61,1)), ((0,0,3,62,1),), (), (), (),
+        ((3,0,0,63,1),), (), (), (),
     ),
     (
-        ((-1,0,0,0,10),), ((-2,1,0,10,1),(-2,0,0,11,0)), (), (), (), ((2,1,0,11,2),),
-        ((3,0,3,13,4),(2,1,2,17,2)), ((3,0,0,19,3),), ((2,1,3,22,3),),
-        ((2,1,1,25,2),(0,1,0,27,2),(2,0,0,29,1)),
-        ((3,0,1,30,2),(1,1,0,32,2),(2,0,2,34,1),(1,1,3,35,2),(0,1,3,37,2)), ((3,0,2,39,3),),
-        ((1,1,1,42,2),(2,0,3,44,1),(1,1,2,45,2),(0,0,1,47,1),(2,0,1,48,1)),
-        ((0,0,0,49,1),(0,1,1,50,1),(1,0,0,51,1)), ((0,1,2,52,1),(0,0,2,53,1),(1,0,3,54,1)), (),
-        ((0,0,3,55,1),), (), ((1,0,1,56,1),(1,0,2,57,1)), (), (), (),
+        ((-1,0,0,0,11),), ((-2,1,0,11,3),(-2,0,0,14,1)), (), (), (), ((2,1,2,15,2),),
+        ((3,0,1,17,1),(2,1,0,18,2)), ((3,0,0,20,1),(2,1,3,21,2)), ((3,0,2,23,3),(2,1,1,26,2)),
+        ((3,0,3,28,1),(1,1,1,29,2),(2,0,2,31,1)), ((1,1,3,32,2),(2,0,0,34,1),(1,1,2,35,2)),
+        ((1,1,0,37,2),(2,0,3,39,1)), ((0,1,1,40,1),(2,0,1,41,1),(0,1,0,42,2)), ((1,0,1,44,1),(0,1,2,45,2)),
+        ((1,0,3,47,1),(0,1,3,48,2)), (), ((1,0,2,50,1),(1,0,0,51,1)), (), ((0,0,0,52,1),), (),
+        ((0,0,2,53,1),), ((0,0,3,54,1),(0,0,1,55,1)),
     ),
 )
-ORDER = (15936025, 13869387, 470813, 4245423)
+ORDER = (13869401, 13924435, 12664421, 575407)
 
 
 def contract_last(left, right):

time: 32.2 us -> 31.4 us (0.975)
  Pallas kernels: 31.4 us -> 30.7 us
    pallas_call x1, Pallas kernels: 31.4 us -> 30.7 us  [kernel_shards(): pl.pallas_call(functools.partial(whole_kernel, count, heads), out_shape=p...]
where the time goes in v8:
time: 31.4 us; the launch traced here: 31.3 us
  Pallas kernels  30.7 us (98%)
  local copies, waits for them, and re-layouts  0.62 us (2%)
    pallas_call x1, Pallas kernels, kernel_shards(): pl.pallas_call(functools.partial(whole_kernel, count, heads), out_shape=p...  30.7 us

profile of v8, /device:TPU:0, one launch (start us, length us, event | category | flops | bytes accessed | tf_op | source)
XLA Modules:
  0.0 31.3 jit_solution(12941433298380071823)
XLA Ops:
  0.0 30.7 %shard_map.136 = f32[8,1000]{1,0:T(8,128)S(1)} custom-call(bf16[8,16,588]{2,1,0:T(8,128)(2,1)} %patches.1, bf16[1,1280]{1,0:T(2,128)(2,1)} %cls_token.1, bf16[1,257,1280]{2,1,0:T(8,128)(2,1)} %pos_embed.1, f32[1,1280]{1,0:T(1,128)} %ln1_gain.1, f32[1,1280]{1,0:T(1,128)} %ln1_bias.1, bf16[1,588,1280]{2,1,0:T(8,128)(2,1)} %patch_weight.1, ...), custom_call_target="tpu_custom_call" | custom-call | tf_op jit(solution)/shard_map/pallas_call | solution.py:726
  30.7 0.6 %copy.16 = f32[8,1000]{1,0:T(8,128)} copy(f32[8,1000]{1,0:T(8,128)S(1)} %shard_map.136) | data formatting | bytes 64000

commit v9 on v8

--- a/solution.py
+++ b/solution.py
@@ -399,20 +399,34 @@
             tell(me - PLANE, 0)
             tell(me + PLANE, 0)
 
+    def events_at(place, group):
+        for origin, own, part_of, low, number in EVENTS[place][group]:
+            if origin == -2:
+                learn(place, own)
+            if origin >= 0:
+                got(line_of[origin][own], part_of)
+            for slot in range(low, low + number):
+                sent(place, slot).start()
+
+    def narrowed(value, low, high, act, busy):
+        live = [place for place in range(low, high) if busy(place)]
+        if not live:
+            return
+        if high - low == 1:
+            act(low)
+            return
+        middle = (low + high) // 2
+        pl.when(value < middle)(lambda: narrowed(value, low, middle, act, busy))
+        pl.when(value >= middle)(lambda: narrowed(value, middle, high, act, busy))
+
     def events(group):
-        for place in range(LINE):
-            entries = EVENTS[place][group]
-            if entries:
-
-                @pl.when(plane == place)
-                def _(place=place, entries=entries):
-                    for origin, own, part_of, low, number in entries:
-                        if origin == -2:
-                            learn(place, own)
-                        if origin >= 0:
-                            got(line_of[origin][own], part_of)
-                        for slot in range(low, low + number):
-                            sent(place, slot).start()
+        narrowed(
+            plane,
+            0,
+            LINE,
+            lambda place: events_at(place, group),
+            lambda place: bool(EVENTS[place][group]),
+        )
 
     events(0)
     for load in loads[7:]:
@@ -544,8 +558,7 @@
         ends[...] = product[fold_rows - ends.shape[0] :]
 
     def chip_step(turn, carry):
-        for index in range(1, 2 * LINE):
-            pl.when(turn == index)(functools.partial(events, first_step + 2 * index))
+        narrowed(turn, 1, 2 * LINE, lambda index: events(first_step + 2 * index), lambda index: True)
         base = base_of(turn)
         got_from_twin(base)
         scores = kept[:heads, :]
@@ -553,8 +566,13 @@
         back(base_of(turn - 1), scores, rate)
         front(base)
 
-        for index in range(1, 2 * LINE - 1):
-            pl.when(turn == index)(functools.partial(events, first_step + 2 * index + 1))
+        narrowed(
+            turn,
+            1,
+            2 * LINE,
+            lambda index: events(first_step + 2 * index + 1),
+            lambda index: index < 2 * LINE - 1,
+        )
 
         @pl.when(turn < FOLD_PARTS)
         def _():

time: 31.4 us -> 31.2 us (level)
  no operation moved by 1% of the time
where the time goes in v9:
time: 31.2 us; the launch traced here: 31.1 us
  Pallas kernels  30.4 us (97%)
  local copies, waits for them, and re-layouts  0.62 us (2%)
    pallas_call x1, Pallas kernels, kernel_shards(): pl.pallas_call(functools.partial(whole_kernel, count, heads), out_shape=p...  30.4 us

profile of v9, /device:TPU:0, one launch (start us, length us, event | category | flops | bytes accessed | tf_op | source)
XLA Modules:
  0.0 31.1 jit_solution(12673664359948994039)
XLA Ops:
  0.0 30.4 %shard_map.136 = f32[8,1000]{1,0:T(8,128)S(1)} custom-call(bf16[8,16,588]{2,1,0:T(8,128)(2,1)} %patches.1, bf16[1,1280]{1,0:T(2,128)(2,1)} %cls_token.1, bf16[1,257,1280]{2,1,0:T(8,128)(2,1)} %pos_embed.1, f32[1,1280]{1,0:T(1,128)} %ln1_gain.1, f32[1,1280]{1,0:T(1,128)} %ln1_bias.1, bf16[1,588,1280]{2,1,0:T(8,128)(2,1)} %patch_weight.1, ...), custom_call_target="tpu_custom_call" | custom-call | tf_op jit(solution)/shard_map/pallas_call | solution.py:744
  30.4 0.6 %copy.16 = f32[8,1000]{1,0:T(8,128)} copy(f32[8,1000]{1,0:T(8,128)S(1)} %shard_map.136) | data formatting | bytes 64000

commit v10 on v9

--- a/solution.py
+++ b/solution.py
@@ -592,11 +592,11 @@
     plain = ends[last - 3 : last - 2, :] + ends[last - 2 : last - 1, :]
     lead_value = ends[last - 1 :, :]
     values = jnp.dot(
-        split_in_two(gathered[...]), folded[...], preferred_element_type=f32
+        gathered[...].astype(bf16), folded[...], preferred_element_type=f32
     )
     share = 1.0 / total[:, :1]
     lead_chance = jnp.exp(first - peak[:, :1]) * share
-    values = (values[:pairs] + values[pairs:]) * share
+    values = values * share
     values = values + plain + (lead_value - plain) * lead_chance
     pair_head = lax.broadcasted_iota(jnp.int32, (pairs, inner), 0) % heads
     pair_column = lax.broadcasted_iota(jnp.int32, (pairs, inner), 1)

time: 31.2 us -> 31.2 us (level)
  no operation moved by 1% of the time
where the time goes in v10:
time: 31.2 us; the launch traced here: 31 us
  Pallas kernels  30.4 us (97%)
  local copies, waits for them, and re-layouts  0.62 us (2%)
    pallas_call x1, Pallas kernels, kernel_shards(): pl.pallas_call(functools.partial(whole_kernel, count, heads), out_shape=p...  30.4 us

profile of v10, /device:TPU:0, one launch (start us, length us, event | category | flops | bytes accessed | tf_op | source)
XLA Modules:
  0.0 31.0 jit_solution(13931337686115880980)
XLA Ops:
  0.0 30.4 %shard_map.136 = f32[8,1000]{1,0:T(8,128)S(1)} custom-call(bf16[8,16,588]{2,1,0:T(8,128)(2,1)} %patches.1, bf16[1,1280]{1,0:T(2,128)(2,1)} %cls_token.1, bf16[1,257,1280]{2,1,0:T(8,128)(2,1)} %pos_embed.1, f32[1,1280]{1,0:T(1,128)} %ln1_gain.1, f32[1,1280]{1,0:T(1,128)} %ln1_bias.1, bf16[1,588,1280]{2,1,0:T(8,128)(2,1)} %patch_weight.1, ...), custom_call_target="tpu_custom_call" | custom-call | tf_op jit(solution)/shard_map/pallas_call | solution.py:744
  30.4 0.6 %copy.16 = f32[8,1000]{1,0:T(8,128)} copy(f32[8,1000]{1,0:T(8,128)S(1)} %shard_map.136) | data formatting | bytes 64000
